TPU v7x, 128 devices: a whole 4x4x4 slice. The times are simulated.
128 devices in a mesh: ctx: 16 (over y, z), wt: 8 (over x, core).
Axes of the slice: x: 4, y: 4, z: 4, core: 2. Of those that a mesh axis runs over, the one named last changes fastest.
Arguments:
- frames: bfloat16 [1024, 1280], P('wt'), may hold values from -6 to 6
- span_source: int32 [64], P('wt'), may hold values from 0 to 7, as said below
- adapter_weight: bfloat16 [1280, 4096], P(None, 'ctx'), may hold values from -0.15625 to 0.15625
- adapter_bias: float32 [4096], P('ctx'), may hold values from -3 to 3
- norm_gain: float32 [4096], replicated, may hold values from 0.25 to 1.75
- qkv_weight: bfloat16 [4096, 3, 4096], P('wt', None, 'ctx'), may hold values from -0.09375 to 0.09375
- out_weight: bfloat16 [4096, 4096], P('ctx', 'wt'), may hold values from -0.125 to 0.125
- k_cache: bfloat16 [16, 2048, 4096], P('wt', 'ctx'), may hold values from -600 to 600
- v_cache: bfloat16 [16, 2048, 4096], P('wt', 'ctx'), may hold values from -12 to 12
- lengths: int32 [16], P('wt'), may hold values from 1 to 2048
Outputs:
- attn_out: bfloat16 [1024, 4096], P('wt', 'ctx')
- new_keys: bfloat16 [1024, 4096], P('wt', 'ctx')
- new_values: bfloat16 [1024, 4096], P('wt', 'ctx')
Inputs may be any that keep to these rules, and one draw needn't show every extreme that they name: `span_source`: each aligned block of 8 entries is a permutation of 0 to 7.
All inputs are finite; a program needn't handle non-finite values.
Results may differ from a plain program's by a relative error of at most 0.02.
Values may be sent and summed in bfloat16 or wider, within the bound.
No kernel may reach another device: no remote copies, remote signals or barrier semaphores. Data moves between devices by JAX's collectives and lax.ppermute only.
A program may use at most 64 MiB of HBM per device.

v0:
```python
import jax
import jax.numpy as jnp
from jax import lax
from jax.experimental import pallas as pl
from jax.experimental.pallas import tpu as pltpu
from jax.sharding import PartitionSpec as P


HEAD = 128
SIDE = 4
FLOOR = -1e30

bf16 = jnp.bfloat16
f32 = jnp.float32


def y_shift(x, k):
    pairs = [
        (y * SIDE + z, ((y + k) % SIDE) * SIDE + z) for y in range(SIDE) for z in range(SIDE)
    ]
    return lax.ppermute(x, "ctx", pairs)


def z_shift(x, k):
    pairs = [
        (y * SIDE + z, y * SIDE + (z + k) % SIDE) for y in range(SIDE) for z in range(SIDE)
    ]
    return lax.ppermute(x, "ctx", pairs)


def x_shift(x, k):
    pairs = [(2 * i + c, 2 * ((i + k) % SIDE) + c) for i in range(SIDE) for c in range(2)]
    return lax.ppermute(x, "wt", pairs)


def other_core(x):
    return lax.ppermute(x, "wt", [(i, i ^ 1) for i in range(2 * SIDE)])


def swap_xy(x):
    def place(i, y, z, c):
        return (y * SIDE + z) * 2 * SIDE + 2 * i + c

    pairs = [
        (place(i, y, z, c), place(y, i, z, c))
        for i in range(SIDE)
        for y in range(SIDE)
        for z in range(SIDE)
        for c in range(2)
    ]
    return lax.ppermute(x, ("ctx", "wt"), pairs)


ORDER = (1, 3, 2)


def from_ring(x, shift):
    got = {k: shift(x, k) for k in ORDER}
    return [x, got[1], got[2], got[3]]


def over_x(x):
    mine = from_ring(x, x_shift)
    return [p for m in mine for p in (m, other_core(m))]


VMEM = pl.BlockSpec(memory_space=pltpu.VMEM)
SMEM = pl.BlockSpec(memory_space=pltpu.SMEM)
ANY = pl.BlockSpec(memory_space=pl.ANY)


def held(x):
    return pltpu.with_memory_space_constraint(x, pltpu.VMEM)


def kernel_call(body, ins, out_shape, scratch=(), limit=12):
    single = not isinstance(out_shape, tuple)
    return pl.pallas_call(
        body,
        in_specs=[s for s, _ in ins],
        out_specs=VMEM if single else tuple(VMEM for _ in out_shape),
        out_shape=out_shape,
        scratch_shapes=list(scratch),
        compiler_params=pltpu.CompilerParams(vmem_limit_bytes=limit << 20),
    )(*[held(a) if s is VMEM else a for s, a in ins])


def near(dims, kind):
    return pltpu.VMEM(dims, kind)


def far(dims, kind):
    return jax.ShapeDtypeStruct(dims, kind)


def matmul(a, b):
    return jnp.dot(a, b, preferred_element_type=f32)


def matmul_t(a, b):
    return lax.dot_general(a, b, (((1,), (1,)), ((), ())), preferred_element_type=f32)


def adapter_body(source, frames, weight, bias, kinds, out, query_weight, other_weight, ordered, sems):
    copies = (
        pltpu.make_async_copy(kinds.at[0], query_weight, sems.at[0]),
        pltpu.make_async_copy(kinds.at[1:3], other_weight, sems.at[1]),
    )
    for copy in copies:
        copy.start()
    spans = source.shape[0]
    rows = frames.shape[0] // spans
    for g in range(spans):
        start = pl.multiple_of(source[g] * rows, rows)
        ordered[g * rows : (g + 1) * rows, :] = frames[pl.ds(start, rows), :]
    out[...] = (matmul(ordered[...], weight[...]) + bias[...]).astype(bf16)
    for copy in copies:
        copy.wait()


def stack_body(a0, a1, a2, a3, out):
    for k, a in enumerate((a0, a1, a2, a3)):
        out[k] = a[...]


def stacked(parts):
    dims = (SIDE, *parts[0].shape)
    return kernel_call(stack_body, [(VMEM, p) for p in parts], near(dims, bf16))


def spin(u, cosine, sine):
    return u * cosine + pltpu.roll(u, HEAD // 2, 1) * sine


def pieces_product(place, normed, weights, take):
    total = None
    for n, weight in enumerate(weights):
        shard = 2 * ((place[0] + SIDE - n // 2) % SIDE) + (place[1] + n) % 2
        w = take(weight)
        half = w.shape[0] // 2
        part = matmul(normed[2 * shard], w[:half]) + matmul(normed[2 * shard + 1], w[half:])
        total = part if total is None else total + part
    return total


def query_body(place, s0, s1, s2, s3, gain, cosine, sine, *rest):
    weights, (query, normed) = rest[:8], rest[8:]
    stacks = (s0, s1, s2, s3)
    rows = s0.shape[1]
    sums = jnp.zeros((rows, HEAD), f32)
    for stack in stacks:
        for k in range(SIDE):
            wide = stack[k].astype(f32)
            square = wide * wide
            sums = sums + (square[:, :HEAD] + square[:, HEAD:])
    width = SIDE * SIDE * s0.shape[2]
    factor = lax.rsqrt(jnp.sum(sums, axis=-1, keepdims=True) * (1.0 / width) + 1e-06)
    for j, stack in enumerate(stacks):
        for k in range(SIDE):
            block = SIDE * ((place[2] + SIDE - k) % SIDE) + (place[3] + SIDE - j) % SIDE
            normed[block] = (stack[k].astype(f32) * factor * gain[block]).astype(bf16)
    projected = pieces_product(place, normed, weights, lambda w: w[...])
    for h in range(projected.shape[1] // HEAD):
        cut = slice(h * HEAD, (h + 1) * HEAD)
        query[:, cut] = spin(projected[:, cut], cosine[...], sine[...]).astype(bf16)


def key_value_body(place, normed, cosine, sine, *rest):
    weights, (keys, values) = rest[:8], rest[8:]
    projected = pieces_product(place, normed, weights, lambda w: w[0])
    for h in range(projected.shape[1] // HEAD):
        cut = slice(h * HEAD, (h + 1) * HEAD)
        keys[:, cut] = spin(projected[:, cut], cosine[...], sine[...]).astype(bf16)
    values[...] = pieces_product(place, normed, weights, lambda w: w[1]).astype(bf16)


def split_in_three(x):
    high = x.astype(bf16).astype(f32)
    middle = (x - high).astype(bf16).astype(f32)
    return high, middle, x - high - middle


def soft_weights(scores, live):
    scores = jnp.where(live, scores, FLOOR)
    most = jnp.max(scores, axis=-1, keepdims=True)
    weights = jnp.where(live, jnp.exp(scores - most), 0.0)
    return weights, most, jnp.sum(weights, axis=-1, keepdims=True)


def history_body(step, place, lengths, stack, k_cache, v_cache, out, scores, weights):
    meetings, span = k_cache.shape[0], k_cache.shape[1]
    rows = stack.shape[1]
    new = rows // meetings
    heads = 2 * SIDE
    starts = []
    for k in range(SIDE):
        block = SIDE * ((place[2] + SIDE - k) % SIDE) + (place[3] + SIDE - step) % SIDE
        for h in range(2):
            starts.append(pl.multiple_of(block * 256 + h * HEAD, HEAD))
    for i, start in enumerate(starts):
        cut = slice(i % 2 * HEAD, (i % 2 + 1) * HEAD)
        for m in range(meetings):
            here = slice(m * new, (m + 1) * new)
            scores[i, here, :] = matmul_t(
                stack[i // 2, here, cut], k_cache[m, :, pl.ds(start, HEAD)]
            )
    first = (place[2] * SIDE + place[3]) * span
    spot = first + lax.broadcasted_iota(jnp.int32, (rows, span), 1)
    upper = lax.broadcasted_iota(jnp.int32, (rows, span), 0) < new
    live = spot < jnp.where(upper, lengths[0], lengths[1])
    lane = lax.broadcasted_iota(jnp.int32, (rows, HEAD), 1)
    stats = jnp.zeros((rows, HEAD), f32)
    for i in range(heads):
        weight, most, total = soft_weights(scores[i] * HEAD**-0.5, live)
        weights[i] = weight.astype(bf16)
        stats = jnp.where(lane == i, most, jnp.where(lane == heads + i, total, stats))
    for i, start in enumerate(starts):
        for m in range(meetings):
            here = slice(m * new, (m + 1) * new)
            at = i * rows + m * new
            out[at : at + new, :] = matmul(
                weights[i, here, :], v_cache[m, :, pl.ds(start, HEAD)]
            ).astype(bf16)
    turned = jnp.transpose(stats)[: 2 * heads]
    base = heads * rows
    for n, piece in enumerate(split_in_three(turned)):
        out[base + 16 * n : base + 16 * n + 16, :] = piece.astype(bf16)


def turned_columns(pieces, rows):
    used = sum(p.shape[0] for p in pieces)
    fill = [jnp.zeros((rows - used, pieces[0].shape[1]), f32)] if rows > used else []
    return jnp.transpose(jnp.concatenate(list(pieces) + fill, axis=0))


def row_mix_body(p0, p1, p2, p3, own, o1, o2, o3):
    parts = (p0, p1, p2, p3)
    outs = (own, o1, o2, o3)
    heads = 2 * SIDE
    rows = p0.shape[1]
    base = heads * rows
    tops, totals = [], []
    for p in parts:
        tail = p[base : base + 48, :].astype(f32)
        stats = tail[:16] + tail[16:32] + tail[32:]
        tops.append(stats[:heads])
        totals.append(stats[heads:])
    top = jnp.maximum(jnp.maximum(tops[0], tops[1]), jnp.maximum(tops[2], tops[3]))
    factors = [jnp.exp(t - top) for t in tops]
    total = sum(t * f for t, f in zip(totals, factors))
    columns = turned_columns(factors, rows)
    for h in range(heads):
        cut = slice(h * rows, (h + 1) * rows)
        mixed = None
        for i, p in enumerate(parts):
            at = i * heads + h
            term = p[cut, :].astype(f32) * columns[:, at : at + 1]
            mixed = term if mixed is None else mixed + term
        outs[h // 2][(h % 2) * rows : (h % 2 + 1) * rows, :] = mixed.astype(bf16)
    spread = [piece for pair in zip(split_in_three(top), split_in_three(total)) for piece in pair]
    for k in range(SIDE):
        cut = slice(2 * k, 2 * k + 2)
        outs[k][2 * rows : 2 * rows + 16, :] = jnp.concatenate(
            [piece[cut] for piece in spread] + [jnp.zeros((4, rows), f32)], axis=0
        ).astype(bf16)


def new_part_body(query, keys, values, numer, stats_out):
    rows = query.shape[0]
    new = rows // 2
    causal = lax.broadcasted_iota(jnp.int32, (new, new), 0) >= lax.broadcasted_iota(
        jnp.int32, (new, new), 1
    )
    lane = lax.broadcasted_iota(jnp.int32, (new, HEAD), 1)
    stats = []
    for m in range(2):
        here = slice(m * new, (m + 1) * new)
        tile = jnp.zeros((new, HEAD), f32)
        for h in range(2):
            cut = slice(h * HEAD, (h + 1) * HEAD)
            weight, most, total = soft_weights(
                matmul_t(query[here, cut], keys[here, cut]) * HEAD**-0.5, causal
            )
            numer[h * rows + m * new : h * rows + (m + 1) * new, :] = matmul(
                weight.astype(bf16), values[here, cut]
            )
            tile = jnp.where(lane == h, most, jnp.where(lane == 2 + h, total, tile))
        stats.append(tile)
    stats_out[...] = jnp.transpose(jnp.concatenate(stats, axis=0))[:8]


def final_mix_body(p0, p1, p2, p3, numer, new_stats, out):
    parts = (p0, p1, p2, p3)
    rows = numer.shape[0] // 2
    tops, totals = [], []
    for p in parts:
        tail = p[2 * rows : 2 * rows + 16, :].astype(f32)
        tops.append(tail[0:2] + tail[4:6] + tail[8:10])
        totals.append(tail[2:4] + tail[6:8] + tail[10:12])
    tops.append(new_stats[0:2])
    totals.append(new_stats[2:4])
    top = tops[0]
    for t in tops[1:]:
        top = jnp.maximum(top, t)
    factors = [jnp.exp(t - top) for t in tops]
    total = sum(t * f for t, f in zip(totals, factors))
    columns = turned_columns([f / total for f in factors], rows)
    for h in range(2):
        cut = slice(h * rows, (h + 1) * rows)
        mixed = numer[cut, :] * columns[:, 8 + h : 9 + h]
        for i, p in enumerate(parts):
            mixed = mixed + p[cut, :].astype(f32) * columns[:, 2 * i + h : 2 * i + h + 1]
        out[:, h * HEAD : (h + 1) * HEAD] = mixed.astype(bf16)


def project_body(place, a0, a1, a2, a3, *rest):
    weights, (own, o1, o2, o3, across, sums) = rest[:8], rest[8:]
    for k, a in enumerate((a0, a1, a2, a3)):
        across[(place[2] + SIDE - k) % SIDE] = a[...]
    for c in range(2):
        total = None
        for j in range(SIDE):
            part = matmul(across[(place[0] + SIDE - j) % SIDE], weights[2 * j + c][...])
            total = part if total is None else total + part
        first = 2 * ((place[1] + c) % 2)
        sums[first] = total[:, :256]
        sums[first + 1] = total[:, 256:]
    own[...] = sums[place[3]]
    for j, o in enumerate((o1, o2, o3)):
        o[...] = sums[(place[3] + j + 1) % SIDE].astype(bf16)


def total_body(own, g1, g2, g3, out):
    out[...] = (
        own[...] + g1[...].astype(f32) + g2[...].astype(f32) + g3[...].astype(f32)
    ).astype(bf16)


def layer(
    frames,
    span_source,
    adapter_weight,
    adapter_bias,
    norm_gain,
    qkv_weight,
    out_weight,
    k_cache,
    v_cache,
    lengths,
):
    rows = frames.shape[0]
    cols = adapter_weight.shape[1]
    meetings = lengths.shape[0]
    new = rows // meetings
    heads = 2 * SIDE
    ctx_rank = lax.axis_index("ctx")
    wt_rank = lax.axis_index("wt")
    place = jnp.stack(
        [wt_rank // 2, wt_rank % 2, ctx_rank // SIDE, ctx_rank % SIDE]
    ).astype(jnp.int32)

    positions = (lengths[:, None] + jnp.arange(new, dtype=jnp.int32)[None, :]).reshape(rows)
    half = HEAD // 2
    freq = 10000.0 ** (-2.0 * jnp.arange(half, dtype=f32) / HEAD)
    angle = positions.astype(f32)[:, None] * freq[None, :]
    cosine = jnp.cos(angle)
    sine = jnp.sin(angle)
    cosine = jnp.concatenate([cosine, cosine], axis=-1)
    sine = jnp.concatenate([-sine, sine], axis=-1)

    by_kind = jnp.transpose(qkv_weight, (1, 0, 2))
    feats = by_kind.shape[1]
    adapted, query_weight, other_weight = kernel_call(
        adapter_body,
        [
            (SMEM, span_source),
            (VMEM, frames),
            (VMEM, adapter_weight),
            (VMEM, adapter_bias.reshape(1, cols)),
            (ANY, by_kind),
        ],
        (near((rows, cols), bf16), near((feats, cols), bf16), near((2, feats, cols), bf16)),
        [pltpu.VMEM(frames.shape, bf16), pltpu.SemaphoreType.DMA((2,))],
    )
    column = stacked(from_ring(adapted, y_shift))
    stacks = from_ring(column, z_shift)

    query_weights = over_x(query_weight)
    other_weights = over_x(other_weight)
    swapped = swap_xy(out_weight)
    out_weights = over_x(swapped)

    gain = norm_gain.reshape(SIDE * SIDE, 1, cols)
    query, normed = kernel_call(
        query_body,
        [(SMEM, place)]
        + [(VMEM, s) for s in stacks]
        + [(VMEM, gain), (VMEM, cosine), (VMEM, sine)]
        + [(VMEM, w) for w in query_weights],
        (near((rows, cols), bf16), near((SIDE * SIDE, rows, cols), bf16)),
    )
    query_column = stacked(from_ring(query, y_shift))
    query_stacks = from_ring(query_column, z_shift)

    keys, values = kernel_call(
        key_value_body,
        [(SMEM, place), (VMEM, normed), (VMEM, cosine), (VMEM, sine)]
        + [(VMEM, w) for w in other_weights],
        (far((rows, cols), bf16), far((rows, cols), bf16)),
    )

    def history(step):
        return kernel_call(
            lambda *refs: history_body(step, *refs),
            [
                (SMEM, place),
                (SMEM, lengths),
                (VMEM, query_stacks[step]),
                (VMEM, k_cache),
                (VMEM, v_cache),
            ],
            near((heads * rows + 48, HEAD), bf16),
            [
                pltpu.VMEM((heads, rows, HEAD), f32),
                pltpu.VMEM((heads, rows, HEAD), bf16),
            ],
        )

    own = history(0)
    back = {j: z_shift(history(j), -j) for j in ORDER}
    block = near((2 * rows + 16, HEAD), bf16)
    mixed = kernel_call(
        row_mix_body,
        [(VMEM, p) for p in (own, back[1], back[2], back[3])],
        (block, block, block, block),
    )
    returned = {k: y_shift(mixed[k], -k) for k in ORDER}
    numer, new_stats = kernel_call(
        new_part_body,
        [(VMEM, query), (VMEM, keys), (VMEM, values)],
        (near((2 * rows, HEAD), f32), near((8, rows), f32)),
    )
    attended = kernel_call(
        final_mix_body,
        [(VMEM, p) for p in (mixed[0], returned[1], returned[2], returned[3], numer, new_stats)],
        near((rows, cols), bf16),
    )
    across = from_ring(attended, y_shift)
    part = near((rows, cols), bf16)
    sums = kernel_call(
        project_body,
        [(SMEM, place)] + [(VMEM, a) for a in across] + [(VMEM, w) for w in out_weights],
        (near((rows, cols), f32), part, part, part),
        [pltpu.VMEM((SIDE, rows, cols), bf16), pltpu.VMEM((SIDE, rows, cols), f32)],
    )
    got = [z_shift(sums[j], j) for j in ORDER]
    attn_out = kernel_call(
        total_body, [(VMEM, p) for p in (sums[0], *got)], far((rows, cols), bf16)
    )
    return attn_out, keys, values


def solution(mesh):
    return jax.shard_map(
        layer,
        mesh=mesh,
        in_specs=(
            P("wt", None),
            P("wt"),
            P(None, "ctx"),
            P("ctx"),
            P(),
            P("wt", None, "ctx"),
            P("ctx", "wt"),
            P("wt", "ctx", None),
            P("wt", "ctx", None),
            P("wt"),
        ),
        out_specs=(P("wt", "ctx"), P("wt", "ctx"), P("wt", "ctx")),
        check_vma=False,
    )
```

profile of v0, /device:TPU:0, one launch (start us, length us, event | category | flops | bytes accessed | tf_op | source)
XLA Modules:
  0.0 160.5 jit_solution(8792813497794290434)
XLA Ops:
  0.7 1.1 copy-done.3
  1.8 1.1 copy-done.4
  2.9 1.0 copy-done.5
  3.8 0.7 copy-done.14
  5.2 0.9 shard_map.121
  6.1 1.8 %collective-permute-start = (bf16[128,256]{1,0:T(8,128)(2,1)S(1)}, bf16[128,256]{1,0:T(8,128)(2,1)S(1)}, u32[]{:S(2)}, u32[]{:S(2)}) collective-permute-start(bf16[128,256]{1,0:T(8,128)(2,1)S(1)} %get-tuple-element.20.a0), channel_id=1, source_target_pairs={{0,32},{8,40},{16,48},{24,56},{32,64},{40,72},{48,80},{56,88},{64,... | collective-permute-start | bytes 196616 | tf_op jit(solution)/shard_map/ppermute | solution.py:21
  7.8 2.9 %collective-permute-start.1 = (bf16[128,256]{1,0:T(8,128)(2,1)S(1)}, bf16[128,256]{1,0:T(8,128)(2,1)S(1)}, u32[]{:S(2)}, u32[]{:S(2)}) collective-permute-start(bf16[128,256]{1,0:T(8,128)(2,1)S(1)} %get-tuple-element.20.a0), channel_id=1, source_target_pairs={{0,64},{8,72},{16,80},{24,88},{32,96},{40,104},{48,112},{56,120},{... | collective-permute-start | bytes 196616 | tf_op jit(solution)/shard_map/ppermute | solution.py:21
  10.7 1.3 collective-permute-start.2
  12.1 3.0 %collective-permute-start.9 = (bf16[512,256]{1,0:T(8,128)(2,1)S(1)}, bf16[512,256]{1,0:T(8,128)(2,1)S(1)}, u32[]{:S(2)}, u32[]{:S(2)}) collective-permute-start(bf16[512,256]{1,0:T(8,128)(2,1)S(1)} %get-tuple-element.21.rest_0_), channel_id=1, source_target_pairs={{0,4},{1,5},{2,6},{3,7},{4,0},{5,1},{6,2},{7,3},{8,12},{9,13},{10,... | collective-permute-start | bytes 786440 | tf_op jit(solution)/shard_map/ppermute | solution.py:33
  15.1 1.1 collective-permute-start.11
  16.2 0.9 collective-permute-start.7
  17.2 2.0 %collective-permute-start.3 = (bf16[4,128,256]{2,1,0:T(8,128)(2,1)S(1)}, bf16[4,128,256]{2,1,0:T(8,128)(2,1)S(1)}, u32[]{:S(2)}, u32[]{:S(2)}) collective-permute-start(bf16[4,128,256]{2,1,0:T(8,128)(2,1)S(1)} %shard_map.122.s0), channel_id=1, source_target_pairs={{0,8},{8,16},{16,24},{24,0},{32,40},{40,48},{48,56},{56,32},{64,72... | collective-permute-start | bytes 786440 | tf_op jit(solution)/shard_map/ppermute | solution.py:28
  19.3 3.4 %collective-permute-done.9.rest_4_ = bf16[512,256]{1,0:T(8,128)(2,1)S(1)} collective-permute-done((bf16[512,256]{1,0:T(8,128)(2,1)S(1)}, bf16[512,256]{1,0:T(8,128)(2,1)S(1)}, u32[]{:S(2)}, u32[]{:S(2)}) %collective-permute-start.9) | collective-permute-done | bytes 262176 | tf_op jit(solution)/shard_map/ppermute | solution.py:33
  22.8 3.9 %collective-permute-start.4 = (bf16[4,128,256]{2,1,0:T(8,128)(2,1)S(1)}, bf16[4,128,256]{2,1,0:T(8,128)(2,1)}, u32[]{:S(2)}, u32[]{:S(2)}) collective-permute-start(bf16[4,128,256]{2,1,0:T(8,128)(2,1)S(1)} %shard_map.122.s0), channel_id=1, source_target_pairs={{0,16},{8,24},{16,0},{24,8},{32,48},{40,56},{48,32},{56,40},{64,80... | collective-permute-start | bytes 786440 | tf_op jit(solution)/shard_map/ppermute | solution.py:28
  26.6 4.0 %collective-permute-start.5 = (bf16[4,128,256]{2,1,0:T(8,128)(2,1)S(1)}, bf16[4,128,256]{2,1,0:T(8,128)(2,1)}, u32[]{:S(2)}, u32[]{:S(2)}) collective-permute-start(bf16[4,128,256]{2,1,0:T(8,128)(2,1)S(1)} %shard_map.122.s0), channel_id=1, source_target_pairs={{0,24},{8,0},{16,8},{24,16},{32,56},{40,32},{48,40},{56,48},{64,88... | collective-permute-start | bytes 786440 | tf_op jit(solution)/shard_map/ppermute | solution.py:28
  30.7 0.7 copy-done.6
  31.9 0.7 copy-done.8
  32.6 1.0 fusion
  33.6 1.2 pad_maximum_fusion
  35.1 1.0 collective-permute-start.26
  36.3 1.1 collective-permute-done.5.s3
  37.4 0.9 copy-done.7
  38.3 0.9 copy-done.9
  39.3 2.5 %shard_map.123 = (bf16[128,256]{1,0:T(8,128)(2,1)S(1)}, bf16[16,128,256]{2,1,0:T(8,128)(2,1)S(1)}) custom-call(s32[4]{0:T(128)S(1)} %pad_add_fusion.place.refs_0_, bf16[4,128,256]{2,1,0:T(8,128)(2,1)S(1)} %shard_map.122.s0, bf16[4,128,256]{2,1,0:T(8,128)(2,1)S(1)} %copy-done.9, bf16[4,128,256]{2,1,0:T(8,128)(2,1)} %collective-permute-done.4.s2, ...), custom_call_target="tpu_custom_call" | custom-call | tf_op jit(solution)/shard_map/pallas_call | solution.py:78
  41.7 0.7 collective-permute-start.13
  42.5 2.5 %collective-permute-start.28 = (bf16[2,512,256]{2,1,0:T(8,128)(2,1)S(1)}, bf16[2,512,256]{2,1,0:T(8,128)(2,1)S(1)}, u32[]{:S(2)}, u32[]{:S(2)}) collective-permute-start(bf16[2,512,256]{2,1,0:T(8,128)(2,1)S(1)} %get-tuple-element.28.rest_0_), channel_id=1, source_target_pairs={{0,4},{1,5},{2,6},{3,7},{4,0},{5,1},{6,2},{7,3},{8,12},{9,13},{10,... | collective-permute-start | bytes 1572872 | tf_op jit(solution)/shard_map/ppermute | solution.py:33
  45.0 2.1 %collective-permute-start.30 = (bf16[2,512,256]{2,1,0:T(8,128)(2,1)S(1)}, bf16[2,512,256]{2,1,0:T(8,128)(2,1)S(1)}, u32[]{:S(2)}, u32[]{:S(2)}) collective-permute-start(bf16[2,512,256]{2,1,0:T(8,128)(2,1)S(1)} %get-tuple-element.28.rest_0_), channel_id=1, source_target_pairs={{0,6},{1,7},{2,0},{3,1},{4,2},{5,3},{6,4},{7,5},{8,14},{9,15},{10,... | collective-permute-start | bytes 1572872 | tf_op jit(solution)/shard_map/ppermute | solution.py:33
  47.1 0.7 collective-permute-start.35
  47.8 5.8 %collective-permute-start.14 = (bf16[128,256]{1,0:T(8,128)(2,1)S(1)}, bf16[128,256]{1,0:T(8,128)(2,1)S(1)}, u32[]{:S(2)}, u32[]{:S(2)}) collective-permute-start(bf16[128,256]{1,0:T(8,128)(2,1)S(1)} %get-tuple-element.22.a0.query), channel_id=1, source_target_pairs={{0,64},{8,72},{16,80},{24,88},{32,96},{40,104},{48,112},{56,120},{... | collective-permute-start | bytes 196616 | tf_op jit(solution)/shard_map/ppermute | solution.py:21
  53.6 2.2 %collective-permute-done.14.a2 = bf16[128,256]{1,0:T(8,128)(2,1)S(1)} collective-permute-done((bf16[128,256]{1,0:T(8,128)(2,1)S(1)}, bf16[128,256]{1,0:T(8,128)(2,1)S(1)}, u32[]{:S(2)}, u32[]{:S(2)}) %collective-permute-start.14) | collective-permute-done | bytes 65568 | tf_op jit(solution)/shard_map/ppermute | solution.py:21
  55.9 1.7 %collective-permute-start.15 = (bf16[128,256]{1,0:T(8,128)(2,1)S(1)}, bf16[128,256]{1,0:T(8,128)(2,1)S(1)}, u32[]{:S(2)}, u32[]{:S(2)}) collective-permute-start(bf16[128,256]{1,0:T(8,128)(2,1)S(1)} %get-tuple-element.22.a0.query), channel_id=1, source_target_pairs={{0,96},{8,104},{16,112},{24,120},{32,0},{40,8},{48,16},{56,24},{64... | collective-permute-start | bytes 196616 | tf_op jit(solution)/shard_map/ppermute | solution.py:21
  57.6 2.5 %collective-permute-done.15.a3 = bf16[128,256]{1,0:T(8,128)(2,1)S(1)} collective-permute-done((bf16[128,256]{1,0:T(8,128)(2,1)S(1)}, bf16[128,256]{1,0:T(8,128)(2,1)S(1)}, u32[]{:S(2)}, u32[]{:S(2)}) %collective-permute-start.15) | collective-permute-done | bytes 65568 | tf_op jit(solution)/shard_map/ppermute | solution.py:21
  60.7 14.4 %collective-permute-start.37 = (bf16[256,512]{1,0:T(8,128)(2,1)S(1)}, bf16[256,512]{1,0:T(8,128)(2,1)S(1)}, u32[]{:S(2)}, u32[]{:S(2)}) collective-permute-start(bf16[256,512]{1,0:T(8,128)(2,1)S(1)} %collective-permute-done.35.rest_0_), channel_id=1, source_target_pairs={{0,2},{1,3},{2,4},{3,5},{4,6},{5,7},{6,0},{7,1},{8,10},{9,11},{10,... | collective-permute-start | bytes 786440 | tf_op jit(solution)/shard_map/ppermute | solution.py:33
  75.1 12.2 %collective-permute-start.39 = (bf16[256,512]{1,0:T(8,128)(2,1)S(1)}, bf16[256,512]{1,0:T(8,128)(2,1)S(1)}, u32[]{:S(2)}, u32[]{:S(2)}) collective-permute-start(bf16[256,512]{1,0:T(8,128)(2,1)S(1)} %collective-permute-done.35.rest_0_), channel_id=1, source_target_pairs={{0,4},{1,5},{2,6},{3,7},{4,0},{5,1},{6,2},{7,3},{8,12},{9,13},{10,... | collective-permute-start | bytes 786440 | tf_op jit(solution)/shard_map/ppermute | solution.py:33
  87.3 4.4 %collective-permute-start.18 = (bf16[4,128,256]{2,1,0:T(8,128)(2,1)S(1)}, bf16[4,128,256]{2,1,0:T(8,128)(2,1)S(1)}, u32[]{:S(2)}, u32[]{:S(2)}) collective-permute-start(bf16[4,128,256]{2,1,0:T(8,128)(2,1)S(1)} %shard_map.124.refs_2_), channel_id=1, source_target_pairs={{0,16},{8,24},{16,0},{24,8},{32,48},{40,56},{48,32},{56,40},{64,80... | collective-permute-start | bytes 786440 | tf_op jit(solution)/shard_map/ppermute | solution.py:28
  91.7 1.6 copy-done.1
  93.2 1.3 shard_map.126
  94.6 0.7 collective-permute-start.17
  95.3 5.7 %collective-permute-start.41 = (bf16[256,512]{1,0:T(8,128)(2,1)S(1)}, bf16[256,512]{1,0:T(8,128)(2,1)S(1)}, u32[]{:S(2)}, u32[]{:S(2)}) collective-permute-start(bf16[256,512]{1,0:T(8,128)(2,1)S(1)} %collective-permute-done.35.rest_0_), channel_id=1, source_target_pairs={{0,6},{1,7},{2,0},{3,1},{4,2},{5,3},{6,4},{7,5},{8,14},{9,15},{10,... | collective-permute-start | bytes 786440 | tf_op jit(solution)/shard_map/ppermute | solution.py:33
  101.5 2.4 %collective-permute-done.20.refs_2_ = bf16[4,128,256]{2,1,0:T(8,128)(2,1)S(1)} collective-permute-done((bf16[4,128,256]{2,1,0:T(8,128)(2,1)S(1)}, bf16[4,128,256]{2,1,0:T(8,128)(2,1)S(1)}, u32[]{:S(2)}, u32[]{:S(2)}) %collective-permute-start.20) | collective-permute-done | bytes 262176 | tf_op jit(solution)/shard_map/ppermute | solution.py:28
  103.9 1.3 shard_map.127
  105.2 1.3 shard_map.128
  106.5 1.2 collective-permute-start.19
  108.7 8.9 %collective-permute-done.19.p2 = bf16[1072,128]{1,0:T(8,128)(2,1)S(1)} collective-permute-done((bf16[1072,128]{1,0:T(8,128)(2,1)S(1)}, bf16[1072,128]{1,0:T(8,128)(2,1)S(1)}, u32[]{:S(2)}, u32[]{:S(2)}) %collective-permute-start.19) | collective-permute-done | bytes 274464 | tf_op jit(solution)/shard_map/ppermute | solution.py:28
  117.6 5.4 %collective-permute-done.21.p3 = bf16[1072,128]{1,0:T(8,128)(2,1)S(1)} collective-permute-done((bf16[1072,128]{1,0:T(8,128)(2,1)S(1)}, bf16[1072,128]{1,0:T(8,128)(2,1)S(1)}, u32[]{:S(2)}, u32[]{:S(2)}) %collective-permute-start.21) | collective-permute-done | bytes 274464 | tf_op jit(solution)/shard_map/ppermute | solution.py:28
  123.0 1.3 shard_map.125.p0
  124.3 0.8 shard_map.129
  125.9 3.9 %collective-permute-done.22.p1 = bf16[272,128]{1,0:T(8,128)(2,1)S(1)} collective-permute-done((bf16[272,128]{1,0:T(8,128)(2,1)S(1)}, bf16[272,128]{1,0:T(8,128)(2,1)S(1)}, u32[]{:S(2)}, u32[]{:S(2)}) %collective-permute-start.22) | collective-permute-done | bytes 69664 | tf_op jit(solution)/shard_map/ppermute | solution.py:21
  129.8 5.8 %collective-permute-done.23.p2 = bf16[272,128]{1,0:T(8,128)(2,1)S(1)} collective-permute-done((bf16[272,128]{1,0:T(8,128)(2,1)S(1)}, bf16[272,128]{1,0:T(8,128)(2,1)S(1)}, u32[]{:S(2)}, u32[]{:S(2)}) %collective-permute-start.23) | collective-permute-done | bytes 69664 | tf_op jit(solution)/shard_map/ppermute | solution.py:21
  135.6 2.0 %shard_map.130 = (bf16[128,256]{1,0:T(8,128)(2,1)}, bf16[128,256]{1,0:T(8,128)(2,1)}) custom-call(s32[4]{0:T(128)S(1)} %pad_add_fusion.place.refs_0_, bf16[16,128,256]{2,1,0:T(8,128)(2,1)S(1)} %get-tuple-element.27.normed, f32[128,128]{1,0:T(8,128)S(1)} %get-tuple-element.40.cosine, f32[128,128]{1,0:T(8,128)S(1)} %get-tuple-element.41.sine, ...), custom_call_target="tpu_custom_call" | custom-call | tf_op jit(solution)/shard_map/pallas_call | solution.py:78
  137.6 0.8 copy-done.10
  138.4 0.8 copy-done.11
  139.2 1.0 shard_map.131
  140.2 0.9 collective-permute-done.24.p3
  141.6 3.8 %collective-permute-start.33 = (bf16[128,256]{1,0:T(8,128)(2,1)S(1)}, bf16[128,256]{1,0:T(8,128)(2,1)S(1)}, u32[]{:S(2)}, u32[]{:S(2)}) collective-permute-start(bf16[128,256]{1,0:T(8,128)(2,1)S(1)} %shard_map.132.a0), channel_id=1, source_target_pairs={{0,64},{8,72},{16,80},{24,88},{32,96},{40,104},{48,112},{56,120},{... | collective-permute-start | bytes 196616 | tf_op jit(solution)/shard_map/ppermute | solution.py:21
  145.4 0.9 collective-permute-start.34
  146.3 0.7 collective-permute-done.32.a1
  147.1 1.3 collective-permute-done.33.a2
  148.4 1.3 collective-permute-done.34.a3
  149.7 1.0 shard_map.133
  150.8 3.2 %collective-permute-start.44 = (bf16[128,256]{1,0:T(8,128)(2,1)S(1)}, bf16[128,256]{1,0:T(8,128)(2,1)S(1)}, u32[]{:S(2)}, u32[]{:S(2)}) collective-permute-start(bf16[128,256]{1,0:T(8,128)(2,1)S(1)} %get-tuple-element.35), channel_id=1, source_target_pairs={{0,24},{8,0},{16,8},{24,16},{32,56},{40,32},{48,40},{56,48},{64,88... | collective-permute-start | bytes 196616 | tf_op jit(solution)/shard_map/ppermute | solution.py:28
  154.0 2.3 %collective-permute-done.43.g1 = bf16[128,256]{1,0:T(8,128)(2,1)S(1)} collective-permute-done((bf16[128,256]{1,0:T(8,128)(2,1)S(1)}, bf16[128,256]{1,0:T(8,128)(2,1)S(1)}, u32[]{:S(2)}, u32[]{:S(2)}) %collective-permute-start.43) | collective-permute-done | bytes 65568 | tf_op jit(solution)/shard_map/ppermute | solution.py:28
  156.5 3.3 %collective-permute-done.45.g3 = bf16[128,256]{1,0:T(8,128)(2,1)S(1)} collective-permute-done((bf16[128,256]{1,0:T(8,128)(2,1)S(1)}, bf16[128,256]{1,0:T(8,128)(2,1)S(1)}, u32[]{:S(2)}, u32[]{:S(2)}) %collective-permute-start.45) | collective-permute-done | bytes 65568 | tf_op jit(solution)/shard_map/ppermute | solution.py:28
  159.8 0.7 shard_map.134
  (82 shorter events, 5.5 us)
Async XLA Ops:
  0.6 18.5 %copy-start.13 = (s32[2]{0:T(128)S(1)}, s32[2]{0:T(128)}, u32[]{:S(2)}) copy-start(s32[2]{0:T(128)} %refs_1_.7) | copy-start | bytes 28
  0.6 1.1 copy-start.3
  1.8 1.1 copy-start.4
  2.9 1.0 copy-start.5
  3.8 0.7 copy-start.14
  4.5 0.7 copy-start.15
  5.2 32.2 %copy-start.12 = (f32[4096]{0:T(1024)S(1)}, f32[4096]{0:T(1024)}, u32[]{:S(2)}) copy-start(f32[4096]{0:T(1024)} %param.14) | copy-start | bytes 49156
  6.1 10.2 %collective-permute-start = (bf16[128,256]{1,0:T(8,128)(2,1)S(1)}, bf16[128,256]{1,0:T(8,128)(2,1)S(1)}, u32[]{:S(2)}, u32[]{:S(2)}) collective-permute-start(bf16[128,256]{1,0:T(8,128)(2,1)S(1)} %get-tuple-element.20.a0), channel_id=1, source_target_pairs={{0,32},{8,40},{16,48},{24,56},{32,64},{40,72},{48,80},{56,88},{64,... | collective-permute-start | bytes 196616 | tf_op jit(solution)/shard_map/ppermute | solution.py:21
  7.8 9.3 %collective-permute-start.1 = (bf16[128,256]{1,0:T(8,128)(2,1)S(1)}, bf16[128,256]{1,0:T(8,128)(2,1)S(1)}, u32[]{:S(2)}, u32[]{:S(2)}) collective-permute-start(bf16[128,256]{1,0:T(8,128)(2,1)S(1)} %get-tuple-element.20.a0), channel_id=1, source_target_pairs={{0,64},{8,72},{16,80},{24,88},{32,96},{40,104},{48,112},{56,120},{... | collective-permute-start | bytes 196616 | tf_op jit(solution)/shard_map/ppermute | solution.py:21
  10.7 6.4 %collective-permute-start.2 = (bf16[128,256]{1,0:T(8,128)(2,1)S(1)}, bf16[128,256]{1,0:T(8,128)(2,1)S(1)}, u32[]{:S(2)}, u32[]{:S(2)}) collective-permute-start(bf16[128,256]{1,0:T(8,128)(2,1)S(1)} %get-tuple-element.20.a0), channel_id=1, source_target_pairs={{0,96},{8,104},{16,112},{24,120},{32,0},{40,8},{48,16},{56,24},{64... | collective-permute-start | bytes 196616 | tf_op jit(solution)/shard_map/ppermute | solution.py:21
  12.1 10.7 %collective-permute-start.9 = (bf16[512,256]{1,0:T(8,128)(2,1)S(1)}, bf16[512,256]{1,0:T(8,128)(2,1)S(1)}, u32[]{:S(2)}, u32[]{:S(2)}) collective-permute-start(bf16[512,256]{1,0:T(8,128)(2,1)S(1)} %get-tuple-element.21.rest_0_), channel_id=1, source_target_pairs={{0,4},{1,5},{2,6},{3,7},{4,0},{5,1},{6,2},{7,3},{8,12},{9,13},{10,... | collective-permute-start | bytes 786440 | tf_op jit(solution)/shard_map/ppermute | solution.py:33
  15.1 11.5 %collective-permute-start.11 = (bf16[512,256]{1,0:T(8,128)(2,1)S(1)}, bf16[512,256]{1,0:T(8,128)(2,1)}, u32[]{:S(2)}, u32[]{:S(2)}) collective-permute-start(bf16[512,256]{1,0:T(8,128)(2,1)S(1)} %get-tuple-element.21.rest_0_), channel_id=1, source_target_pairs={{0,6},{1,7},{2,0},{3,1},{4,2},{5,3},{6,4},{7,5},{8,14},{9,15},{10,... | collective-permute-start | bytes 786440 | tf_op jit(solution)/shard_map/ppermute | solution.py:33
  16.2 14.4 %collective-permute-start.7 = (bf16[512,256]{1,0:T(8,128)(2,1)S(1)}, bf16[512,256]{1,0:T(8,128)(2,1)}, u32[]{:S(2)}, u32[]{:S(2)}) collective-permute-start(bf16[512,256]{1,0:T(8,128)(2,1)S(1)} %get-tuple-element.21.rest_0_), channel_id=1, source_target_pairs={{0,2},{1,3},{2,4},{3,5},{4,6},{5,7},{6,0},{7,1},{8,10},{9,11},{10,... | collective-permute-start | bytes 786440 | tf_op jit(solution)/shard_map/ppermute | solution.py:33
  17.1 13.6 %collective-permute-start.6 = (bf16[512,256]{1,0:T(8,128)(2,1)S(1)}, bf16[512,256]{1,0:T(8,128)(2,1)S(1)}, u32[]{:S(2)}, u32[]{:S(2)}) collective-permute-start(bf16[512,256]{1,0:T(8,128)(2,1)S(1)} %get-tuple-element.21.rest_0_), channel_id=1, source_target_pairs={{0,1},{1,0},{2,3},{3,2},{4,5},{5,4},{6,7},{7,6},{8,9},{9,8},{10,11... | collective-permute-start | bytes 786440 | tf_op jit(solution)/shard_map/ppermute | solution.py:37
  17.2 14.8 %collective-permute-start.3 = (bf16[4,128,256]{2,1,0:T(8,128)(2,1)S(1)}, bf16[4,128,256]{2,1,0:T(8,128)(2,1)S(1)}, u32[]{:S(2)}, u32[]{:S(2)}) collective-permute-start(bf16[4,128,256]{2,1,0:T(8,128)(2,1)S(1)} %shard_map.122.s0), channel_id=1, source_target_pairs={{0,8},{8,16},{16,24},{24,0},{32,40},{40,48},{48,56},{56,32},{64,72... | collective-permute-start | bytes 786440 | tf_op jit(solution)/shard_map/ppermute | solution.py:28
  22.8 12.4 %collective-permute-start.4 = (bf16[4,128,256]{2,1,0:T(8,128)(2,1)S(1)}, bf16[4,128,256]{2,1,0:T(8,128)(2,1)}, u32[]{:S(2)}, u32[]{:S(2)}) collective-permute-start(bf16[4,128,256]{2,1,0:T(8,128)(2,1)S(1)} %shard_map.122.s0), channel_id=1, source_target_pairs={{0,16},{8,24},{16,0},{24,8},{32,48},{40,56},{48,32},{56,40},{64,80... | collective-permute-start | bytes 786440 | tf_op jit(solution)/shard_map/ppermute | solution.py:28
  26.6 10.7 %collective-permute-start.5 = (bf16[4,128,256]{2,1,0:T(8,128)(2,1)S(1)}, bf16[4,128,256]{2,1,0:T(8,128)(2,1)}, u32[]{:S(2)}, u32[]{:S(2)}) collective-permute-start(bf16[4,128,256]{2,1,0:T(8,128)(2,1)S(1)} %shard_map.122.s0), channel_id=1, source_target_pairs={{0,24},{8,0},{16,8},{24,16},{32,56},{40,32},{48,40},{56,48},{64,88... | collective-permute-start | bytes 786440 | tf_op jit(solution)/shard_map/ppermute | solution.py:28
  30.7 6.7 %collective-permute-start.10 = (bf16[512,256]{1,0:T(8,128)(2,1)S(1)}, bf16[512,256]{1,0:T(8,128)(2,1)}, u32[]{:S(2)}, u32[]{:S(2)}) collective-permute-start(bf16[512,256]{1,0:T(8,128)(2,1)S(1)} %collective-permute-done.9.rest_4_), channel_id=1, source_target_pairs={{0,1},{1,0},{2,3},{3,2},{4,5},{5,4},{6,7},{7,6},{8,9},{9,8},{10,11... | collective-permute-start | bytes 786440 | tf_op jit(solution)/shard_map/ppermute | solution.py:37
  30.7 0.7 copy-start.6
  31.4 5.9 %collective-permute-start.12 = (bf16[512,256]{1,0:T(8,128)(2,1)}, bf16[512,256]{1,0:T(8,128)(2,1)}, u32[]{:S(2)}, u32[]{:S(2)}) collective-permute-start(bf16[512,256]{1,0:T(8,128)(2,1)} %collective-permute-done.11.rest_6_), channel_id=1, source_target_pairs={{0,1},{1,0},{2,3},{3,2},{4,5},{5,4},{6,7},{7,6},{8,9},{9,8},{10,11... | collective-permute-start | bytes 786440 | tf_op jit(solution)/shard_map/ppermute | solution.py:37
  31.9 0.7 copy-start.8
  32.6 4.7 %collective-permute-start.8 = (bf16[512,256]{1,0:T(8,128)(2,1)}, bf16[512,256]{1,0:T(8,128)(2,1)}, u32[]{:S(2)}, u32[]{:S(2)}) collective-permute-start(bf16[512,256]{1,0:T(8,128)(2,1)} %collective-permute-done.7.rest_2_), channel_id=1, source_target_pairs={{0,1},{1,0},{2,3},{3,2},{4,5},{5,4},{6,7},{7,6},{8,9},{9,8},{10,11... | collective-permute-start | bytes 786440 | tf_op jit(solution)/shard_map/ppermute | solution.py:37
  33.6 58.1 %copy-start = (bf16[2,128,4096]{2,1,0:T(8,128)(2,1)S(1)}, bf16[2,128,4096]{2,1,0:T(8,128)(2,1)}, u32[]{:S(2)}) copy-start(bf16[2,128,4096]{2,1,0:T(8,128)(2,1)} %refs_3_.7) | copy-start | bytes 6291460
  35.1 25.6 %collective-permute-start.26 = (bf16[2,512,256]{2,1,0:T(8,128)(2,1)S(1)}, bf16[2,512,256]{2,1,0:T(8,128)(2,1)S(1)}, u32[]{:S(2)}, u32[]{:S(2)}) collective-permute-start(bf16[2,512,256]{2,1,0:T(8,128)(2,1)S(1)} %get-tuple-element.28.rest_0_), channel_id=1, source_target_pairs={{0,2},{1,3},{2,4},{3,5},{4,6},{5,7},{6,0},{7,1},{8,10},{9,11},{10,... | collective-permute-start | bytes 1572872 | tf_op jit(solution)/shard_map/ppermute | solution.py:33
  37.4 1.0 copy-start.7
  38.3 0.9 copy-start.9
  39.3 7.9 %copy-start.16 = (bf16[256,512]{1,0:T(8,128)(2,1)S(1)}, bf16[256,512]{1,0:T(8,128)(2,1)}, u32[]{:S(2)}) copy-start(bf16[256,512]{1,0:T(8,128)(2,1)} %param.16) | copy-start | bytes 786436
  41.7 6.1 %collective-permute-start.13 = (bf16[128,256]{1,0:T(8,128)(2,1)S(1)}, bf16[128,256]{1,0:T(8,128)(2,1)S(1)}, u32[]{:S(2)}, u32[]{:S(2)}) collective-permute-start(bf16[128,256]{1,0:T(8,128)(2,1)S(1)} %get-tuple-element.22.a0.query), channel_id=1, source_target_pairs={{0,32},{8,40},{16,48},{24,56},{32,64},{40,72},{48,80},{56,88},{64,... | collective-permute-start | bytes 196616 | tf_op jit(solution)/shard_map/ppermute | solution.py:21
  42.5 32.6 %collective-permute-start.28 = (bf16[2,512,256]{2,1,0:T(8,128)(2,1)S(1)}, bf16[2,512,256]{2,1,0:T(8,128)(2,1)S(1)}, u32[]{:S(2)}, u32[]{:S(2)}) collective-permute-start(bf16[2,512,256]{2,1,0:T(8,128)(2,1)S(1)} %get-tuple-element.28.rest_0_), channel_id=1, source_target_pairs={{0,4},{1,5},{2,6},{3,7},{4,0},{5,1},{6,2},{7,3},{8,12},{9,13},{10,... | collective-permute-start | bytes 1572872 | tf_op jit(solution)/shard_map/ppermute | solution.py:33
  45.0 42.2 %collective-permute-start.30 = (bf16[2,512,256]{2,1,0:T(8,128)(2,1)S(1)}, bf16[2,512,256]{2,1,0:T(8,128)(2,1)S(1)}, u32[]{:S(2)}, u32[]{:S(2)}) collective-permute-start(bf16[2,512,256]{2,1,0:T(8,128)(2,1)S(1)} %get-tuple-element.28.rest_0_), channel_id=1, source_target_pairs={{0,6},{1,7},{2,0},{3,1},{4,2},{5,3},{6,4},{7,5},{8,14},{9,15},{10,... | collective-permute-start | bytes 1572872 | tf_op jit(solution)/shard_map/ppermute | solution.py:33
  47.1 13.0 %collective-permute-start.35 = (bf16[256,512]{1,0:T(8,128)(2,1)S(1)}, bf16[256,512]{1,0:T(8,128)(2,1)S(1)}, u32[]{:S(2)}, u32[]{:S(2)}) collective-permute-start(bf16[256,512]{1,0:T(8,128)(2,1)S(1)} %copy-done.16), channel_id=1, source_target_pairs={{0,0},{1,1},{8,8},{9,9},{16,16},{17,17},{24,24},{25,25},{32,2},{33... | collective-permute-start | bytes 786440 | tf_op jit(solution)/shard_map/ppermute | solution.py:51
  47.8 8.1 %collective-permute-start.14 = (bf16[128,256]{1,0:T(8,128)(2,1)S(1)}, bf16[128,256]{1,0:T(8,128)(2,1)S(1)}, u32[]{:S(2)}, u32[]{:S(2)}) collective-permute-start(bf16[128,256]{1,0:T(8,128)(2,1)S(1)} %get-tuple-element.22.a0.query), channel_id=1, source_target_pairs={{0,64},{8,72},{16,80},{24,88},{32,96},{40,104},{48,112},{56,120},{... | collective-permute-start | bytes 196616 | tf_op jit(solution)/shard_map/ppermute | solution.py:21
  55.9 4.3 %collective-permute-start.15 = (bf16[128,256]{1,0:T(8,128)(2,1)S(1)}, bf16[128,256]{1,0:T(8,128)(2,1)S(1)}, u32[]{:S(2)}, u32[]{:S(2)}) collective-permute-start(bf16[128,256]{1,0:T(8,128)(2,1)S(1)} %get-tuple-element.22.a0.query), channel_id=1, source_target_pairs={{0,96},{8,104},{16,112},{24,120},{32,0},{40,8},{48,16},{56,24},{64... | collective-permute-start | bytes 196616 | tf_op jit(solution)/shard_map/ppermute | solution.py:21
  60.1 34.4 %collective-permute-start.25 = (bf16[2,512,256]{2,1,0:T(8,128)(2,1)S(1)}, bf16[2,512,256]{2,1,0:T(8,128)(2,1)S(1)}, u32[]{:S(2)}, u32[]{:S(2)}) collective-permute-start(bf16[2,512,256]{2,1,0:T(8,128)(2,1)S(1)} %get-tuple-element.28.rest_0_), channel_id=1, source_target_pairs={{0,1},{1,0},{2,3},{3,2},{4,5},{5,4},{6,7},{7,6},{8,9},{9,8},{10,11... | collective-permute-start | bytes 1572872 | tf_op jit(solution)/shard_map/ppermute | solution.py:37
  60.2 31.5 %collective-permute-start.16 = (bf16[4,128,256]{2,1,0:T(8,128)(2,1)S(1)}, bf16[4,128,256]{2,1,0:T(8,128)(2,1)S(1)}, u32[]{:S(2)}, u32[]{:S(2)}) collective-permute-start(bf16[4,128,256]{2,1,0:T(8,128)(2,1)S(1)} %shard_map.124.refs_2_), channel_id=1, source_target_pairs={{0,8},{8,16},{16,24},{24,0},{32,40},{40,48},{48,56},{56,32},{64,72... | collective-permute-start | bytes 786440 | tf_op jit(solution)/shard_map/ppermute | solution.py:28
  60.7 34.5 %collective-permute-start.37 = (bf16[256,512]{1,0:T(8,128)(2,1)S(1)}, bf16[256,512]{1,0:T(8,128)(2,1)S(1)}, u32[]{:S(2)}, u32[]{:S(2)}) collective-permute-start(bf16[256,512]{1,0:T(8,128)(2,1)S(1)} %collective-permute-done.35.rest_0_), channel_id=1, source_target_pairs={{0,2},{1,3},{2,4},{3,5},{4,6},{5,7},{6,0},{7,1},{8,10},{9,11},{10,... | collective-permute-start | bytes 786440 | tf_op jit(solution)/shard_map/ppermute | solution.py:33
  75.1 25.9 %collective-permute-start.39 = (bf16[256,512]{1,0:T(8,128)(2,1)S(1)}, bf16[256,512]{1,0:T(8,128)(2,1)S(1)}, u32[]{:S(2)}, u32[]{:S(2)}) collective-permute-start(bf16[256,512]{1,0:T(8,128)(2,1)S(1)} %collective-permute-done.35.rest_0_), channel_id=1, source_target_pairs={{0,4},{1,5},{2,6},{3,7},{4,0},{5,1},{6,2},{7,3},{8,12},{9,13},{10,... | collective-permute-start | bytes 786440 | tf_op jit(solution)/shard_map/ppermute | solution.py:33
  87.3 13.7 %collective-permute-start.18 = (bf16[4,128,256]{2,1,0:T(8,128)(2,1)S(1)}, bf16[4,128,256]{2,1,0:T(8,128)(2,1)S(1)}, u32[]{:S(2)}, u32[]{:S(2)}) collective-permute-start(bf16[4,128,256]{2,1,0:T(8,128)(2,1)S(1)} %shard_map.124.refs_2_), channel_id=1, source_target_pairs={{0,16},{8,24},{16,0},{24,8},{32,48},{40,56},{48,32},{56,40},{64,80... | collective-permute-start | bytes 786440 | tf_op jit(solution)/shard_map/ppermute | solution.py:28
  91.6 12.2 %collective-permute-start.20 = (bf16[4,128,256]{2,1,0:T(8,128)(2,1)S(1)}, bf16[4,128,256]{2,1,0:T(8,128)(2,1)S(1)}, u32[]{:S(2)}, u32[]{:S(2)}) collective-permute-start(bf16[4,128,256]{2,1,0:T(8,128)(2,1)S(1)} %shard_map.124.refs_2_), channel_id=1, source_target_pairs={{0,24},{8,0},{16,8},{24,16},{32,56},{40,32},{48,40},{56,48},{64,88... | collective-permute-start | bytes 786440 | tf_op jit(solution)/shard_map/ppermute | solution.py:28
  91.7 1.6 copy-start.1
  94.6 13.7 %collective-permute-start.17 = (bf16[1072,128]{1,0:T(8,128)(2,1)S(1)}, bf16[1072,128]{1,0:T(8,128)(2,1)S(1)}, u32[]{:S(2)}, u32[]{:S(2)}) collective-permute-start(bf16[1072,128]{1,0:T(8,128)(2,1)S(1)} %shard_map.126), channel_id=1, source_target_pairs={{0,24},{8,0},{16,8},{24,16},{32,56},{40,32},{48,40},{56,48},{64,88... | collective-permute-start | bytes 823304 | tf_op jit(solution)/shard_map/ppermute | solution.py:28
  95.3 11.2 %collective-permute-start.41 = (bf16[256,512]{1,0:T(8,128)(2,1)S(1)}, bf16[256,512]{1,0:T(8,128)(2,1)S(1)}, u32[]{:S(2)}, u32[]{:S(2)}) collective-permute-start(bf16[256,512]{1,0:T(8,128)(2,1)S(1)} %collective-permute-done.35.rest_0_), channel_id=1, source_target_pairs={{0,6},{1,7},{2,0},{3,1},{4,2},{5,3},{6,4},{7,5},{8,14},{9,15},{10,... | collective-permute-start | bytes 786440 | tf_op jit(solution)/shard_map/ppermute | solution.py:33
  101.0 24.1 %collective-permute-start.27 = (bf16[2,512,256]{2,1,0:T(8,128)(2,1)S(1)}, bf16[2,512,256]{2,1,0:T(8,128)(2,1)S(1)}, u32[]{:S(2)}, u32[]{:S(2)}) collective-permute-start(bf16[2,512,256]{2,1,0:T(8,128)(2,1)S(1)} %collective-permute-done.26.rest_2_), channel_id=1, source_target_pairs={{0,1},{1,0},{2,3},{3,2},{4,5},{5,4},{6,7},{7,6},{8,9},{9,8},{10,11... | collective-permute-start | bytes 1572872 | tf_op jit(solution)/shard_map/ppermute | solution.py:37
  101.0 24.2 %collective-permute-start.29 = (bf16[2,512,256]{2,1,0:T(8,128)(2,1)S(1)}, bf16[2,512,256]{2,1,0:T(8,128)(2,1)S(1)}, u32[]{:S(2)}, u32[]{:S(2)}) collective-permute-start(bf16[2,512,256]{2,1,0:T(8,128)(2,1)S(1)} %collective-permute-done.28.rest_4_), channel_id=1, source_target_pairs={{0,1},{1,0},{2,3},{3,2},{4,5},{5,4},{6,7},{7,6},{8,9},{9,8},{10,11... | collective-permute-start | bytes 1572872 | tf_op jit(solution)/shard_map/ppermute | solution.py:37
  103.9 21.9 %collective-permute-start.31 = (bf16[2,512,256]{2,1,0:T(8,128)(2,1)S(1)}, bf16[2,512,256]{2,1,0:T(8,128)(2,1)S(1)}, u32[]{:S(2)}, u32[]{:S(2)}) collective-permute-start(bf16[2,512,256]{2,1,0:T(8,128)(2,1)S(1)} %collective-permute-done.30.rest_6_), channel_id=1, source_target_pairs={{0,1},{1,0},{2,3},{3,2},{4,5},{5,4},{6,7},{7,6},{8,9},{9,8},{10,11... | collective-permute-start | bytes 1572872 | tf_op jit(solution)/shard_map/ppermute | solution.py:37
  105.2 17.8 %copy-start.2 = (bf16[2,128,4096]{2,1,0:T(8,128)(2,1)S(1)}, bf16[2,128,4096]{2,1,0:T(8,128)(2,1)}, u32[]{:S(2)}) copy-start(bf16[2,128,4096]{2,1,0:T(8,128)(2,1)} %refs_4_.7) | copy-start | bytes 6291460
  106.5 11.1 %collective-permute-start.19 = (bf16[1072,128]{1,0:T(8,128)(2,1)S(1)}, bf16[1072,128]{1,0:T(8,128)(2,1)S(1)}, u32[]{:S(2)}, u32[]{:S(2)}) collective-permute-start(bf16[1072,128]{1,0:T(8,128)(2,1)S(1)} %shard_map.127), channel_id=1, source_target_pairs={{0,16},{8,24},{16,0},{24,8},{32,48},{40,56},{48,32},{56,40},{64,80... | collective-permute-start | bytes 823304 | tf_op jit(solution)/shard_map/ppermute | solution.py:28
  108.2 14.7 %collective-permute-start.21 = (bf16[1072,128]{1,0:T(8,128)(2,1)S(1)}, bf16[1072,128]{1,0:T(8,128)(2,1)S(1)}, u32[]{:S(2)}, u32[]{:S(2)}) collective-permute-start(bf16[1072,128]{1,0:T(8,128)(2,1)S(1)} %shard_map.128), channel_id=1, source_target_pairs={{0,8},{8,16},{16,24},{24,0},{32,40},{40,48},{48,56},{56,32},{64,72... | collective-permute-start | bytes 823304 | tf_op jit(solution)/shard_map/ppermute | solution.py:28
  117.6 24.0 %collective-permute-start.36 = (bf16[256,512]{1,0:T(8,128)(2,1)S(1)}, bf16[256,512]{1,0:T(8,128)(2,1)S(1)}, u32[]{:S(2)}, u32[]{:S(2)}) collective-permute-start(bf16[256,512]{1,0:T(8,128)(2,1)S(1)} %collective-permute-done.35.rest_0_), channel_id=1, source_target_pairs={{0,1},{1,0},{2,3},{3,2},{4,5},{5,4},{6,7},{7,6},{8,9},{9,8},{10,11... | collective-permute-start | bytes 786440 | tf_op jit(solution)/shard_map/ppermute | solution.py:37
  123.0 22.5 %collective-permute-start.38 = (bf16[256,512]{1,0:T(8,128)(2,1)S(1)}, bf16[256,512]{1,0:T(8,128)(2,1)S(1)}, u32[]{:S(2)}, u32[]{:S(2)}) collective-permute-start(bf16[256,512]{1,0:T(8,128)(2,1)S(1)} %collective-permute-done.37.rest_2_), channel_id=1, source_target_pairs={{0,1},{1,0},{2,3},{3,2},{4,5},{5,4},{6,7},{7,6},{8,9},{9,8},{10,11... | collective-permute-start | bytes 786440 | tf_op jit(solution)/shard_map/ppermute | solution.py:37
  125.1 4.6 %collective-permute-start.22 = (bf16[272,128]{1,0:T(8,128)(2,1)S(1)}, bf16[272,128]{1,0:T(8,128)(2,1)S(1)}, u32[]{:S(2)}, u32[]{:S(2)}) collective-permute-start(bf16[272,128]{1,0:T(8,128)(2,1)S(1)} %get-tuple-element.24), channel_id=1, source_target_pairs={{0,96},{8,104},{16,112},{24,120},{32,0},{40,8},{48,16},{56,24},{64... | collective-permute-start | bytes 208904 | tf_op jit(solution)/shard_map/ppermute | solution.py:21
  125.2 21.1 %collective-permute-start.40 = (bf16[256,512]{1,0:T(8,128)(2,1)S(1)}, bf16[256,512]{1,0:T(8,128)(2,1)S(1)}, u32[]{:S(2)}, u32[]{:S(2)}) collective-permute-start(bf16[256,512]{1,0:T(8,128)(2,1)S(1)} %collective-permute-done.39.rest_4_), channel_id=1, source_target_pairs={{0,1},{1,0},{2,3},{3,2},{4,5},{5,4},{6,7},{7,6},{8,9},{9,8},{10,11... | collective-permute-start | bytes 786440 | tf_op jit(solution)/shard_map/ppermute | solution.py:37
  125.8 20.5 %collective-permute-start.42 = (bf16[256,512]{1,0:T(8,128)(2,1)S(1)}, bf16[256,512]{1,0:T(8,128)(2,1)S(1)}, u32[]{:S(2)}, u32[]{:S(2)}) collective-permute-start(bf16[256,512]{1,0:T(8,128)(2,1)S(1)} %collective-permute-done.41.rest_6_), channel_id=1, source_target_pairs={{0,1},{1,0},{2,3},{3,2},{4,5},{5,4},{6,7},{7,6},{8,9},{9,8},{10,11... | collective-permute-start | bytes 786440 | tf_op jit(solution)/shard_map/ppermute | solution.py:37
  129.8 5.8 %collective-permute-start.23 = (bf16[272,128]{1,0:T(8,128)(2,1)S(1)}, bf16[272,128]{1,0:T(8,128)(2,1)S(1)}, u32[]{:S(2)}, u32[]{:S(2)}) collective-permute-start(bf16[272,128]{1,0:T(8,128)(2,1)S(1)} %get-tuple-element.25), channel_id=1, source_target_pairs={{0,64},{8,72},{16,80},{24,88},{32,96},{40,104},{48,112},{56,120},{... | collective-permute-start | bytes 208904 | tf_op jit(solution)/shard_map/ppermute | solution.py:21
  135.6 5.5 %collective-permute-start.24 = (bf16[272,128]{1,0:T(8,128)(2,1)S(1)}, bf16[272,128]{1,0:T(8,128)(2,1)S(1)}, u32[]{:S(2)}, u32[]{:S(2)}) collective-permute-start(bf16[272,128]{1,0:T(8,128)(2,1)S(1)} %get-tuple-element.26), channel_id=1, source_target_pairs={{0,32},{8,40},{16,48},{24,56},{32,64},{40,72},{48,80},{56,88},{64,... | collective-permute-start | bytes 208904 | tf_op jit(solution)/shard_map/ppermute | solution.py:21
  137.6 0.8 copy-start.10
  138.4 0.8 copy-start.11
  141.5 5.5 %collective-permute-start.32 = (bf16[128,256]{1,0:T(8,128)(2,1)S(1)}, bf16[128,256]{1,0:T(8,128)(2,1)S(1)}, u32[]{:S(2)}, u32[]{:S(2)}) collective-permute-start(bf16[128,256]{1,0:T(8,128)(2,1)S(1)} %shard_map.132.a0), channel_id=1, source_target_pairs={{0,32},{8,40},{16,48},{24,56},{32,64},{40,72},{48,80},{56,88},{64,... | collective-permute-start | bytes 196616 | tf_op jit(solution)/shard_map/ppermute | solution.py:21
  141.6 6.8 %collective-permute-start.33 = (bf16[128,256]{1,0:T(8,128)(2,1)S(1)}, bf16[128,256]{1,0:T(8,128)(2,1)S(1)}, u32[]{:S(2)}, u32[]{:S(2)}) collective-permute-start(bf16[128,256]{1,0:T(8,128)(2,1)S(1)} %shard_map.132.a0), channel_id=1, source_target_pairs={{0,64},{8,72},{16,80},{24,88},{32,96},{40,104},{48,112},{56,120},{... | collective-permute-start | bytes 196616 | tf_op jit(solution)/shard_map/ppermute | solution.py:21
  145.4 4.3 %collective-permute-start.34 = (bf16[128,256]{1,0:T(8,128)(2,1)S(1)}, bf16[128,256]{1,0:T(8,128)(2,1)S(1)}, u32[]{:S(2)}, u32[]{:S(2)}) collective-permute-start(bf16[128,256]{1,0:T(8,128)(2,1)S(1)} %shard_map.132.a0), channel_id=1, source_target_pairs={{0,96},{8,104},{16,112},{24,120},{32,0},{40,8},{48,16},{56,24},{64... | collective-permute-start | bytes 196616 | tf_op jit(solution)/shard_map/ppermute | solution.py:21
  150.7 5.6 %collective-permute-start.43 = (bf16[128,256]{1,0:T(8,128)(2,1)S(1)}, bf16[128,256]{1,0:T(8,128)(2,1)S(1)}, u32[]{:S(2)}, u32[]{:S(2)}) collective-permute-start(bf16[128,256]{1,0:T(8,128)(2,1)S(1)} %get-tuple-element.34), channel_id=1, source_target_pairs={{0,8},{8,16},{16,24},{24,0},{32,40},{40,48},{48,56},{56,32},{64,72... | collective-permute-start | bytes 196616 | tf_op jit(solution)/shard_map/ppermute | solution.py:28
  150.8 5.7 %collective-permute-start.44 = (bf16[128,256]{1,0:T(8,128)(2,1)S(1)}, bf16[128,256]{1,0:T(8,128)(2,1)S(1)}, u32[]{:S(2)}, u32[]{:S(2)}) collective-permute-start(bf16[128,256]{1,0:T(8,128)(2,1)S(1)} %get-tuple-element.35), channel_id=1, source_target_pairs={{0,24},{8,0},{16,8},{24,16},{32,56},{40,32},{48,40},{56,48},{64,88... | collective-permute-start | bytes 196616 | tf_op jit(solution)/shard_map/ppermute | solution.py:28
  154.0 5.8 %collective-permute-start.45 = (bf16[128,256]{1,0:T(8,128)(2,1)S(1)}, bf16[128,256]{1,0:T(8,128)(2,1)S(1)}, u32[]{:S(2)}, u32[]{:S(2)}) collective-permute-start(bf16[128,256]{1,0:T(8,128)(2,1)S(1)} %get-tuple-element.36), channel_id=1, source_target_pairs={{0,16},{8,24},{16,0},{24,8},{32,48},{40,56},{48,32},{56,40},{64,80... | collective-permute-start | bytes 196616 | tf_op jit(solution)/shard_map/ppermute | solution.py:28
where the time goes:
time: 161 us; the launch traced here: 160 us
  starting transfers between devices  85 us (53%)
  waiting for transfers between devices  46.6 us (29%)
  Pallas kernels  14.5 us (9%)
  local copies, waits for them, and re-layouts  11.2 us (7%)
  other arithmetic  2.27 us (1%)
    ppermute x9, starting transfers between devices, x_shift(): return lax.ppermute(x, 'wt', pairs)  43 us
    ppermute x12, waiting for transfers between devices, z_shift(): return lax.ppermute(x, 'ctx', pairs)  24.4 us
    ppermute x12, starting transfers between devices, z_shift(): return lax.ppermute(x, 'ctx', pairs)  20.4 us
    ppermute x12, starting transfers between devices, y_shift(): return lax.ppermute(x, 'ctx', pairs)  19.2 us
    ppermute x12, waiting for transfers between devices, y_shift(): return lax.ppermute(x, 'ctx', pairs)  18.7 us
    pallas_call x14, Pallas kernels, kernel_call(): pl.pallas_call(body, in_specs=[s for s, _ in ins], out_specs=VMEM if sing...  14.5 us
    unnamed x34, local copies, waits for them, and re-layouts  11.1 us
    ppermute x9, waiting for transfers between devices, x_shift(): return lax.ppermute(x, 'wt', pairs)  3.46 us
  transfers between devices with their start and end apart: 46, of which 18 were waited for; matrix products, arithmetic and copies ran while one was open for 1% of the time, Pallas kernels for 7%

commit v1 on v0

--- a/solution.py
+++ b/solution.py
@@ -55,7 +55,9 @@
 
 
 def from_ring(x, shift):
-    got = {k: shift(x, k) for k in ORDER}
+    got = {}
+    for k in ORDER:
+        got[k] = shift(x, k)
     return [x, got[1], got[2], got[3]]
 
 
@@ -67,10 +69,21 @@
 VMEM = pl.BlockSpec(memory_space=pltpu.VMEM)
 SMEM = pl.BlockSpec(memory_space=pltpu.SMEM)
 ANY = pl.BlockSpec(memory_space=pl.ANY)
+WHOLE = pl.BlockSpec()
 
 
 def held(x):
     return pltpu.with_memory_space_constraint(x, pltpu.VMEM)
+
+
+def outside(x):
+    return pltpu.with_memory_space_constraint(x, pltpu.HBM)
+
+
+def placed(spec, x):
+    if spec is SMEM:
+        return x
+    return held(x) if spec is VMEM else outside(x)
 
 
 def kernel_call(body, ins, out_shape, scratch=(), limit=12):
@@ -82,7 +95,7 @@
         out_shape=out_shape,
         scratch_shapes=list(scratch),
         compiler_params=pltpu.CompilerParams(vmem_limit_bytes=limit << 20),
-    )(*[held(a) if s is VMEM else a for s, a in ins])
+    )(*[placed(s, a) for s, a in ins])
 
 
 def near(dims, kind):
@@ -359,14 +372,14 @@
         [wt_rank // 2, wt_rank % 2, ctx_rank // SIDE, ctx_rank % SIDE]
     ).astype(jnp.int32)
 
-    positions = (lengths[:, None] + jnp.arange(new, dtype=jnp.int32)[None, :]).reshape(rows)
+    token = lax.broadcasted_iota(jnp.int32, (rows, HEAD), 0)
+    lane = lax.broadcasted_iota(jnp.int32, (rows, HEAD), 1)
     half = HEAD // 2
-    freq = 10000.0 ** (-2.0 * jnp.arange(half, dtype=f32) / HEAD)
-    angle = positions.astype(f32)[:, None] * freq[None, :]
+    positions = jnp.where(token < new, lengths[0], lengths[1] - new) + token
+    freq = 10000.0 ** (-2.0 * (jnp.arange(HEAD, dtype=jnp.int32) % half).astype(f32) / HEAD)
+    angle = positions.astype(f32) * freq[None, :]
     cosine = jnp.cos(angle)
-    sine = jnp.sin(angle)
-    cosine = jnp.concatenate([cosine, cosine], axis=-1)
-    sine = jnp.concatenate([-sine, sine], axis=-1)
+    sine = jnp.where(lane < half, -jnp.sin(angle), jnp.sin(angle))
 
     by_kind = jnp.transpose(qkv_weight, (1, 0, 2))
     feats = by_kind.shape[1]
@@ -374,9 +387,9 @@
         adapter_body,
         [
             (SMEM, span_source),
-            (VMEM, frames),
-            (VMEM, adapter_weight),
-            (VMEM, adapter_bias.reshape(1, cols)),
+            (WHOLE, frames),
+            (WHOLE, adapter_weight),
+            (WHOLE, adapter_bias.reshape(1, cols)),
             (ANY, by_kind),
         ],
         (near((rows, cols), bf16), near((feats, cols), bf16), near((2, feats, cols), bf16)),
@@ -406,7 +419,7 @@
         key_value_body,
         [(SMEM, place), (VMEM, normed), (VMEM, cosine), (VMEM, sine)]
         + [(VMEM, w) for w in other_weights],
-        (far((rows, cols), bf16), far((rows, cols), bf16)),
+        (near((rows, cols), bf16), near((rows, cols), bf16)),
     )
 
     def history(step):

time: 161 us -> 155 us (0.963)
  local copies, waits for them, and re-layouts: 11.2 us -> 4.84 us
  waiting for transfers between devices: 46.6 us -> 50 us
  starting transfers between devices: 85 us -> 82.1 us
    unnamed x34 -> x16, local copies, waits for them, and re-layouts: 11.1 us -> 3.53 us
    ppermute x12, waiting for transfers between devices: 24.4 us -> 27.2 us  [z_shift(): return lax.ppermute(x, 'ctx', pairs)]
    ppermute x12, waiting for transfers between devices: 18.7 us -> 21.1 us  [y_shift(): return lax.ppermute(x, 'ctx', pairs)]
    ppermute x9, waiting for transfers between devices: 3.46 us -> 1.61 us  [x_shift(): return lax.ppermute(x, 'wt', pairs)]
  transfers between devices with their start and end apart: 46 -> 46, of which waited for: 18 -> 17; matrix products, arithmetic and copies ran while one was open for 1% -> 2% of each run, Pallas kernels for 7% -> 7%
where the time goes in v1:
time: 155 us
  starting transfers between devices  82.1 us (53%)
  waiting for transfers between devices  50 us (32%)
  Pallas kernels  15.2 us (10%)
  local copies, waits for them, and re-layouts  4.84 us (3%)
  between operations  1.6 us (1%)
    ppermute x9, starting transfers between devices, x_shift(): return lax.ppermute(x, 'wt', pairs)  42.5 us
    ppermute x12, waiting for transfers between devices, z_shift(): return lax.ppermute(x, 'ctx', pairs)  27.2 us
    ppermute x12, waiting for transfers between devices, y_shift(): return lax.ppermute(x, 'ctx', pairs)  21.1 us
    ppermute x12, starting transfers between devices, z_shift(): return lax.ppermute(x, 'ctx', pairs)  19.1 us
    ppermute x12, starting transfers between devices, y_shift(): return lax.ppermute(x, 'ctx', pairs)  18 us
    pallas_call x14, Pallas kernels, kernel_call(): pl.pallas_call(body, in_specs=[s for s, _ in ins], out_specs=VMEM if sing...  15.2 us
    unnamed x16, local copies, waits for them, and re-layouts  3.53 us
  transfers between devices with their start and end apart: 46, of which 17 were waited for; matrix products, arithmetic and copies ran while one was open for 2% of the time, Pallas kernels for 7%

profile of v1, /device:TPU:0, one launch (start us, length us, event | category | flops | bytes accessed | tf_op | source)
XLA Modules:
  0.0 154.8 jit_solution(16445281866975601462)
XLA Ops:
  0.7 0.7 copy-done.5
  1.3 2.4 %shard_map.121 = (bf16[128,256]{1,0:T(8,128)(2,1)S(1)}, bf16[512,256]{1,0:T(8,128)(2,1)S(1)}, bf16[2,512,256]{2,1,0:T(8,128)(2,1)S(1)}) custom-call(s32[8]{0:T(128)S(1)} %copy-done.5, bf16[128,1280]{1,0:T(8,128)(2,1)} %frames.1, bf16[1280,256]{1,0:T(8,128)(2,1)} %weight.1, f32[1,256]{1,0:T(1,128)} %bitcast.11, bf16[3,512,256]{2,1,0:T(8,128)(2,1)} %bitcast.10), custom_call_target="tpu_custom_call" | custom-call | tf_op jit(solution)/shard_map/pallas_call | solution.py:91
  3.7 1.8 %collective-permute-start = (bf16[128,256]{1,0:T(8,128)(2,1)S(1)}, bf16[128,256]{1,0:T(8,128)(2,1)S(1)}, u32[]{:S(2)}, u32[]{:S(2)}) collective-permute-start(bf16[128,256]{1,0:T(8,128)(2,1)S(1)} %get-tuple-element.20.a0), channel_id=1, source_target_pairs={{0,32},{8,40},{16,48},{24,56},{32,64},{40,72},{48,80},{56,88},{64,... | collective-permute-start | bytes 196616 | tf_op jit(solution)/shard_map/ppermute | solution.py:21
  5.4 2.9 %collective-permute-start.1 = (bf16[128,256]{1,0:T(8,128)(2,1)S(1)}, bf16[128,256]{1,0:T(8,128)(2,1)S(1)}, u32[]{:S(2)}, u32[]{:S(2)}) collective-permute-start(bf16[128,256]{1,0:T(8,128)(2,1)S(1)} %get-tuple-element.20.a0), channel_id=1, source_target_pairs={{0,64},{8,72},{16,80},{24,88},{32,96},{40,104},{48,112},{56,120},{... | collective-permute-start | bytes 196616 | tf_op jit(solution)/shard_map/ppermute | solution.py:21
  8.3 1.3 collective-permute-start.2
  9.7 3.0 %collective-permute-start.9 = (bf16[512,256]{1,0:T(8,128)(2,1)S(1)}, bf16[512,256]{1,0:T(8,128)(2,1)S(1)}, u32[]{:S(2)}, u32[]{:S(2)}) collective-permute-start(bf16[512,256]{1,0:T(8,128)(2,1)S(1)} %get-tuple-element.21.rest_0_), channel_id=1, source_target_pairs={{0,4},{1,5},{2,6},{3,7},{4,0},{5,1},{6,2},{7,3},{8,12},{9,13},{10,... | collective-permute-start | bytes 786440 | tf_op jit(solution)/shard_map/ppermute | solution.py:33
  12.7 1.1 collective-permute-start.11
  13.8 1.3 fusion.3
  15.2 0.9 collective-permute-start.7
  16.1 2.0 %collective-permute-start.3 = (bf16[4,128,256]{2,1,0:T(8,128)(2,1)S(1)}, bf16[4,128,256]{2,1,0:T(8,128)(2,1)}, u32[]{:S(2)}, u32[]{:S(2)}) collective-permute-start(bf16[4,128,256]{2,1,0:T(8,128)(2,1)S(1)} %shard_map.122.s0), channel_id=1, source_target_pairs={{0,8},{8,16},{16,24},{24,0},{32,40},{40,48},{48,56},{56,32},{64,72... | collective-permute-start | bytes 786440 | tf_op jit(solution)/shard_map/ppermute | solution.py:28
  18.8 1.6 %collective-permute-done.9.rest_4_ = bf16[512,256]{1,0:T(8,128)(2,1)S(1)} collective-permute-done((bf16[512,256]{1,0:T(8,128)(2,1)S(1)}, bf16[512,256]{1,0:T(8,128)(2,1)S(1)}, u32[]{:S(2)}, u32[]{:S(2)}) %collective-permute-start.9) | collective-permute-done | bytes 262176 | tf_op jit(solution)/shard_map/ppermute | solution.py:33
  20.4 3.9 %collective-permute-start.4 = (bf16[4,128,256]{2,1,0:T(8,128)(2,1)S(1)}, bf16[4,128,256]{2,1,0:T(8,128)(2,1)}, u32[]{:S(2)}, u32[]{:S(2)}) collective-permute-start(bf16[4,128,256]{2,1,0:T(8,128)(2,1)S(1)} %shard_map.122.s0), channel_id=1, source_target_pairs={{0,16},{8,24},{16,0},{24,8},{32,48},{40,56},{48,32},{56,40},{64,80... | collective-permute-start | bytes 786440 | tf_op jit(solution)/shard_map/ppermute | solution.py:28
  24.2 0.6 add_convert_fusion
  25.0 3.3 %collective-permute-start.5 = (bf16[4,128,256]{2,1,0:T(8,128)(2,1)S(1)}, bf16[4,128,256]{2,1,0:T(8,128)(2,1)S(1)}, u32[]{:S(2)}, u32[]{:S(2)}) collective-permute-start(bf16[4,128,256]{2,1,0:T(8,128)(2,1)S(1)} %shard_map.122.s0), channel_id=1, source_target_pairs={{0,24},{8,0},{16,8},{24,16},{32,56},{40,32},{48,40},{56,48},{64,88... | collective-permute-start | bytes 786440 | tf_op jit(solution)/shard_map/ppermute | solution.py:28
  28.3 0.5 collective-permute-start.12
  28.9 0.3 negate_select_fusion
  29.2 4.9 %collective-permute-done.4.s2 = bf16[4,128,256]{2,1,0:T(8,128)(2,1)} collective-permute-done((bf16[4,128,256]{2,1,0:T(8,128)(2,1)S(1)}, bf16[4,128,256]{2,1,0:T(8,128)(2,1)}, u32[]{:S(2)}, u32[]{:S(2)}) %collective-permute-start.4) | collective-permute-done | bytes 262176 | tf_op jit(solution)/shard_map/ppermute | solution.py:28
  34.1 0.6 collective-permute-start.26
  35.0 2.3 %shard_map.123 = (bf16[128,256]{1,0:T(8,128)(2,1)S(1)}, bf16[16,128,256]{2,1,0:T(8,128)(2,1)S(1)}) custom-call(s32[4]{0:T(128)S(1)} %pad_add_fusion.place.refs_0_, bf16[4,128,256]{2,1,0:T(8,128)(2,1)S(1)} %shard_map.122.s0, bf16[4,128,256]{2,1,0:T(8,128)(2,1)} %collective-permute-done.3.s1, bf16[4,128,256]{2,1,0:T(8,128)(2,1)} %collective-permute-done.4.s2, ...), custom_call_target="tpu_custom_call" | custom-call | tf_op jit(solution)/shard_map/pallas_call | solution.py:91
  37.2 0.7 collective-permute-start.13
  38.0 3.1 %collective-permute-start.28 = (bf16[2,512,256]{2,1,0:T(8,128)(2,1)S(1)}, bf16[2,512,256]{2,1,0:T(8,128)(2,1)S(1)}, u32[]{:S(2)}, u32[]{:S(2)}) collective-permute-start(bf16[2,512,256]{2,1,0:T(8,128)(2,1)S(1)} %get-tuple-element.28.rest_0_), channel_id=1, source_target_pairs={{0,4},{1,5},{2,6},{3,7},{4,0},{5,1},{6,2},{7,3},{8,12},{9,13},{10,... | collective-permute-start | bytes 1572872 | tf_op jit(solution)/shard_map/ppermute | solution.py:33
  41.0 1.6 %collective-permute-start.30 = (bf16[2,512,256]{2,1,0:T(8,128)(2,1)S(1)}, bf16[2,512,256]{2,1,0:T(8,128)(2,1)S(1)}, u32[]{:S(2)}, u32[]{:S(2)}) collective-permute-start(bf16[2,512,256]{2,1,0:T(8,128)(2,1)S(1)} %get-tuple-element.28.rest_0_), channel_id=1, source_target_pairs={{0,6},{1,7},{2,0},{3,1},{4,2},{5,3},{6,4},{7,5},{8,14},{9,15},{10,... | collective-permute-start | bytes 1572872 | tf_op jit(solution)/shard_map/ppermute | solution.py:33
  42.6 0.7 collective-permute-start.35
  43.3 5.8 %collective-permute-start.14 = (bf16[128,256]{1,0:T(8,128)(2,1)S(1)}, bf16[128,256]{1,0:T(8,128)(2,1)S(1)}, u32[]{:S(2)}, u32[]{:S(2)}) collective-permute-start(bf16[128,256]{1,0:T(8,128)(2,1)S(1)} %get-tuple-element.22.a0.query), channel_id=1, source_target_pairs={{0,64},{8,72},{16,80},{24,88},{32,96},{40,104},{48,112},{56,120},{... | collective-permute-start | bytes 196616 | tf_op jit(solution)/shard_map/ppermute | solution.py:21
  49.1 2.2 %collective-permute-done.14.a2 = bf16[128,256]{1,0:T(8,128)(2,1)S(1)} collective-permute-done((bf16[128,256]{1,0:T(8,128)(2,1)S(1)}, bf16[128,256]{1,0:T(8,128)(2,1)S(1)}, u32[]{:S(2)}, u32[]{:S(2)}) %collective-permute-start.14) | collective-permute-done | bytes 65568 | tf_op jit(solution)/shard_map/ppermute | solution.py:21
  51.4 2.0 %collective-permute-start.15 = (bf16[128,256]{1,0:T(8,128)(2,1)S(1)}, bf16[128,256]{1,0:T(8,128)(2,1)S(1)}, u32[]{:S(2)}, u32[]{:S(2)}) collective-permute-start(bf16[128,256]{1,0:T(8,128)(2,1)S(1)} %get-tuple-element.22.a0.query), channel_id=1, source_target_pairs={{0,96},{8,104},{16,112},{24,120},{32,0},{40,8},{48,16},{56,24},{64... | collective-permute-start | bytes 196616 | tf_op jit(solution)/shard_map/ppermute | solution.py:21
  53.4 2.3 %collective-permute-done.15.a3 = bf16[128,256]{1,0:T(8,128)(2,1)S(1)} collective-permute-done((bf16[128,256]{1,0:T(8,128)(2,1)S(1)}, bf16[128,256]{1,0:T(8,128)(2,1)S(1)}, u32[]{:S(2)}, u32[]{:S(2)}) %collective-permute-start.15) | collective-permute-done | bytes 65568 | tf_op jit(solution)/shard_map/ppermute | solution.py:21
  55.7 0.6 collective-permute-start.16
  56.2 15.2 %collective-permute-start.37 = (bf16[256,512]{1,0:T(8,128)(2,1)S(1)}, bf16[256,512]{1,0:T(8,128)(2,1)S(1)}, u32[]{:S(2)}, u32[]{:S(2)}) collective-permute-start(bf16[256,512]{1,0:T(8,128)(2,1)S(1)} %collective-permute-done.35.rest_0_), channel_id=1, source_target_pairs={{0,2},{1,3},{2,4},{3,5},{4,6},{5,7},{6,0},{7,1},{8,10},{9,11},{10,... | collective-permute-start | bytes 786440 | tf_op jit(solution)/shard_map/ppermute | solution.py:33
  71.4 11.3 %collective-permute-start.39 = (bf16[256,512]{1,0:T(8,128)(2,1)S(1)}, bf16[256,512]{1,0:T(8,128)(2,1)S(1)}, u32[]{:S(2)}, u32[]{:S(2)}) collective-permute-start(bf16[256,512]{1,0:T(8,128)(2,1)S(1)} %collective-permute-done.35.rest_0_), channel_id=1, source_target_pairs={{0,4},{1,5},{2,6},{3,7},{4,0},{5,1},{6,2},{7,3},{8,12},{9,13},{10,... | collective-permute-start | bytes 786440 | tf_op jit(solution)/shard_map/ppermute | solution.py:33
  82.8 4.3 %collective-permute-start.18 = (bf16[4,128,256]{2,1,0:T(8,128)(2,1)S(1)}, bf16[4,128,256]{2,1,0:T(8,128)(2,1)S(1)}, u32[]{:S(2)}, u32[]{:S(2)}) collective-permute-start(bf16[4,128,256]{2,1,0:T(8,128)(2,1)S(1)} %shard_map.124.refs_2_), channel_id=1, source_target_pairs={{0,16},{8,24},{16,0},{24,8},{32,48},{40,56},{48,32},{56,40},{64,80... | collective-permute-start | bytes 786440 | tf_op jit(solution)/shard_map/ppermute | solution.py:28
  87.1 1.6 %copy-done.1 = bf16[2,128,4096]{2,1,0:T(8,128)(2,1)S(1)} copy-done((bf16[2,128,4096]{2,1,0:T(8,128)(2,1)S(1)}, bf16[2,128,4096]{2,1,0:T(8,128)(2,1)}, u32[]{:S(2)}) %copy-start.1) | copy-done | bytes 2097176
  88.6 1.3 shard_map.126
  90.0 0.7 collective-permute-start.17
  90.7 5.7 %collective-permute-start.41 = (bf16[256,512]{1,0:T(8,128)(2,1)S(1)}, bf16[256,512]{1,0:T(8,128)(2,1)S(1)}, u32[]{:S(2)}, u32[]{:S(2)}) collective-permute-start(bf16[256,512]{1,0:T(8,128)(2,1)S(1)} %collective-permute-done.35.rest_0_), channel_id=1, source_target_pairs={{0,6},{1,7},{2,0},{3,1},{4,2},{5,3},{6,4},{7,5},{8,14},{9,15},{10,... | collective-permute-start | bytes 786440 | tf_op jit(solution)/shard_map/ppermute | solution.py:33
  96.4 0.5 collective-permute-start.29
  96.9 2.4 %collective-permute-done.20.refs_2_ = bf16[4,128,256]{2,1,0:T(8,128)(2,1)S(1)} collective-permute-done((bf16[4,128,256]{2,1,0:T(8,128)(2,1)S(1)}, bf16[4,128,256]{2,1,0:T(8,128)(2,1)S(1)}, u32[]{:S(2)}, u32[]{:S(2)}) %collective-permute-start.20) | collective-permute-done | bytes 262176 | tf_op jit(solution)/shard_map/ppermute | solution.py:28
  99.2 1.3 shard_map.127
  100.6 1.3 shard_map.128
  101.9 0.7 collective-permute-start.19
  102.6 1.0 collective-permute-done.17.p1
  103.6 0.4 collective-permute-start.21
  104.0 8.9 %collective-permute-done.19.p2 = bf16[1072,128]{1,0:T(8,128)(2,1)S(1)} collective-permute-done((bf16[1072,128]{1,0:T(8,128)(2,1)S(1)}, bf16[1072,128]{1,0:T(8,128)(2,1)S(1)}, u32[]{:S(2)}, u32[]{:S(2)}) %collective-permute-start.19) | collective-permute-done | bytes 274464 | tf_op jit(solution)/shard_map/ppermute | solution.py:28
  113.0 5.4 %collective-permute-done.21.p3 = bf16[1072,128]{1,0:T(8,128)(2,1)S(1)} collective-permute-done((bf16[1072,128]{1,0:T(8,128)(2,1)S(1)}, bf16[1072,128]{1,0:T(8,128)(2,1)S(1)}, u32[]{:S(2)}, u32[]{:S(2)}) %collective-permute-start.21) | collective-permute-done | bytes 274464 | tf_op jit(solution)/shard_map/ppermute | solution.py:28
  118.4 1.3 shard_map.125.p0
  119.7 0.8 shard_map.129
  120.6 0.6 collective-permute-start.40
  121.3 3.9 %collective-permute-done.22.p1 = bf16[272,128]{1,0:T(8,128)(2,1)S(1)} collective-permute-done((bf16[272,128]{1,0:T(8,128)(2,1)S(1)}, bf16[272,128]{1,0:T(8,128)(2,1)S(1)}, u32[]{:S(2)}, u32[]{:S(2)}) %collective-permute-start.22) | collective-permute-done | bytes 69664 | tf_op jit(solution)/shard_map/ppermute | solution.py:21
  125.1 5.8 %collective-permute-done.23.p2 = bf16[272,128]{1,0:T(8,128)(2,1)S(1)} collective-permute-done((bf16[272,128]{1,0:T(8,128)(2,1)S(1)}, bf16[272,128]{1,0:T(8,128)(2,1)S(1)}, u32[]{:S(2)}, u32[]{:S(2)}) %collective-permute-start.23) | collective-permute-done | bytes 69664 | tf_op jit(solution)/shard_map/ppermute | solution.py:21
  131.0 1.3 shard_map.130
  132.3 1.0 shard_map.131
  133.3 3.2 %collective-permute-done.24.p3 = bf16[272,128]{1,0:T(8,128)(2,1)S(1)} collective-permute-done((bf16[272,128]{1,0:T(8,128)(2,1)S(1)}, bf16[272,128]{1,0:T(8,128)(2,1)S(1)}, u32[]{:S(2)}, u32[]{:S(2)}) %collective-permute-start.24) | collective-permute-done | bytes 69664 | tf_op jit(solution)/shard_map/ppermute | solution.py:21
  136.5 0.4 shard_map.132.a0
  137.0 1.7 %collective-permute-start.33 = (bf16[128,256]{1,0:T(8,128)(2,1)S(1)}, bf16[128,256]{1,0:T(8,128)(2,1)S(1)}, u32[]{:S(2)}, u32[]{:S(2)}) collective-permute-start(bf16[128,256]{1,0:T(8,128)(2,1)S(1)} %shard_map.132.a0), channel_id=1, source_target_pairs={{0,64},{8,72},{16,80},{24,88},{32,96},{40,104},{48,112},{56,120},{... | collective-permute-start | bytes 196616 | tf_op jit(solution)/shard_map/ppermute | solution.py:21
  138.7 1.6 %collective-permute-start.34 = (bf16[128,256]{1,0:T(8,128)(2,1)S(1)}, bf16[128,256]{1,0:T(8,128)(2,1)S(1)}, u32[]{:S(2)}, u32[]{:S(2)}) collective-permute-start(bf16[128,256]{1,0:T(8,128)(2,1)S(1)} %shard_map.132.a0), channel_id=1, source_target_pairs={{0,96},{8,104},{16,112},{24,120},{32,0},{40,8},{48,16},{56,24},{64... | collective-permute-start | bytes 196616 | tf_op jit(solution)/shard_map/ppermute | solution.py:21
  140.3 2.9 %collective-permute-done.32.a1 = bf16[128,256]{1,0:T(8,128)(2,1)S(1)} collective-permute-done((bf16[128,256]{1,0:T(8,128)(2,1)S(1)}, bf16[128,256]{1,0:T(8,128)(2,1)S(1)}, u32[]{:S(2)}, u32[]{:S(2)}) %collective-permute-start.32) | collective-permute-done | bytes 65568 | tf_op jit(solution)/shard_map/ppermute | solution.py:21
  143.1 0.9 collective-permute-done.34.a3
  144.0 1.0 shard_map.133
  145.1 3.2 %collective-permute-start.44 = (bf16[128,256]{1,0:T(8,128)(2,1)S(1)}, bf16[128,256]{1,0:T(8,128)(2,1)S(1)}, u32[]{:S(2)}, u32[]{:S(2)}) collective-permute-start(bf16[128,256]{1,0:T(8,128)(2,1)S(1)} %get-tuple-element.35), channel_id=1, source_target_pairs={{0,24},{8,0},{16,8},{24,16},{32,56},{40,32},{48,40},{56,48},{64,88... | collective-permute-start | bytes 196616 | tf_op jit(solution)/shard_map/ppermute | solution.py:28
  148.3 0.6 copy.13
  149.0 0.6 copy.14
  149.6 1.0 collective-permute-done.43.g1
  150.8 3.3 %collective-permute-done.45.g3 = bf16[128,256]{1,0:T(8,128)(2,1)S(1)} collective-permute-done((bf16[128,256]{1,0:T(8,128)(2,1)S(1)}, bf16[128,256]{1,0:T(8,128)(2,1)S(1)}, u32[]{:S(2)}, u32[]{:S(2)}) %collective-permute-start.45) | collective-permute-done | bytes 65568 | tf_op jit(solution)/shard_map/ppermute | solution.py:28
  154.1 0.7 shard_map.134
  (64 shorter events, 1.1 us)
Async XLA Ops:
  0.6 34.3 %copy-start.4 = (f32[4096]{0:T(1024)S(1)}, f32[4096]{0:T(1024)}, u32[]{:S(2)}) copy-start(f32[4096]{0:T(1024)} %param.14) | copy-start | bytes 49156
  0.6 0.7 copy-start.5
  3.7 11.5 %collective-permute-start = (bf16[128,256]{1,0:T(8,128)(2,1)S(1)}, bf16[128,256]{1,0:T(8,128)(2,1)S(1)}, u32[]{:S(2)}, u32[]{:S(2)}) collective-permute-start(bf16[128,256]{1,0:T(8,128)(2,1)S(1)} %get-tuple-element.20.a0), channel_id=1, source_target_pairs={{0,32},{8,40},{16,48},{24,56},{32,64},{40,72},{48,80},{56,88},{64,... | collective-permute-start | bytes 196616 | tf_op jit(solution)/shard_map/ppermute | solution.py:21
  5.4 10.6 %collective-permute-start.1 = (bf16[128,256]{1,0:T(8,128)(2,1)S(1)}, bf16[128,256]{1,0:T(8,128)(2,1)S(1)}, u32[]{:S(2)}, u32[]{:S(2)}) collective-permute-start(bf16[128,256]{1,0:T(8,128)(2,1)S(1)} %get-tuple-element.20.a0), channel_id=1, source_target_pairs={{0,64},{8,72},{16,80},{24,88},{32,96},{40,104},{48,112},{56,120},{... | collective-permute-start | bytes 196616 | tf_op jit(solution)/shard_map/ppermute | solution.py:21
  8.3 7.7 %collective-permute-start.2 = (bf16[128,256]{1,0:T(8,128)(2,1)S(1)}, bf16[128,256]{1,0:T(8,128)(2,1)S(1)}, u32[]{:S(2)}, u32[]{:S(2)}) collective-permute-start(bf16[128,256]{1,0:T(8,128)(2,1)S(1)} %get-tuple-element.20.a0), channel_id=1, source_target_pairs={{0,96},{8,104},{16,112},{24,120},{32,0},{40,8},{48,16},{56,24},{64... | collective-permute-start | bytes 196616 | tf_op jit(solution)/shard_map/ppermute | solution.py:21
  9.7 10.7 %collective-permute-start.9 = (bf16[512,256]{1,0:T(8,128)(2,1)S(1)}, bf16[512,256]{1,0:T(8,128)(2,1)S(1)}, u32[]{:S(2)}, u32[]{:S(2)}) collective-permute-start(bf16[512,256]{1,0:T(8,128)(2,1)S(1)} %get-tuple-element.21.rest_0_), channel_id=1, source_target_pairs={{0,4},{1,5},{2,6},{3,7},{4,0},{5,1},{6,2},{7,3},{8,12},{9,13},{10,... | collective-permute-start | bytes 786440 | tf_op jit(solution)/shard_map/ppermute | solution.py:33
  12.7 12.2 %collective-permute-start.11 = (bf16[512,256]{1,0:T(8,128)(2,1)S(1)}, bf16[512,256]{1,0:T(8,128)(2,1)}, u32[]{:S(2)}, u32[]{:S(2)}) collective-permute-start(bf16[512,256]{1,0:T(8,128)(2,1)S(1)} %get-tuple-element.21.rest_0_), channel_id=1, source_target_pairs={{0,6},{1,7},{2,0},{3,1},{4,2},{5,3},{6,4},{7,5},{8,14},{9,15},{10,... | collective-permute-start | bytes 786440 | tf_op jit(solution)/shard_map/ppermute | solution.py:33
  15.2 13.1 %collective-permute-start.7 = (bf16[512,256]{1,0:T(8,128)(2,1)S(1)}, bf16[512,256]{1,0:T(8,128)(2,1)}, u32[]{:S(2)}, u32[]{:S(2)}) collective-permute-start(bf16[512,256]{1,0:T(8,128)(2,1)S(1)} %get-tuple-element.21.rest_0_), channel_id=1, source_target_pairs={{0,2},{1,3},{2,4},{3,5},{4,6},{5,7},{6,0},{7,1},{8,10},{9,11},{10,... | collective-permute-start | bytes 786440 | tf_op jit(solution)/shard_map/ppermute | solution.py:33
  16.0 12.2 %collective-permute-start.6 = (bf16[512,256]{1,0:T(8,128)(2,1)S(1)}, bf16[512,256]{1,0:T(8,128)(2,1)}, u32[]{:S(2)}, u32[]{:S(2)}) collective-permute-start(bf16[512,256]{1,0:T(8,128)(2,1)S(1)} %get-tuple-element.21.rest_0_), channel_id=1, source_target_pairs={{0,1},{1,0},{2,3},{3,2},{4,5},{5,4},{6,7},{7,6},{8,9},{9,8},{10,11... | collective-permute-start | bytes 786440 | tf_op jit(solution)/shard_map/ppermute | solution.py:37
  16.1 70.9 %copy-start = (bf16[2,128,4096]{2,1,0:T(8,128)(2,1)S(1)}, bf16[2,128,4096]{2,1,0:T(8,128)(2,1)}, u32[]{:S(2)}) copy-start(bf16[2,128,4096]{2,1,0:T(8,128)(2,1)} %refs_3_.7) | copy-start | bytes 6291460
  16.1 70.9 %copy-start.3 = (s32[2]{0:T(128)S(1)}, s32[2]{0:T(128)}, u32[]{:S(2)}) copy-start(s32[2]{0:T(128)} %refs_1_.7) | copy-start | bytes 28
  16.1 12.7 %collective-permute-start.3 = (bf16[4,128,256]{2,1,0:T(8,128)(2,1)S(1)}, bf16[4,128,256]{2,1,0:T(8,128)(2,1)}, u32[]{:S(2)}, u32[]{:S(2)}) collective-permute-start(bf16[4,128,256]{2,1,0:T(8,128)(2,1)S(1)} %shard_map.122.s0), channel_id=1, source_target_pairs={{0,8},{8,16},{16,24},{24,0},{32,40},{40,48},{48,56},{56,32},{64,72... | collective-permute-start | bytes 786440 | tf_op jit(solution)/shard_map/ppermute | solution.py:28
  20.4 13.7 %collective-permute-start.4 = (bf16[4,128,256]{2,1,0:T(8,128)(2,1)S(1)}, bf16[4,128,256]{2,1,0:T(8,128)(2,1)}, u32[]{:S(2)}, u32[]{:S(2)}) collective-permute-start(bf16[4,128,256]{2,1,0:T(8,128)(2,1)S(1)} %shard_map.122.s0), channel_id=1, source_target_pairs={{0,16},{8,24},{16,0},{24,8},{32,48},{40,56},{48,32},{56,40},{64,80... | collective-permute-start | bytes 786440 | tf_op jit(solution)/shard_map/ppermute | solution.py:28
  24.9 17.7 %copy-start.6 = (bf16[256,512]{1,0:T(8,128)(2,1)S(1)}, bf16[256,512]{1,0:T(8,128)(2,1)}, u32[]{:S(2)}) copy-start(bf16[256,512]{1,0:T(8,128)(2,1)} %param.16) | copy-start | bytes 786436
  25.0 10.0 %collective-permute-start.5 = (bf16[4,128,256]{2,1,0:T(8,128)(2,1)S(1)}, bf16[4,128,256]{2,1,0:T(8,128)(2,1)S(1)}, u32[]{:S(2)}, u32[]{:S(2)}) collective-permute-start(bf16[4,128,256]{2,1,0:T(8,128)(2,1)S(1)} %shard_map.122.s0), channel_id=1, source_target_pairs={{0,24},{8,0},{16,8},{24,16},{32,56},{40,32},{48,40},{56,48},{64,88... | collective-permute-start | bytes 786440 | tf_op jit(solution)/shard_map/ppermute | solution.py:28
  28.3 6.7 %collective-permute-start.10 = (bf16[512,256]{1,0:T(8,128)(2,1)S(1)}, bf16[512,256]{1,0:T(8,128)(2,1)S(1)}, u32[]{:S(2)}, u32[]{:S(2)}) collective-permute-start(bf16[512,256]{1,0:T(8,128)(2,1)S(1)} %collective-permute-done.9.rest_4_), channel_id=1, source_target_pairs={{0,1},{1,0},{2,3},{3,2},{4,5},{5,4},{6,7},{7,6},{8,9},{9,8},{10,11... | collective-permute-start | bytes 786440 | tf_op jit(solution)/shard_map/ppermute | solution.py:37
  28.3 6.6 %collective-permute-start.12 = (bf16[512,256]{1,0:T(8,128)(2,1)}, bf16[512,256]{1,0:T(8,128)(2,1)S(1)}, u32[]{:S(2)}, u32[]{:S(2)}) collective-permute-start(bf16[512,256]{1,0:T(8,128)(2,1)} %collective-permute-done.11.rest_6_), channel_id=1, source_target_pairs={{0,1},{1,0},{2,3},{3,2},{4,5},{5,4},{6,7},{7,6},{8,9},{9,8},{10,11... | collective-permute-start | bytes 786440 | tf_op jit(solution)/shard_map/ppermute | solution.py:37
  28.8 6.1 %collective-permute-start.8 = (bf16[512,256]{1,0:T(8,128)(2,1)}, bf16[512,256]{1,0:T(8,128)(2,1)S(1)}, u32[]{:S(2)}, u32[]{:S(2)}) collective-permute-start(bf16[512,256]{1,0:T(8,128)(2,1)} %collective-permute-done.7.rest_2_), channel_id=1, source_target_pairs={{0,1},{1,0},{2,3},{3,2},{4,5},{5,4},{6,7},{7,6},{8,9},{9,8},{10,11... | collective-permute-start | bytes 786440 | tf_op jit(solution)/shard_map/ppermute | solution.py:37
  34.1 22.1 %collective-permute-start.26 = (bf16[2,512,256]{2,1,0:T(8,128)(2,1)S(1)}, bf16[2,512,256]{2,1,0:T(8,128)(2,1)S(1)}, u32[]{:S(2)}, u32[]{:S(2)}) collective-permute-start(bf16[2,512,256]{2,1,0:T(8,128)(2,1)S(1)} %get-tuple-element.28.rest_0_), channel_id=1, source_target_pairs={{0,2},{1,3},{2,4},{3,5},{4,6},{5,7},{6,0},{7,1},{8,10},{9,11},{10,... | collective-permute-start | bytes 1572872 | tf_op jit(solution)/shard_map/ppermute | solution.py:33
  37.2 6.1 %collective-permute-start.13 = (bf16[128,256]{1,0:T(8,128)(2,1)S(1)}, bf16[128,256]{1,0:T(8,128)(2,1)S(1)}, u32[]{:S(2)}, u32[]{:S(2)}) collective-permute-start(bf16[128,256]{1,0:T(8,128)(2,1)S(1)} %get-tuple-element.22.a0.query), channel_id=1, source_target_pairs={{0,32},{8,40},{16,48},{24,56},{32,64},{40,72},{48,80},{56,88},{64,... | collective-permute-start | bytes 196616 | tf_op jit(solution)/shard_map/ppermute | solution.py:21
  38.0 33.5 %collective-permute-start.28 = (bf16[2,512,256]{2,1,0:T(8,128)(2,1)S(1)}, bf16[2,512,256]{2,1,0:T(8,128)(2,1)S(1)}, u32[]{:S(2)}, u32[]{:S(2)}) collective-permute-start(bf16[2,512,256]{2,1,0:T(8,128)(2,1)S(1)} %get-tuple-element.28.rest_0_), channel_id=1, source_target_pairs={{0,4},{1,5},{2,6},{3,7},{4,0},{5,1},{6,2},{7,3},{8,12},{9,13},{10,... | collective-permute-start | bytes 1572872 | tf_op jit(solution)/shard_map/ppermute | solution.py:33
  41.0 41.7 %collective-permute-start.30 = (bf16[2,512,256]{2,1,0:T(8,128)(2,1)S(1)}, bf16[2,512,256]{2,1,0:T(8,128)(2,1)S(1)}, u32[]{:S(2)}, u32[]{:S(2)}) collective-permute-start(bf16[2,512,256]{2,1,0:T(8,128)(2,1)S(1)} %get-tuple-element.28.rest_0_), channel_id=1, source_target_pairs={{0,6},{1,7},{2,0},{3,1},{4,2},{5,3},{6,4},{7,5},{8,14},{9,15},{10,... | collective-permute-start | bytes 1572872 | tf_op jit(solution)/shard_map/ppermute | solution.py:33
  42.6 13.0 %collective-permute-start.35 = (bf16[256,512]{1,0:T(8,128)(2,1)S(1)}, bf16[256,512]{1,0:T(8,128)(2,1)S(1)}, u32[]{:S(2)}, u32[]{:S(2)}) collective-permute-start(bf16[256,512]{1,0:T(8,128)(2,1)S(1)} %copy-done.6), channel_id=1, source_target_pairs={{0,0},{1,1},{8,8},{9,9},{16,16},{17,17},{24,24},{25,25},{32,2},{33... | collective-permute-start | bytes 786440 | tf_op jit(solution)/shard_map/ppermute | solution.py:51
  43.3 8.1 %collective-permute-start.14 = (bf16[128,256]{1,0:T(8,128)(2,1)S(1)}, bf16[128,256]{1,0:T(8,128)(2,1)S(1)}, u32[]{:S(2)}, u32[]{:S(2)}) collective-permute-start(bf16[128,256]{1,0:T(8,128)(2,1)S(1)} %get-tuple-element.22.a0.query), channel_id=1, source_target_pairs={{0,64},{8,72},{16,80},{24,88},{32,96},{40,104},{48,112},{56,120},{... | collective-permute-start | bytes 196616 | tf_op jit(solution)/shard_map/ppermute | solution.py:21
  51.4 4.3 %collective-permute-start.15 = (bf16[128,256]{1,0:T(8,128)(2,1)S(1)}, bf16[128,256]{1,0:T(8,128)(2,1)S(1)}, u32[]{:S(2)}, u32[]{:S(2)}) collective-permute-start(bf16[128,256]{1,0:T(8,128)(2,1)S(1)} %get-tuple-element.22.a0.query), channel_id=1, source_target_pairs={{0,96},{8,104},{16,112},{24,120},{32,0},{40,8},{48,16},{56,24},{64... | collective-permute-start | bytes 196616 | tf_op jit(solution)/shard_map/ppermute | solution.py:21
  55.6 34.3 %collective-permute-start.25 = (bf16[2,512,256]{2,1,0:T(8,128)(2,1)S(1)}, bf16[2,512,256]{2,1,0:T(8,128)(2,1)S(1)}, u32[]{:S(2)}, u32[]{:S(2)}) collective-permute-start(bf16[2,512,256]{2,1,0:T(8,128)(2,1)S(1)} %get-tuple-element.28.rest_0_), channel_id=1, source_target_pairs={{0,1},{1,0},{2,3},{3,2},{4,5},{5,4},{6,7},{7,6},{8,9},{9,8},{10,11... | collective-permute-start | bytes 1572872 | tf_op jit(solution)/shard_map/ppermute | solution.py:37
  55.7 31.4 %collective-permute-start.16 = (bf16[4,128,256]{2,1,0:T(8,128)(2,1)S(1)}, bf16[4,128,256]{2,1,0:T(8,128)(2,1)S(1)}, u32[]{:S(2)}, u32[]{:S(2)}) collective-permute-start(bf16[4,128,256]{2,1,0:T(8,128)(2,1)S(1)} %shard_map.124.refs_2_), channel_id=1, source_target_pairs={{0,8},{8,16},{16,24},{24,0},{32,40},{40,48},{48,56},{56,32},{64,72... | collective-permute-start | bytes 786440 | tf_op jit(solution)/shard_map/ppermute | solution.py:28
  56.2 34.4 %collective-permute-start.37 = (bf16[256,512]{1,0:T(8,128)(2,1)S(1)}, bf16[256,512]{1,0:T(8,128)(2,1)S(1)}, u32[]{:S(2)}, u32[]{:S(2)}) collective-permute-start(bf16[256,512]{1,0:T(8,128)(2,1)S(1)} %collective-permute-done.35.rest_0_), channel_id=1, source_target_pairs={{0,2},{1,3},{2,4},{3,5},{4,6},{5,7},{6,0},{7,1},{8,10},{9,11},{10,... | collective-permute-start | bytes 786440 | tf_op jit(solution)/shard_map/ppermute | solution.py:33
  71.4 24.9 %collective-permute-start.39 = (bf16[256,512]{1,0:T(8,128)(2,1)S(1)}, bf16[256,512]{1,0:T(8,128)(2,1)S(1)}, u32[]{:S(2)}, u32[]{:S(2)}) collective-permute-start(bf16[256,512]{1,0:T(8,128)(2,1)S(1)} %collective-permute-done.35.rest_0_), channel_id=1, source_target_pairs={{0,4},{1,5},{2,6},{3,7},{4,0},{5,1},{6,2},{7,3},{8,12},{9,13},{10,... | collective-permute-start | bytes 786440 | tf_op jit(solution)/shard_map/ppermute | solution.py:33
  82.8 13.6 %collective-permute-start.18 = (bf16[4,128,256]{2,1,0:T(8,128)(2,1)S(1)}, bf16[4,128,256]{2,1,0:T(8,128)(2,1)S(1)}, u32[]{:S(2)}, u32[]{:S(2)}) collective-permute-start(bf16[4,128,256]{2,1,0:T(8,128)(2,1)S(1)} %shard_map.124.refs_2_), channel_id=1, source_target_pairs={{0,16},{8,24},{16,0},{24,8},{32,48},{40,56},{48,32},{56,40},{64,80... | collective-permute-start | bytes 786440 | tf_op jit(solution)/shard_map/ppermute | solution.py:28
  87.0 12.2 %collective-permute-start.20 = (bf16[4,128,256]{2,1,0:T(8,128)(2,1)S(1)}, bf16[4,128,256]{2,1,0:T(8,128)(2,1)S(1)}, u32[]{:S(2)}, u32[]{:S(2)}) collective-permute-start(bf16[4,128,256]{2,1,0:T(8,128)(2,1)S(1)} %shard_map.124.refs_2_), channel_id=1, source_target_pairs={{0,24},{8,0},{16,8},{24,16},{32,56},{40,32},{48,40},{56,48},{64,88... | collective-permute-start | bytes 786440 | tf_op jit(solution)/shard_map/ppermute | solution.py:28
  87.0 1.6 %copy-start.1 = (bf16[2,128,4096]{2,1,0:T(8,128)(2,1)S(1)}, bf16[2,128,4096]{2,1,0:T(8,128)(2,1)}, u32[]{:S(2)}) copy-start(bf16[2,128,4096]{2,1,0:T(8,128)(2,1)} %refs_4_.7) | copy-start | bytes 6291460
  90.0 13.6 %collective-permute-start.17 = (bf16[1072,128]{1,0:T(8,128)(2,1)S(1)}, bf16[1072,128]{1,0:T(8,128)(2,1)S(1)}, u32[]{:S(2)}, u32[]{:S(2)}) collective-permute-start(bf16[1072,128]{1,0:T(8,128)(2,1)S(1)} %shard_map.126), channel_id=1, source_target_pairs={{0,24},{8,0},{16,8},{24,16},{32,56},{40,32},{48,40},{56,48},{64,88... | collective-permute-start | bytes 823304 | tf_op jit(solution)/shard_map/ppermute | solution.py:28
  90.7 11.2 %collective-permute-start.41 = (bf16[256,512]{1,0:T(8,128)(2,1)S(1)}, bf16[256,512]{1,0:T(8,128)(2,1)S(1)}, u32[]{:S(2)}, u32[]{:S(2)}) collective-permute-start(bf16[256,512]{1,0:T(8,128)(2,1)S(1)} %collective-permute-done.35.rest_0_), channel_id=1, source_target_pairs={{0,6},{1,7},{2,0},{3,1},{4,2},{5,3},{6,4},{7,5},{8,14},{9,15},{10,... | collective-permute-start | bytes 786440 | tf_op jit(solution)/shard_map/ppermute | solution.py:33
  96.4 24.1 %collective-permute-start.27 = (bf16[2,512,256]{2,1,0:T(8,128)(2,1)S(1)}, bf16[2,512,256]{2,1,0:T(8,128)(2,1)S(1)}, u32[]{:S(2)}, u32[]{:S(2)}) collective-permute-start(bf16[2,512,256]{2,1,0:T(8,128)(2,1)S(1)} %collective-permute-done.26.rest_2_), channel_id=1, source_target_pairs={{0,1},{1,0},{2,3},{3,2},{4,5},{5,4},{6,7},{7,6},{8,9},{9,8},{10,11... | collective-permute-start | bytes 1572872 | tf_op jit(solution)/shard_map/ppermute | solution.py:37
  96.4 24.2 %collective-permute-start.29 = (bf16[2,512,256]{2,1,0:T(8,128)(2,1)S(1)}, bf16[2,512,256]{2,1,0:T(8,128)(2,1)S(1)}, u32[]{:S(2)}, u32[]{:S(2)}) collective-permute-start(bf16[2,512,256]{2,1,0:T(8,128)(2,1)S(1)} %collective-permute-done.28.rest_4_), channel_id=1, source_target_pairs={{0,1},{1,0},{2,3},{3,2},{4,5},{5,4},{6,7},{7,6},{8,9},{9,8},{10,11... | collective-permute-start | bytes 1572872 | tf_op jit(solution)/shard_map/ppermute | solution.py:37
  99.2 21.9 %collective-permute-start.31 = (bf16[2,512,256]{2,1,0:T(8,128)(2,1)S(1)}, bf16[2,512,256]{2,1,0:T(8,128)(2,1)S(1)}, u32[]{:S(2)}, u32[]{:S(2)}) collective-permute-start(bf16[2,512,256]{2,1,0:T(8,128)(2,1)S(1)} %collective-permute-done.30.rest_6_), channel_id=1, source_target_pairs={{0,1},{1,0},{2,3},{3,2},{4,5},{5,4},{6,7},{7,6},{8,9},{9,8},{10,11... | collective-permute-start | bytes 1572872 | tf_op jit(solution)/shard_map/ppermute | solution.py:37
  100.6 17.8 %copy-start.2 = (bf16[2,128,4096]{2,1,0:T(8,128)(2,1)S(1)}, bf16[2,128,4096]{2,1,0:T(8,128)(2,1)}, u32[]{:S(2)}) copy-start(bf16[2,128,4096]{2,1,0:T(8,128)(2,1)} %refs_4_.7) | copy-start | bytes 6291460
  101.9 11.1 %collective-permute-start.19 = (bf16[1072,128]{1,0:T(8,128)(2,1)S(1)}, bf16[1072,128]{1,0:T(8,128)(2,1)S(1)}, u32[]{:S(2)}, u32[]{:S(2)}) collective-permute-start(bf16[1072,128]{1,0:T(8,128)(2,1)S(1)} %shard_map.127), channel_id=1, source_target_pairs={{0,16},{8,24},{16,0},{24,8},{32,48},{40,56},{48,32},{56,40},{64,80... | collective-permute-start | bytes 823304 | tf_op jit(solution)/shard_map/ppermute | solution.py:28
  103.6 14.7 %collective-permute-start.21 = (bf16[1072,128]{1,0:T(8,128)(2,1)S(1)}, bf16[1072,128]{1,0:T(8,128)(2,1)S(1)}, u32[]{:S(2)}, u32[]{:S(2)}) collective-permute-start(bf16[1072,128]{1,0:T(8,128)(2,1)S(1)} %shard_map.128), channel_id=1, source_target_pairs={{0,8},{8,16},{16,24},{24,0},{32,40},{40,48},{48,56},{56,32},{64,72... | collective-permute-start | bytes 823304 | tf_op jit(solution)/shard_map/ppermute | solution.py:28
  113.0 24.0 %collective-permute-start.36 = (bf16[256,512]{1,0:T(8,128)(2,1)S(1)}, bf16[256,512]{1,0:T(8,128)(2,1)S(1)}, u32[]{:S(2)}, u32[]{:S(2)}) collective-permute-start(bf16[256,512]{1,0:T(8,128)(2,1)S(1)} %collective-permute-done.35.rest_0_), channel_id=1, source_target_pairs={{0,1},{1,0},{2,3},{3,2},{4,5},{5,4},{6,7},{7,6},{8,9},{9,8},{10,11... | collective-permute-start | bytes 786440 | tf_op jit(solution)/shard_map/ppermute | solution.py:37
  118.3 20.4 %collective-permute-start.38 = (bf16[256,512]{1,0:T(8,128)(2,1)S(1)}, bf16[256,512]{1,0:T(8,128)(2,1)S(1)}, u32[]{:S(2)}, u32[]{:S(2)}) collective-permute-start(bf16[256,512]{1,0:T(8,128)(2,1)S(1)} %collective-permute-done.37.rest_2_), channel_id=1, source_target_pairs={{0,1},{1,0},{2,3},{3,2},{4,5},{5,4},{6,7},{7,6},{8,9},{9,8},{10,11... | collective-permute-start | bytes 786440 | tf_op jit(solution)/shard_map/ppermute | solution.py:37
  120.5 4.6 %collective-permute-start.22 = (bf16[272,128]{1,0:T(8,128)(2,1)S(1)}, bf16[272,128]{1,0:T(8,128)(2,1)S(1)}, u32[]{:S(2)}, u32[]{:S(2)}) collective-permute-start(bf16[272,128]{1,0:T(8,128)(2,1)S(1)} %get-tuple-element.24), channel_id=1, source_target_pairs={{0,96},{8,104},{16,112},{24,120},{32,0},{40,8},{48,16},{56,24},{64... | collective-permute-start | bytes 208904 | tf_op jit(solution)/shard_map/ppermute | solution.py:21
  120.6 19.7 %collective-permute-start.40 = (bf16[256,512]{1,0:T(8,128)(2,1)S(1)}, bf16[256,512]{1,0:T(8,128)(2,1)S(1)}, u32[]{:S(2)}, u32[]{:S(2)}) collective-permute-start(bf16[256,512]{1,0:T(8,128)(2,1)S(1)} %collective-permute-done.39.rest_4_), channel_id=1, source_target_pairs={{0,1},{1,0},{2,3},{3,2},{4,5},{5,4},{6,7},{7,6},{8,9},{9,8},{10,11... | collective-permute-start | bytes 786440 | tf_op jit(solution)/shard_map/ppermute | solution.py:37
  121.2 19.1 %collective-permute-start.42 = (bf16[256,512]{1,0:T(8,128)(2,1)S(1)}, bf16[256,512]{1,0:T(8,128)(2,1)S(1)}, u32[]{:S(2)}, u32[]{:S(2)}) collective-permute-start(bf16[256,512]{1,0:T(8,128)(2,1)S(1)} %collective-permute-done.41.rest_6_), channel_id=1, source_target_pairs={{0,1},{1,0},{2,3},{3,2},{4,5},{5,4},{6,7},{7,6},{8,9},{9,8},{10,11... | collective-permute-start | bytes 786440 | tf_op jit(solution)/shard_map/ppermute | solution.py:37
  125.1 5.8 %collective-permute-start.23 = (bf16[272,128]{1,0:T(8,128)(2,1)S(1)}, bf16[272,128]{1,0:T(8,128)(2,1)S(1)}, u32[]{:S(2)}, u32[]{:S(2)}) collective-permute-start(bf16[272,128]{1,0:T(8,128)(2,1)S(1)} %get-tuple-element.25), channel_id=1, source_target_pairs={{0,64},{8,72},{16,80},{24,88},{32,96},{40,104},{48,112},{56,120},{... | collective-permute-start | bytes 208904 | tf_op jit(solution)/shard_map/ppermute | solution.py:21
  131.0 5.5 %collective-permute-start.24 = (bf16[272,128]{1,0:T(8,128)(2,1)S(1)}, bf16[272,128]{1,0:T(8,128)(2,1)S(1)}, u32[]{:S(2)}, u32[]{:S(2)}) collective-permute-start(bf16[272,128]{1,0:T(8,128)(2,1)S(1)} %get-tuple-element.26), channel_id=1, source_target_pairs={{0,32},{8,40},{16,48},{24,56},{32,64},{40,72},{48,80},{56,88},{64,... | collective-permute-start | bytes 208904 | tf_op jit(solution)/shard_map/ppermute | solution.py:21
  136.9 6.2 %collective-permute-start.32 = (bf16[128,256]{1,0:T(8,128)(2,1)S(1)}, bf16[128,256]{1,0:T(8,128)(2,1)S(1)}, u32[]{:S(2)}, u32[]{:S(2)}) collective-permute-start(bf16[128,256]{1,0:T(8,128)(2,1)S(1)} %shard_map.132.a0), channel_id=1, source_target_pairs={{0,32},{8,40},{16,48},{24,56},{32,64},{40,72},{48,80},{56,88},{64,... | collective-permute-start | bytes 196616 | tf_op jit(solution)/shard_map/ppermute | solution.py:21
  137.0 6.2 %collective-permute-start.33 = (bf16[128,256]{1,0:T(8,128)(2,1)S(1)}, bf16[128,256]{1,0:T(8,128)(2,1)S(1)}, u32[]{:S(2)}, u32[]{:S(2)}) collective-permute-start(bf16[128,256]{1,0:T(8,128)(2,1)S(1)} %shard_map.132.a0), channel_id=1, source_target_pairs={{0,64},{8,72},{16,80},{24,88},{32,96},{40,104},{48,112},{56,120},{... | collective-permute-start | bytes 196616 | tf_op jit(solution)/shard_map/ppermute | solution.py:21
  138.7 5.3 %collective-permute-start.34 = (bf16[128,256]{1,0:T(8,128)(2,1)S(1)}, bf16[128,256]{1,0:T(8,128)(2,1)S(1)}, u32[]{:S(2)}, u32[]{:S(2)}) collective-permute-start(bf16[128,256]{1,0:T(8,128)(2,1)S(1)} %shard_map.132.a0), channel_id=1, source_target_pairs={{0,96},{8,104},{16,112},{24,120},{32,0},{40,8},{48,16},{56,24},{64... | collective-permute-start | bytes 196616 | tf_op jit(solution)/shard_map/ppermute | solution.py:21
  145.0 5.5 %collective-permute-start.43 = (bf16[128,256]{1,0:T(8,128)(2,1)S(1)}, bf16[128,256]{1,0:T(8,128)(2,1)S(1)}, u32[]{:S(2)}, u32[]{:S(2)}) collective-permute-start(bf16[128,256]{1,0:T(8,128)(2,1)S(1)} %get-tuple-element.34), channel_id=1, source_target_pairs={{0,8},{8,16},{16,24},{24,0},{32,40},{40,48},{48,56},{56,32},{64,72... | collective-permute-start | bytes 196616 | tf_op jit(solution)/shard_map/ppermute | solution.py:28
  145.1 5.7 %collective-permute-start.44 = (bf16[128,256]{1,0:T(8,128)(2,1)S(1)}, bf16[128,256]{1,0:T(8,128)(2,1)S(1)}, u32[]{:S(2)}, u32[]{:S(2)}) collective-permute-start(bf16[128,256]{1,0:T(8,128)(2,1)S(1)} %get-tuple-element.35), channel_id=1, source_target_pairs={{0,24},{8,0},{16,8},{24,16},{32,56},{40,32},{48,40},{56,48},{64,88... | collective-permute-start | bytes 196616 | tf_op jit(solution)/shard_map/ppermute | solution.py:28
  148.3 5.8 %collective-permute-start.45 = (bf16[128,256]{1,0:T(8,128)(2,1)S(1)}, bf16[128,256]{1,0:T(8,128)(2,1)S(1)}, u32[]{:S(2)}, u32[]{:S(2)}) collective-permute-start(bf16[128,256]{1,0:T(8,128)(2,1)S(1)} %get-tuple-element.36), channel_id=1, source_target_pairs={{0,16},{8,24},{16,0},{24,8},{32,48},{40,56},{48,32},{56,40},{64,80... | collective-permute-start | bytes 196616 | tf_op jit(solution)/shard_map/ppermute | solution.py:28

commit v2 on v1

--- a/solution.py
+++ b/solution.py
@@ -1,5 +1,6 @@
 import jax
 import jax.numpy as jnp
+import numpy as np
 from jax import lax
 from jax.experimental import pallas as pl
 from jax.experimental.pallas import tpu as pltpu
@@ -63,7 +64,10 @@
 
 def over_x(x):
     mine = from_ring(x, x_shift)
-    return [p for m in mine for p in (m, other_core(m))]
+    both = []
+    for m in mine:
+        both += [m, other_core(m)]
+    return both
 
 
 VMEM = pl.BlockSpec(memory_space=pltpu.VMEM)
@@ -81,8 +85,6 @@
 
 
 def placed(spec, x):
-    if spec is SMEM:
-        return x
     return held(x) if spec is VMEM else outside(x)
 
 
@@ -106,6 +108,12 @@
     return jax.ShapeDtypeStruct(dims, kind)
 
 
+def position():
+    ctx_rank = lax.axis_index("ctx")
+    wt_rank = lax.axis_index("wt")
+    return wt_rank // 2, wt_rank % 2, ctx_rank // SIDE, ctx_rank % SIDE
+
+
 def matmul(a, b):
     return jnp.dot(a, b, preferred_element_type=f32)
 
@@ -114,13 +122,49 @@
     return lax.dot_general(a, b, (((1,), (1,)), ((), ())), preferred_element_type=f32)
 
 
-def adapter_body(source, frames, weight, bias, kinds, out, query_weight, other_weight, ordered, sems):
+def turns(count, step):
+    freq = 10000.0 ** (-2.0 * (np.arange(HEAD) % (HEAD // 2)) / HEAD)
+    angle = step * np.arange(count)[:, None] * freq[None, :]
+    return np.stack([np.cos(angle), np.sin(angle)]).astype(np.float32)
+
+
+def rope_tables(lengths, coarse, fine, cosine, sine, new):
+    lane = lax.broadcasted_iota(jnp.int32, (new, HEAD), 1)
+    for m in range(cosine.shape[0] // new):
+        high = lengths[m] // new
+        low = lengths[m] - high * new
+        c1, s1 = coarse[0, pl.ds(high, 1), :], coarse[1, pl.ds(high, 1), :]
+        c2, s2 = fine[0, pl.ds(low, new), :], fine[1, pl.ds(low, new), :]
+        here = slice(m * new, (m + 1) * new)
+        cosine[here, :] = c1 * c2 - s1 * s2
+        value = s1 * c2 + c1 * s2
+        sine[here, :] = jnp.where(lane < HEAD // 2, -value, value)
+
+
+def adapter_body(
+    source,
+    lengths,
+    frames,
+    weight,
+    bias,
+    coarse,
+    fine,
+    kinds,
+    out,
+    query_weight,
+    other_weight,
+    cosine,
+    sine,
+    ordered,
+    sems,
+):
     copies = (
         pltpu.make_async_copy(kinds.at[0], query_weight, sems.at[0]),
         pltpu.make_async_copy(kinds.at[1:3], other_weight, sems.at[1]),
     )
     for copy in copies:
         copy.start()
+    rope_tables(lengths, coarse, fine, cosine, sine, fine.shape[1] // 2)
     spans = source.shape[0]
     rows = frames.shape[0] // spans
     for g in range(spans):
@@ -156,8 +200,9 @@
     return total
 
 
-def query_body(place, s0, s1, s2, s3, gain, cosine, sine, *rest):
+def query_body(s0, s1, s2, s3, gain, cosine, sine, *rest):
     weights, (query, normed) = rest[:8], rest[8:]
+    place = position()
     stacks = (s0, s1, s2, s3)
     rows = s0.shape[1]
     sums = jnp.zeros((rows, HEAD), f32)
@@ -178,8 +223,9 @@
         query[:, cut] = spin(projected[:, cut], cosine[...], sine[...]).astype(bf16)
 
 
-def key_value_body(place, normed, cosine, sine, *rest):
+def key_value_body(normed, cosine, sine, *rest):
     weights, (keys, values) = rest[:8], rest[8:]
+    place = position()
     projected = pieces_product(place, normed, weights, lambda w: w[0])
     for h in range(projected.shape[1] // HEAD):
         cut = slice(h * HEAD, (h + 1) * HEAD)
@@ -200,8 +246,9 @@
     return weights, most, jnp.sum(weights, axis=-1, keepdims=True)
 
 
-def history_body(step, place, lengths, stack, k_cache, v_cache, out, scores, weights):
+def history_body(step, lengths, stack, k_cache, v_cache, out, scores, weights):
     meetings, span = k_cache.shape[0], k_cache.shape[1]
+    place = position()
     rows = stack.shape[1]
     new = rows // meetings
     heads = 2 * SIDE
@@ -326,8 +373,9 @@
         out[:, h * HEAD : (h + 1) * HEAD] = mixed.astype(bf16)
 
 
-def project_body(place, a0, a1, a2, a3, *rest):
+def project_body(a0, a1, a2, a3, *rest):
     weights, (own, o1, o2, o3, across, sums) = rest[:8], rest[8:]
+    place = position()
     for k, a in enumerate((a0, a1, a2, a3)):
         across[(place[2] + SIDE - k) % SIDE] = a[...]
     for c in range(2):
@@ -366,33 +414,30 @@
     meetings = lengths.shape[0]
     new = rows // meetings
     heads = 2 * SIDE
-    ctx_rank = lax.axis_index("ctx")
-    wt_rank = lax.axis_index("wt")
-    place = jnp.stack(
-        [wt_rank // 2, wt_rank % 2, ctx_rank // SIDE, ctx_rank % SIDE]
-    ).astype(jnp.int32)
-
-    token = lax.broadcasted_iota(jnp.int32, (rows, HEAD), 0)
-    lane = lax.broadcasted_iota(jnp.int32, (rows, HEAD), 1)
-    half = HEAD // 2
-    positions = jnp.where(token < new, lengths[0], lengths[1] - new) + token
-    freq = 10000.0 ** (-2.0 * (jnp.arange(HEAD, dtype=jnp.int32) % half).astype(f32) / HEAD)
-    angle = positions.astype(f32) * freq[None, :]
-    cosine = jnp.cos(angle)
-    sine = jnp.where(lane < half, -jnp.sin(angle), jnp.sin(angle))
-
     by_kind = jnp.transpose(qkv_weight, (1, 0, 2))
     feats = by_kind.shape[1]
-    adapted, query_weight, other_weight = kernel_call(
+    longest = SIDE * SIDE * k_cache.shape[1]
+    coarse = jnp.asarray(turns(longest // new + 8, new))
+    fine = jnp.asarray(turns(2 * new, 1))
+    adapted, query_weight, other_weight, cosine, sine = kernel_call(
         adapter_body,
         [
             (SMEM, span_source),
+            (SMEM, lengths),
             (WHOLE, frames),
             (WHOLE, adapter_weight),
             (WHOLE, adapter_bias.reshape(1, cols)),
+            (WHOLE, coarse),
+            (WHOLE, fine),
             (ANY, by_kind),
         ],
-        (near((rows, cols), bf16), near((feats, cols), bf16), near((2, feats, cols), bf16)),
+        (
+            near((rows, cols), bf16),
+            near((feats, cols), bf16),
+            near((2, feats, cols), bf16),
+            near((rows, HEAD), f32),
+            near((rows, HEAD), f32),
+        ),
         [pltpu.VMEM(frames.shape, bf16), pltpu.SemaphoreType.DMA((2,))],
     )
     column = stacked(from_ring(adapted, y_shift))
@@ -406,18 +451,20 @@
     gain = norm_gain.reshape(SIDE * SIDE, 1, cols)
     query, normed = kernel_call(
         query_body,
-        [(SMEM, place)]
-        + [(VMEM, s) for s in stacks]
+        [(VMEM, s) for s in stacks]
         + [(VMEM, gain), (VMEM, cosine), (VMEM, sine)]
         + [(VMEM, w) for w in query_weights],
-        (near((rows, cols), bf16), near((SIDE * SIDE, rows, cols), bf16)),
+        (
+            near((rows, cols), bf16),
+            near((SIDE * SIDE, rows, cols), bf16),
+        ),
     )
     query_column = stacked(from_ring(query, y_shift))
     query_stacks = from_ring(query_column, z_shift)
 
     keys, values = kernel_call(
         key_value_body,
-        [(SMEM, place), (VMEM, normed), (VMEM, cosine), (VMEM, sine)]
+        [(VMEM, normed), (VMEM, cosine), (VMEM, sine)]
         + [(VMEM, w) for w in other_weights],
         (near((rows, cols), bf16), near((rows, cols), bf16)),
     )
@@ -426,7 +473,6 @@
         return kernel_call(
             lambda *refs: history_body(step, *refs),
             [
-                (SMEM, place),
                 (SMEM, lengths),
                 (VMEM, query_stacks[step]),
                 (VMEM, k_cache),
@@ -462,7 +508,7 @@
     part = near((rows, cols), bf16)
     sums = kernel_call(
         project_body,
-        [(SMEM, place)] + [(VMEM, a) for a in across] + [(VMEM, w) for w in out_weights],
+        [(VMEM, a) for a in across] + [(VMEM, w) for w in out_weights],
         (near((rows, cols), f32), part, part, part),
         [pltpu.VMEM((SIDE, rows, cols), bf16), pltpu.VMEM((SIDE, rows, cols), f32)],
     )

time: 155 us -> 153 us (0.987)
  waiting for transfers between devices: 50 us -> 54.2 us
  local copies, waits for them, and re-layouts: 4.84 us -> 1.27 us
  Pallas kernels: 15.2 us -> 13.5 us
    unnamed x16 -> x10, local copies, waits for them, and re-layouts: 3.53 us -> 1.27 us
    ppermute x9, waiting for transfers between devices: 1.61 us -> 3.62 us  [x_shift(): return lax.ppermute(x, 'wt', pairs)]
    ppermute x12, waiting for transfers between devices: 27.2 us -> 29 us  [z_shift(): return lax.ppermute(x, 'ctx', pairs)]
    pallas_call x14, Pallas kernels: 15.2 us -> 13.5 us  [kernel_call(): pl.pallas_call(body, in_specs=[s for s, _ in ins], out_specs=VMEM if sing...]
  transfers between devices with their start and end apart: 46 -> 46, of which waited for: 17 -> 17; matrix products, arithmetic and copies ran while one was open for 2% -> 1% of each run, Pallas kernels for 7% -> 6%
where the time goes in v2:
time: 153 us
  starting transfers between devices  83 us (54%)
  waiting for transfers between devices  54.2 us (35%)
  Pallas kernels  13.5 us (9%)
    ppermute x9, starting transfers between devices, x_shift(): return lax.ppermute(x, 'wt', pairs)  42.5 us
    ppermute x12, waiting for transfers between devices, z_shift(): return lax.ppermute(x, 'ctx', pairs)  29 us
    ppermute x12, waiting for transfers between devices, y_shift(): return lax.ppermute(x, 'ctx', pairs)  21.6 us
    ppermute x12, starting transfers between devices, z_shift(): return lax.ppermute(x, 'ctx', pairs)  20 us
    ppermute x12, starting transfers between devices, y_shift(): return lax.ppermute(x, 'ctx', pairs)  18.1 us
    pallas_call x14, Pallas kernels, kernel_call(): pl.pallas_call(body, in_specs=[s for s, _ in ins], out_specs=VMEM if sing...  13.5 us
    ppermute x9, waiting for transfers between devices, x_shift(): return lax.ppermute(x, 'wt', pairs)  3.62 us
  transfers between devices with their start and end apart: 46, of which 17 were waited for; matrix products, arithmetic and copies ran while one was open for 1% of the time, Pallas kernels for 6%

profile of v2, /device:TPU:0, one launch (start us, length us, event | category | flops | bytes accessed | tf_op | source)
XLA Modules:
  0.0 152.8 jit_solution(4165068726469625689)
XLA Ops:
  0.7 2.5 %shard_map.139 = (bf16[128,256]{1,0:T(8,128)(2,1)S(1)}, bf16[512,256]{1,0:T(8,128)(2,1)S(1)}, bf16[2,512,256]{2,1,0:T(8,128)(2,1)S(1)}, f32[128,128]{1,0:T(8,128)S(1)}, f32[128,128]{1,0:T(8,128)S(1)}) custom-call(s32[8]{0:T(128)} %source.1, s32[2]{0:T(128)} %refs_0_.7, bf16[128,1280]{1,0:T(8,128)(2,1)} %frames.1, bf16[1280,256]{1,0:T(8,128)(2,1)} %weight.1, ...), custom_call_target="tpu_custom_call" | custom-call | tf_op jit(solution)/shard_map/pallas_call | solution.py:93
  3.2 1.8 %collective-permute-start = (bf16[128,256]{1,0:T(8,128)(2,1)S(1)}, bf16[128,256]{1,0:T(8,128)(2,1)S(1)}, u32[]{:S(2)}, u32[]{:S(2)}) collective-permute-start(bf16[128,256]{1,0:T(8,128)(2,1)S(1)} %get-tuple-element.22.a0), channel_id=1, source_target_pairs={{0,32},{8,40},{16,48},{24,56},{32,64},{40,72},{48,80},{56,88},{64,... | collective-permute-start | bytes 196616 | tf_op jit(solution)/shard_map/ppermute | solution.py:22
  4.9 2.9 %collective-permute-start.1 = (bf16[128,256]{1,0:T(8,128)(2,1)S(1)}, bf16[128,256]{1,0:T(8,128)(2,1)S(1)}, u32[]{:S(2)}, u32[]{:S(2)}) collective-permute-start(bf16[128,256]{1,0:T(8,128)(2,1)S(1)} %get-tuple-element.22.a0), channel_id=1, source_target_pairs={{0,64},{8,72},{16,80},{24,88},{32,96},{40,104},{48,112},{56,120},{... | collective-permute-start | bytes 196616 | tf_op jit(solution)/shard_map/ppermute | solution.py:22
  7.8 1.3 collective-permute-start.2
  9.2 3.0 %collective-permute-start.9 = (bf16[512,256]{1,0:T(8,128)(2,1)S(1)}, bf16[512,256]{1,0:T(8,128)(2,1)S(1)}, u32[]{:S(2)}, u32[]{:S(2)}) collective-permute-start(bf16[512,256]{1,0:T(8,128)(2,1)S(1)} %get-tuple-element.25.rest_0_), channel_id=1, source_target_pairs={{0,4},{1,5},{2,6},{3,7},{4,0},{5,1},{6,2},{7,3},{8,12},{9,13},{10,... | collective-permute-start | bytes 786440 | tf_op jit(solution)/shard_map/ppermute | solution.py:34
  12.2 1.1 collective-permute-start.11
  13.3 0.9 collective-permute-start.7
  14.3 2.0 %collective-permute-start.3 = (bf16[4,128,256]{2,1,0:T(8,128)(2,1)S(1)}, bf16[4,128,256]{2,1,0:T(8,128)(2,1)S(1)}, u32[]{:S(2)}, u32[]{:S(2)}) collective-permute-start(bf16[4,128,256]{2,1,0:T(8,128)(2,1)S(1)} %shard_map.140.s0), channel_id=1, source_target_pairs={{0,8},{8,16},{16,24},{24,0},{32,40},{40,48},{48,56},{56,32},{64,72... | collective-permute-start | bytes 786440 | tf_op jit(solution)/shard_map/ppermute | solution.py:29
  16.2 3.6 %collective-permute-done.9.rest_4_ = bf16[512,256]{1,0:T(8,128)(2,1)S(1)} collective-permute-done((bf16[512,256]{1,0:T(8,128)(2,1)S(1)}, bf16[512,256]{1,0:T(8,128)(2,1)S(1)}, u32[]{:S(2)}, u32[]{:S(2)}) %collective-permute-start.9) | collective-permute-done | bytes 262176 | tf_op jit(solution)/shard_map/ppermute | solution.py:34
  19.8 3.9 %collective-permute-start.4 = (bf16[4,128,256]{2,1,0:T(8,128)(2,1)S(1)}, bf16[4,128,256]{2,1,0:T(8,128)(2,1)S(1)}, u32[]{:S(2)}, u32[]{:S(2)}) collective-permute-start(bf16[4,128,256]{2,1,0:T(8,128)(2,1)S(1)} %shard_map.140.s0), channel_id=1, source_target_pairs={{0,16},{8,24},{16,0},{24,8},{32,48},{40,56},{48,32},{56,40},{64,80... | collective-permute-start | bytes 786440 | tf_op jit(solution)/shard_map/ppermute | solution.py:29
  23.7 3.9 %collective-permute-start.5 = (bf16[4,128,256]{2,1,0:T(8,128)(2,1)S(1)}, bf16[4,128,256]{2,1,0:T(8,128)(2,1)S(1)}, u32[]{:S(2)}, u32[]{:S(2)}) collective-permute-start(bf16[4,128,256]{2,1,0:T(8,128)(2,1)S(1)} %shard_map.140.s0), channel_id=1, source_target_pairs={{0,24},{8,0},{16,8},{24,16},{32,56},{40,32},{48,40},{56,48},{64,88... | collective-permute-start | bytes 786440 | tf_op jit(solution)/shard_map/ppermute | solution.py:29
  27.7 0.5 collective-permute-start.12
  28.2 0.1 collective-permute-start.8
  28.3 3.9 %collective-permute-done.4.s2 = bf16[4,128,256]{2,1,0:T(8,128)(2,1)S(1)} collective-permute-done((bf16[4,128,256]{2,1,0:T(8,128)(2,1)S(1)}, bf16[4,128,256]{2,1,0:T(8,128)(2,1)S(1)}, u32[]{:S(2)}, u32[]{:S(2)}) %collective-permute-start.4) | collective-permute-done | bytes 262176 | tf_op jit(solution)/shard_map/ppermute | solution.py:29
  32.1 0.6 collective-permute-start.26
  32.7 1.7 %collective-permute-done.5.s3 = bf16[4,128,256]{2,1,0:T(8,128)(2,1)S(1)} collective-permute-done((bf16[4,128,256]{2,1,0:T(8,128)(2,1)S(1)}, bf16[4,128,256]{2,1,0:T(8,128)(2,1)S(1)}, u32[]{:S(2)}, u32[]{:S(2)}) %collective-permute-start.5) | collective-permute-done | bytes 262176 | tf_op jit(solution)/shard_map/ppermute | solution.py:29
  34.4 1.0 shard_map.141
  35.4 0.7 collective-permute-start.13
  36.2 2.5 %collective-permute-start.28 = (bf16[2,512,256]{2,1,0:T(8,128)(2,1)S(1)}, bf16[2,512,256]{2,1,0:T(8,128)(2,1)S(1)}, u32[]{:S(2)}, u32[]{:S(2)}) collective-permute-start(bf16[2,512,256]{2,1,0:T(8,128)(2,1)S(1)} %get-tuple-element.32.rest_0_), channel_id=1, source_target_pairs={{0,4},{1,5},{2,6},{3,7},{4,0},{5,1},{6,2},{7,3},{8,12},{9,13},{10,... | collective-permute-start | bytes 1572872 | tf_op jit(solution)/shard_map/ppermute | solution.py:34
  38.7 2.1 %collective-permute-start.30 = (bf16[2,512,256]{2,1,0:T(8,128)(2,1)S(1)}, bf16[2,512,256]{2,1,0:T(8,128)(2,1)S(1)}, u32[]{:S(2)}, u32[]{:S(2)}) collective-permute-start(bf16[2,512,256]{2,1,0:T(8,128)(2,1)S(1)} %get-tuple-element.32.rest_0_), channel_id=1, source_target_pairs={{0,6},{1,7},{2,0},{3,1},{4,2},{5,3},{6,4},{7,5},{8,14},{9,15},{10,... | collective-permute-start | bytes 1572872 | tf_op jit(solution)/shard_map/ppermute | solution.py:34
  40.8 0.7 collective-permute-start.35
  41.5 5.8 %collective-permute-start.14 = (bf16[128,256]{1,0:T(8,128)(2,1)S(1)}, bf16[128,256]{1,0:T(8,128)(2,1)S(1)}, u32[]{:S(2)}, u32[]{:S(2)}) collective-permute-start(bf16[128,256]{1,0:T(8,128)(2,1)S(1)} %get-tuple-element.26.a0.query), channel_id=1, source_target_pairs={{0,64},{8,72},{16,80},{24,88},{32,96},{40,104},{48,112},{56,120},{... | collective-permute-start | bytes 196616 | tf_op jit(solution)/shard_map/ppermute | solution.py:22
  47.3 2.2 %collective-permute-done.14.a2 = bf16[128,256]{1,0:T(8,128)(2,1)S(1)} collective-permute-done((bf16[128,256]{1,0:T(8,128)(2,1)S(1)}, bf16[128,256]{1,0:T(8,128)(2,1)S(1)}, u32[]{:S(2)}, u32[]{:S(2)}) %collective-permute-start.14) | collective-permute-done | bytes 65568 | tf_op jit(solution)/shard_map/ppermute | solution.py:22
  49.6 2.1 %collective-permute-start.15 = (bf16[128,256]{1,0:T(8,128)(2,1)S(1)}, bf16[128,256]{1,0:T(8,128)(2,1)S(1)}, u32[]{:S(2)}, u32[]{:S(2)}) collective-permute-start(bf16[128,256]{1,0:T(8,128)(2,1)S(1)} %get-tuple-element.26.a0.query), channel_id=1, source_target_pairs={{0,96},{8,104},{16,112},{24,120},{32,0},{40,8},{48,16},{56,24},{64... | collective-permute-start | bytes 196616 | tf_op jit(solution)/shard_map/ppermute | solution.py:22
  51.6 2.2 %collective-permute-done.15.a3 = bf16[128,256]{1,0:T(8,128)(2,1)S(1)} collective-permute-done((bf16[128,256]{1,0:T(8,128)(2,1)S(1)}, bf16[128,256]{1,0:T(8,128)(2,1)S(1)}, u32[]{:S(2)}, u32[]{:S(2)}) %collective-permute-start.15) | collective-permute-done | bytes 65568 | tf_op jit(solution)/shard_map/ppermute | solution.py:22
  53.9 0.5 collective-permute-start.16
  54.3 15.1 %collective-permute-start.37 = (bf16[256,512]{1,0:T(8,128)(2,1)S(1)}, bf16[256,512]{1,0:T(8,128)(2,1)S(1)}, u32[]{:S(2)}, u32[]{:S(2)}) collective-permute-start(bf16[256,512]{1,0:T(8,128)(2,1)S(1)} %collective-permute-done.35.rest_0_), channel_id=1, source_target_pairs={{0,2},{1,3},{2,4},{3,5},{4,6},{5,7},{6,0},{7,1},{8,10},{9,11},{10,... | collective-permute-start | bytes 786440 | tf_op jit(solution)/shard_map/ppermute | solution.py:34
  69.5 11.4 %collective-permute-start.39 = (bf16[256,512]{1,0:T(8,128)(2,1)S(1)}, bf16[256,512]{1,0:T(8,128)(2,1)S(1)}, u32[]{:S(2)}, u32[]{:S(2)}) collective-permute-start(bf16[256,512]{1,0:T(8,128)(2,1)S(1)} %collective-permute-done.35.rest_0_), channel_id=1, source_target_pairs={{0,4},{1,5},{2,6},{3,7},{4,0},{5,1},{6,2},{7,3},{8,12},{9,13},{10,... | collective-permute-start | bytes 786440 | tf_op jit(solution)/shard_map/ppermute | solution.py:34
  80.8 4.4 %collective-permute-start.18 = (bf16[4,128,256]{2,1,0:T(8,128)(2,1)S(1)}, bf16[4,128,256]{2,1,0:T(8,128)(2,1)S(1)}, u32[]{:S(2)}, u32[]{:S(2)}) collective-permute-start(bf16[4,128,256]{2,1,0:T(8,128)(2,1)S(1)} %shard_map.142.refs_1_), channel_id=1, source_target_pairs={{0,16},{8,24},{16,0},{24,8},{32,48},{40,56},{48,32},{56,40},{64,80... | collective-permute-start | bytes 786440 | tf_op jit(solution)/shard_map/ppermute | solution.py:29
  85.2 1.5 shard_map.144
  86.7 0.7 collective-permute-start.17
  87.4 5.7 %collective-permute-start.41 = (bf16[256,512]{1,0:T(8,128)(2,1)S(1)}, bf16[256,512]{1,0:T(8,128)(2,1)S(1)}, u32[]{:S(2)}, u32[]{:S(2)}) collective-permute-start(bf16[256,512]{1,0:T(8,128)(2,1)S(1)} %collective-permute-done.35.rest_0_), channel_id=1, source_target_pairs={{0,6},{1,7},{2,0},{3,1},{4,2},{5,3},{6,4},{7,5},{8,14},{9,15},{10,... | collective-permute-start | bytes 786440 | tf_op jit(solution)/shard_map/ppermute | solution.py:34
  93.1 0.5 collective-permute-start.29
  93.6 3.8 %collective-permute-done.20.refs_1_ = bf16[4,128,256]{2,1,0:T(8,128)(2,1)S(1)} collective-permute-done((bf16[4,128,256]{2,1,0:T(8,128)(2,1)S(1)}, bf16[4,128,256]{2,1,0:T(8,128)(2,1)S(1)}, u32[]{:S(2)}, u32[]{:S(2)}) %collective-permute-start.20) | collective-permute-done | bytes 262176 | tf_op jit(solution)/shard_map/ppermute | solution.py:29
  97.4 1.5 shard_map.145
  98.9 1.5 shard_map.146
  100.3 0.7 collective-permute-start.19
  101.0 0.8 collective-permute-done.17.p1
  101.8 0.7 collective-permute-start.21
  102.5 8.9 %collective-permute-done.19.p2 = bf16[1072,128]{1,0:T(8,128)(2,1)S(1)} collective-permute-done((bf16[1072,128]{1,0:T(8,128)(2,1)S(1)}, bf16[1072,128]{1,0:T(8,128)(2,1)S(1)}, u32[]{:S(2)}, u32[]{:S(2)}) %collective-permute-start.19) | collective-permute-done | bytes 274464 | tf_op jit(solution)/shard_map/ppermute | solution.py:29
  111.4 5.4 %collective-permute-done.21.p3 = bf16[1072,128]{1,0:T(8,128)(2,1)S(1)} collective-permute-done((bf16[1072,128]{1,0:T(8,128)(2,1)S(1)}, bf16[1072,128]{1,0:T(8,128)(2,1)S(1)}, u32[]{:S(2)}, u32[]{:S(2)}) %collective-permute-start.21) | collective-permute-done | bytes 274464 | tf_op jit(solution)/shard_map/ppermute | solution.py:29
  116.8 1.4 shard_map.143.p0
  118.2 0.8 shard_map.147
  119.1 0.6 collective-permute-start.40
  119.7 0.1 collective-permute-start.42
  119.8 3.9 %collective-permute-done.22.p1 = bf16[272,128]{1,0:T(8,128)(2,1)S(1)} collective-permute-done((bf16[272,128]{1,0:T(8,128)(2,1)S(1)}, bf16[272,128]{1,0:T(8,128)(2,1)S(1)}, u32[]{:S(2)}, u32[]{:S(2)}) %collective-permute-start.22) | collective-permute-done | bytes 69664 | tf_op jit(solution)/shard_map/ppermute | solution.py:22
  123.7 5.8 %collective-permute-done.23.p2 = bf16[272,128]{1,0:T(8,128)(2,1)S(1)} collective-permute-done((bf16[272,128]{1,0:T(8,128)(2,1)S(1)}, bf16[272,128]{1,0:T(8,128)(2,1)S(1)}, u32[]{:S(2)}, u32[]{:S(2)}) %collective-permute-start.23) | collective-permute-done | bytes 69664 | tf_op jit(solution)/shard_map/ppermute | solution.py:22
  129.5 0.8 shard_map.148
  130.3 1.0 shard_map.149
  131.3 3.7 %collective-permute-done.24.p3 = bf16[272,128]{1,0:T(8,128)(2,1)S(1)} collective-permute-done((bf16[272,128]{1,0:T(8,128)(2,1)S(1)}, bf16[272,128]{1,0:T(8,128)(2,1)S(1)}, u32[]{:S(2)}, u32[]{:S(2)}) %collective-permute-start.24) | collective-permute-done | bytes 69664 | tf_op jit(solution)/shard_map/ppermute | solution.py:22
  135.0 0.4 shard_map.150.a0
  135.5 1.7 %collective-permute-start.33 = (bf16[128,256]{1,0:T(8,128)(2,1)S(1)}, bf16[128,256]{1,0:T(8,128)(2,1)S(1)}, u32[]{:S(2)}, u32[]{:S(2)}) collective-permute-start(bf16[128,256]{1,0:T(8,128)(2,1)S(1)} %shard_map.150.a0), channel_id=1, source_target_pairs={{0,64},{8,72},{16,80},{24,88},{32,96},{40,104},{48,112},{56,120},{... | collective-permute-start | bytes 196616 | tf_op jit(solution)/shard_map/ppermute | solution.py:22
  137.3 1.6 %collective-permute-start.34 = (bf16[128,256]{1,0:T(8,128)(2,1)S(1)}, bf16[128,256]{1,0:T(8,128)(2,1)S(1)}, u32[]{:S(2)}, u32[]{:S(2)}) collective-permute-start(bf16[128,256]{1,0:T(8,128)(2,1)S(1)} %shard_map.150.a0), channel_id=1, source_target_pairs={{0,96},{8,104},{16,112},{24,120},{32,0},{40,8},{48,16},{56,24},{64... | collective-permute-start | bytes 196616 | tf_op jit(solution)/shard_map/ppermute | solution.py:22
  138.8 2.9 %collective-permute-done.32.a1 = bf16[128,256]{1,0:T(8,128)(2,1)S(1)} collective-permute-done((bf16[128,256]{1,0:T(8,128)(2,1)S(1)}, bf16[128,256]{1,0:T(8,128)(2,1)S(1)}, u32[]{:S(2)}, u32[]{:S(2)}) %collective-permute-start.32) | collective-permute-done | bytes 65568 | tf_op jit(solution)/shard_map/ppermute | solution.py:22
  141.7 0.9 collective-permute-done.34.a3
  142.6 0.5 shard_map.151
  143.0 0.1 collective-permute-start.43
  143.1 3.2 %collective-permute-start.44 = (bf16[128,256]{1,0:T(8,128)(2,1)S(1)}, bf16[128,256]{1,0:T(8,128)(2,1)S(1)}, u32[]{:S(2)}, u32[]{:S(2)}) collective-permute-start(bf16[128,256]{1,0:T(8,128)(2,1)S(1)} %get-tuple-element.39), channel_id=1, source_target_pairs={{0,24},{8,0},{16,8},{24,16},{32,56},{40,32},{48,40},{56,48},{64,88... | collective-permute-start | bytes 196616 | tf_op jit(solution)/shard_map/ppermute | solution.py:29
  146.3 0.6 copy.15
  147.0 0.6 copy.16
  147.6 1.0 collective-permute-done.43.g1
  148.6 0.3 collective-permute-done.44.g2
  148.9 3.3 %collective-permute-done.45.g3 = bf16[128,256]{1,0:T(8,128)(2,1)S(1)} collective-permute-done((bf16[128,256]{1,0:T(8,128)(2,1)S(1)}, bf16[128,256]{1,0:T(8,128)(2,1)S(1)}, u32[]{:S(2)}, u32[]{:S(2)}) %collective-permute-start.45) | collective-permute-done | bytes 65568 | tf_op jit(solution)/shard_map/ppermute | solution.py:29
  152.1 0.7 shard_map.152
  (52 shorter events, 0.3 us)
Async XLA Ops:
  0.6 33.8 %copy-start.2 = (f32[4096]{0:T(1024)S(1)}, f32[4096]{0:T(1024)}, u32[]{:S(2)}) copy-start(f32[4096]{0:T(1024)} %param.16) | copy-start | bytes 49156
  0.6 40.2 %copy-start.3 = (bf16[256,512]{1,0:T(8,128)(2,1)S(1)}, bf16[256,512]{1,0:T(8,128)(2,1)}, u32[]{:S(2)}) copy-start(bf16[256,512]{1,0:T(8,128)(2,1)} %param.18) | copy-start | bytes 786436
  3.2 10.2 %collective-permute-start = (bf16[128,256]{1,0:T(8,128)(2,1)S(1)}, bf16[128,256]{1,0:T(8,128)(2,1)S(1)}, u32[]{:S(2)}, u32[]{:S(2)}) collective-permute-start(bf16[128,256]{1,0:T(8,128)(2,1)S(1)} %get-tuple-element.22.a0), channel_id=1, source_target_pairs={{0,32},{8,40},{16,48},{24,56},{32,64},{40,72},{48,80},{56,88},{64,... | collective-permute-start | bytes 196616 | tf_op jit(solution)/shard_map/ppermute | solution.py:22
  4.9 9.3 %collective-permute-start.1 = (bf16[128,256]{1,0:T(8,128)(2,1)S(1)}, bf16[128,256]{1,0:T(8,128)(2,1)S(1)}, u32[]{:S(2)}, u32[]{:S(2)}) collective-permute-start(bf16[128,256]{1,0:T(8,128)(2,1)S(1)} %get-tuple-element.22.a0), channel_id=1, source_target_pairs={{0,64},{8,72},{16,80},{24,88},{32,96},{40,104},{48,112},{56,120},{... | collective-permute-start | bytes 196616 | tf_op jit(solution)/shard_map/ppermute | solution.py:22
  7.8 6.4 %collective-permute-start.2 = (bf16[128,256]{1,0:T(8,128)(2,1)S(1)}, bf16[128,256]{1,0:T(8,128)(2,1)S(1)}, u32[]{:S(2)}, u32[]{:S(2)}) collective-permute-start(bf16[128,256]{1,0:T(8,128)(2,1)S(1)} %get-tuple-element.22.a0), channel_id=1, source_target_pairs={{0,96},{8,104},{16,112},{24,120},{32,0},{40,8},{48,16},{56,24},{64... | collective-permute-start | bytes 196616 | tf_op jit(solution)/shard_map/ppermute | solution.py:22
  9.2 76.1 %copy-start = (bf16[2,128,4096]{2,1,0:T(8,128)(2,1)S(1)}, bf16[2,128,4096]{2,1,0:T(8,128)(2,1)}, u32[]{:S(2)}) copy-start(bf16[2,128,4096]{2,1,0:T(8,128)(2,1)} %refs_2_.7) | copy-start | bytes 6291460
  9.2 76.1 %copy-start.1 = (bf16[2,128,4096]{2,1,0:T(8,128)(2,1)S(1)}, bf16[2,128,4096]{2,1,0:T(8,128)(2,1)}, u32[]{:S(2)}) copy-start(bf16[2,128,4096]{2,1,0:T(8,128)(2,1)} %refs_3_.7) | copy-start | bytes 6291460
  9.2 10.7 %collective-permute-start.9 = (bf16[512,256]{1,0:T(8,128)(2,1)S(1)}, bf16[512,256]{1,0:T(8,128)(2,1)S(1)}, u32[]{:S(2)}, u32[]{:S(2)}) collective-permute-start(bf16[512,256]{1,0:T(8,128)(2,1)S(1)} %get-tuple-element.25.rest_0_), channel_id=1, source_target_pairs={{0,4},{1,5},{2,6},{3,7},{4,0},{5,1},{6,2},{7,3},{8,12},{9,13},{10,... | collective-permute-start | bytes 786440 | tf_op jit(solution)/shard_map/ppermute | solution.py:34
  12.2 11.5 %collective-permute-start.11 = (bf16[512,256]{1,0:T(8,128)(2,1)S(1)}, bf16[512,256]{1,0:T(8,128)(2,1)S(1)}, u32[]{:S(2)}, u32[]{:S(2)}) collective-permute-start(bf16[512,256]{1,0:T(8,128)(2,1)S(1)} %get-tuple-element.25.rest_0_), channel_id=1, source_target_pairs={{0,6},{1,7},{2,0},{3,1},{4,2},{5,3},{6,4},{7,5},{8,14},{9,15},{10,... | collective-permute-start | bytes 786440 | tf_op jit(solution)/shard_map/ppermute | solution.py:34
  13.3 14.3 %collective-permute-start.7 = (bf16[512,256]{1,0:T(8,128)(2,1)S(1)}, bf16[512,256]{1,0:T(8,128)(2,1)S(1)}, u32[]{:S(2)}, u32[]{:S(2)}) collective-permute-start(bf16[512,256]{1,0:T(8,128)(2,1)S(1)} %get-tuple-element.25.rest_0_), channel_id=1, source_target_pairs={{0,2},{1,3},{2,4},{3,5},{4,6},{5,7},{6,0},{7,1},{8,10},{9,11},{10,... | collective-permute-start | bytes 786440 | tf_op jit(solution)/shard_map/ppermute | solution.py:34
  14.2 13.4 %collective-permute-start.6 = (bf16[512,256]{1,0:T(8,128)(2,1)S(1)}, bf16[512,256]{1,0:T(8,128)(2,1)S(1)}, u32[]{:S(2)}, u32[]{:S(2)}) collective-permute-start(bf16[512,256]{1,0:T(8,128)(2,1)S(1)} %get-tuple-element.25.rest_0_), channel_id=1, source_target_pairs={{0,1},{1,0},{2,3},{3,2},{4,5},{5,4},{6,7},{7,6},{8,9},{9,8},{10,11... | collective-permute-start | bytes 786440 | tf_op jit(solution)/shard_map/ppermute | solution.py:38
  14.3 13.9 %collective-permute-start.3 = (bf16[4,128,256]{2,1,0:T(8,128)(2,1)S(1)}, bf16[4,128,256]{2,1,0:T(8,128)(2,1)S(1)}, u32[]{:S(2)}, u32[]{:S(2)}) collective-permute-start(bf16[4,128,256]{2,1,0:T(8,128)(2,1)S(1)} %shard_map.140.s0), channel_id=1, source_target_pairs={{0,8},{8,16},{16,24},{24,0},{32,40},{40,48},{48,56},{56,32},{64,72... | collective-permute-start | bytes 786440 | tf_op jit(solution)/shard_map/ppermute | solution.py:29
  19.8 12.3 %collective-permute-start.4 = (bf16[4,128,256]{2,1,0:T(8,128)(2,1)S(1)}, bf16[4,128,256]{2,1,0:T(8,128)(2,1)S(1)}, u32[]{:S(2)}, u32[]{:S(2)}) collective-permute-start(bf16[4,128,256]{2,1,0:T(8,128)(2,1)S(1)} %shard_map.140.s0), channel_id=1, source_target_pairs={{0,16},{8,24},{16,0},{24,8},{32,48},{40,56},{48,32},{56,40},{64,80... | collective-permute-start | bytes 786440 | tf_op jit(solution)/shard_map/ppermute | solution.py:29
  23.7 10.7 %collective-permute-start.5 = (bf16[4,128,256]{2,1,0:T(8,128)(2,1)S(1)}, bf16[4,128,256]{2,1,0:T(8,128)(2,1)S(1)}, u32[]{:S(2)}, u32[]{:S(2)}) collective-permute-start(bf16[4,128,256]{2,1,0:T(8,128)(2,1)S(1)} %shard_map.140.s0), channel_id=1, source_target_pairs={{0,24},{8,0},{16,8},{24,16},{32,56},{40,32},{48,40},{56,48},{64,88... | collective-permute-start | bytes 786440 | tf_op jit(solution)/shard_map/ppermute | solution.py:29
  27.7 6.8 %collective-permute-start.10 = (bf16[512,256]{1,0:T(8,128)(2,1)S(1)}, bf16[512,256]{1,0:T(8,128)(2,1)S(1)}, u32[]{:S(2)}, u32[]{:S(2)}) collective-permute-start(bf16[512,256]{1,0:T(8,128)(2,1)S(1)} %collective-permute-done.9.rest_4_), channel_id=1, source_target_pairs={{0,1},{1,0},{2,3},{3,2},{4,5},{5,4},{6,7},{7,6},{8,9},{9,8},{10,11... | collective-permute-start | bytes 786440 | tf_op jit(solution)/shard_map/ppermute | solution.py:38
  27.7 6.8 %collective-permute-start.12 = (bf16[512,256]{1,0:T(8,128)(2,1)S(1)}, bf16[512,256]{1,0:T(8,128)(2,1)S(1)}, u32[]{:S(2)}, u32[]{:S(2)}) collective-permute-start(bf16[512,256]{1,0:T(8,128)(2,1)S(1)} %collective-permute-done.11.rest_6_), channel_id=1, source_target_pairs={{0,1},{1,0},{2,3},{3,2},{4,5},{5,4},{6,7},{7,6},{8,9},{9,8},{10,11... | collective-permute-start | bytes 786440 | tf_op jit(solution)/shard_map/ppermute | solution.py:38
  28.2 6.2 %collective-permute-start.8 = (bf16[512,256]{1,0:T(8,128)(2,1)S(1)}, bf16[512,256]{1,0:T(8,128)(2,1)S(1)}, u32[]{:S(2)}, u32[]{:S(2)}) collective-permute-start(bf16[512,256]{1,0:T(8,128)(2,1)S(1)} %collective-permute-done.7.rest_2_), channel_id=1, source_target_pairs={{0,1},{1,0},{2,3},{3,2},{4,5},{5,4},{6,7},{7,6},{8,9},{9,8},{10,11... | collective-permute-start | bytes 786440 | tf_op jit(solution)/shard_map/ppermute | solution.py:38
  32.1 22.2 %collective-permute-start.26 = (bf16[2,512,256]{2,1,0:T(8,128)(2,1)S(1)}, bf16[2,512,256]{2,1,0:T(8,128)(2,1)S(1)}, u32[]{:S(2)}, u32[]{:S(2)}) collective-permute-start(bf16[2,512,256]{2,1,0:T(8,128)(2,1)S(1)} %get-tuple-element.32.rest_0_), channel_id=1, source_target_pairs={{0,2},{1,3},{2,4},{3,5},{4,6},{5,7},{6,0},{7,1},{8,10},{9,11},{10,... | collective-permute-start | bytes 1572872 | tf_op jit(solution)/shard_map/ppermute | solution.py:34
  35.4 6.1 %collective-permute-start.13 = (bf16[128,256]{1,0:T(8,128)(2,1)S(1)}, bf16[128,256]{1,0:T(8,128)(2,1)S(1)}, u32[]{:S(2)}, u32[]{:S(2)}) collective-permute-start(bf16[128,256]{1,0:T(8,128)(2,1)S(1)} %get-tuple-element.26.a0.query), channel_id=1, source_target_pairs={{0,32},{8,40},{16,48},{24,56},{32,64},{40,72},{48,80},{56,88},{64,... | collective-permute-start | bytes 196616 | tf_op jit(solution)/shard_map/ppermute | solution.py:22
  36.2 33.3 %collective-permute-start.28 = (bf16[2,512,256]{2,1,0:T(8,128)(2,1)S(1)}, bf16[2,512,256]{2,1,0:T(8,128)(2,1)S(1)}, u32[]{:S(2)}, u32[]{:S(2)}) collective-permute-start(bf16[2,512,256]{2,1,0:T(8,128)(2,1)S(1)} %get-tuple-element.32.rest_0_), channel_id=1, source_target_pairs={{0,4},{1,5},{2,6},{3,7},{4,0},{5,1},{6,2},{7,3},{8,12},{9,13},{10,... | collective-permute-start | bytes 1572872 | tf_op jit(solution)/shard_map/ppermute | solution.py:34
  38.7 42.1 %collective-permute-start.30 = (bf16[2,512,256]{2,1,0:T(8,128)(2,1)S(1)}, bf16[2,512,256]{2,1,0:T(8,128)(2,1)S(1)}, u32[]{:S(2)}, u32[]{:S(2)}) collective-permute-start(bf16[2,512,256]{2,1,0:T(8,128)(2,1)S(1)} %get-tuple-element.32.rest_0_), channel_id=1, source_target_pairs={{0,6},{1,7},{2,0},{3,1},{4,2},{5,3},{6,4},{7,5},{8,14},{9,15},{10,... | collective-permute-start | bytes 1572872 | tf_op jit(solution)/shard_map/ppermute | solution.py:34
  40.8 13.0 %collective-permute-start.35 = (bf16[256,512]{1,0:T(8,128)(2,1)S(1)}, bf16[256,512]{1,0:T(8,128)(2,1)S(1)}, u32[]{:S(2)}, u32[]{:S(2)}) collective-permute-start(bf16[256,512]{1,0:T(8,128)(2,1)S(1)} %copy-done.3), channel_id=1, source_target_pairs={{0,0},{1,1},{8,8},{9,9},{16,16},{17,17},{24,24},{25,25},{32,2},{33... | collective-permute-start | bytes 786440 | tf_op jit(solution)/shard_map/ppermute | solution.py:52
  41.5 8.1 %collective-permute-start.14 = (bf16[128,256]{1,0:T(8,128)(2,1)S(1)}, bf16[128,256]{1,0:T(8,128)(2,1)S(1)}, u32[]{:S(2)}, u32[]{:S(2)}) collective-permute-start(bf16[128,256]{1,0:T(8,128)(2,1)S(1)} %get-tuple-element.26.a0.query), channel_id=1, source_target_pairs={{0,64},{8,72},{16,80},{24,88},{32,96},{40,104},{48,112},{56,120},{... | collective-permute-start | bytes 196616 | tf_op jit(solution)/shard_map/ppermute | solution.py:22
  49.6 4.3 %collective-permute-start.15 = (bf16[128,256]{1,0:T(8,128)(2,1)S(1)}, bf16[128,256]{1,0:T(8,128)(2,1)S(1)}, u32[]{:S(2)}, u32[]{:S(2)}) collective-permute-start(bf16[128,256]{1,0:T(8,128)(2,1)S(1)} %get-tuple-element.26.a0.query), channel_id=1, source_target_pairs={{0,96},{8,104},{16,112},{24,120},{32,0},{40,8},{48,16},{56,24},{64... | collective-permute-start | bytes 196616 | tf_op jit(solution)/shard_map/ppermute | solution.py:22
  53.8 32.9 %collective-permute-start.25 = (bf16[2,512,256]{2,1,0:T(8,128)(2,1)S(1)}, bf16[2,512,256]{2,1,0:T(8,128)(2,1)S(1)}, u32[]{:S(2)}, u32[]{:S(2)}) collective-permute-start(bf16[2,512,256]{2,1,0:T(8,128)(2,1)S(1)} %get-tuple-element.32.rest_0_), channel_id=1, source_target_pairs={{0,1},{1,0},{2,3},{3,2},{4,5},{5,4},{6,7},{7,6},{8,9},{9,8},{10,11... | collective-permute-start | bytes 1572872 | tf_op jit(solution)/shard_map/ppermute | solution.py:38
  53.9 31.4 %collective-permute-start.16 = (bf16[4,128,256]{2,1,0:T(8,128)(2,1)S(1)}, bf16[4,128,256]{2,1,0:T(8,128)(2,1)S(1)}, u32[]{:S(2)}, u32[]{:S(2)}) collective-permute-start(bf16[4,128,256]{2,1,0:T(8,128)(2,1)S(1)} %shard_map.142.refs_1_), channel_id=1, source_target_pairs={{0,8},{8,16},{16,24},{24,0},{32,40},{40,48},{48,56},{56,32},{64,72... | collective-permute-start | bytes 786440 | tf_op jit(solution)/shard_map/ppermute | solution.py:29
  54.3 33.1 %collective-permute-start.37 = (bf16[256,512]{1,0:T(8,128)(2,1)S(1)}, bf16[256,512]{1,0:T(8,128)(2,1)S(1)}, u32[]{:S(2)}, u32[]{:S(2)}) collective-permute-start(bf16[256,512]{1,0:T(8,128)(2,1)S(1)} %collective-permute-done.35.rest_0_), channel_id=1, source_target_pairs={{0,2},{1,3},{2,4},{3,5},{4,6},{5,7},{6,0},{7,1},{8,10},{9,11},{10,... | collective-permute-start | bytes 786440 | tf_op jit(solution)/shard_map/ppermute | solution.py:34
  69.5 23.6 %collective-permute-start.39 = (bf16[256,512]{1,0:T(8,128)(2,1)S(1)}, bf16[256,512]{1,0:T(8,128)(2,1)S(1)}, u32[]{:S(2)}, u32[]{:S(2)}) collective-permute-start(bf16[256,512]{1,0:T(8,128)(2,1)S(1)} %collective-permute-done.35.rest_0_), channel_id=1, source_target_pairs={{0,4},{1,5},{2,6},{3,7},{4,0},{5,1},{6,2},{7,3},{8,12},{9,13},{10,... | collective-permute-start | bytes 786440 | tf_op jit(solution)/shard_map/ppermute | solution.py:34
  80.8 12.2 %collective-permute-start.18 = (bf16[4,128,256]{2,1,0:T(8,128)(2,1)S(1)}, bf16[4,128,256]{2,1,0:T(8,128)(2,1)S(1)}, u32[]{:S(2)}, u32[]{:S(2)}) collective-permute-start(bf16[4,128,256]{2,1,0:T(8,128)(2,1)S(1)} %shard_map.142.refs_1_), channel_id=1, source_target_pairs={{0,16},{8,24},{16,0},{24,8},{32,48},{40,56},{48,32},{56,40},{64,80... | collective-permute-start | bytes 786440 | tf_op jit(solution)/shard_map/ppermute | solution.py:29
  85.2 12.2 %collective-permute-start.20 = (bf16[4,128,256]{2,1,0:T(8,128)(2,1)S(1)}, bf16[4,128,256]{2,1,0:T(8,128)(2,1)S(1)}, u32[]{:S(2)}, u32[]{:S(2)}) collective-permute-start(bf16[4,128,256]{2,1,0:T(8,128)(2,1)S(1)} %shard_map.142.refs_1_), channel_id=1, source_target_pairs={{0,24},{8,0},{16,8},{24,16},{32,56},{40,32},{48,40},{56,48},{64,88... | collective-permute-start | bytes 786440 | tf_op jit(solution)/shard_map/ppermute | solution.py:29
  86.7 15.1 %collective-permute-start.17 = (bf16[1072,128]{1,0:T(8,128)(2,1)S(1)}, bf16[1072,128]{1,0:T(8,128)(2,1)S(1)}, u32[]{:S(2)}, u32[]{:S(2)}) collective-permute-start(bf16[1072,128]{1,0:T(8,128)(2,1)S(1)} %shard_map.144), channel_id=1, source_target_pairs={{0,24},{8,0},{16,8},{24,16},{32,56},{40,32},{48,40},{56,48},{64,88... | collective-permute-start | bytes 823304 | tf_op jit(solution)/shard_map/ppermute | solution.py:29
  87.4 13.0 %collective-permute-start.41 = (bf16[256,512]{1,0:T(8,128)(2,1)S(1)}, bf16[256,512]{1,0:T(8,128)(2,1)S(1)}, u32[]{:S(2)}, u32[]{:S(2)}) collective-permute-start(bf16[256,512]{1,0:T(8,128)(2,1)S(1)} %collective-permute-done.35.rest_0_), channel_id=1, source_target_pairs={{0,6},{1,7},{2,0},{3,1},{4,2},{5,3},{6,4},{7,5},{8,14},{9,15},{10,... | collective-permute-start | bytes 786440 | tf_op jit(solution)/shard_map/ppermute | solution.py:34
  93.1 26.0 %collective-permute-start.27 = (bf16[2,512,256]{2,1,0:T(8,128)(2,1)S(1)}, bf16[2,512,256]{2,1,0:T(8,128)(2,1)S(1)}, u32[]{:S(2)}, u32[]{:S(2)}) collective-permute-start(bf16[2,512,256]{2,1,0:T(8,128)(2,1)S(1)} %collective-permute-done.26.rest_2_), channel_id=1, source_target_pairs={{0,1},{1,0},{2,3},{3,2},{4,5},{5,4},{6,7},{7,6},{8,9},{9,8},{10,11... | collective-permute-start | bytes 1572872 | tf_op jit(solution)/shard_map/ppermute | solution.py:38
  93.1 26.1 %collective-permute-start.29 = (bf16[2,512,256]{2,1,0:T(8,128)(2,1)S(1)}, bf16[2,512,256]{2,1,0:T(8,128)(2,1)S(1)}, u32[]{:S(2)}, u32[]{:S(2)}) collective-permute-start(bf16[2,512,256]{2,1,0:T(8,128)(2,1)S(1)} %collective-permute-done.28.rest_4_), channel_id=1, source_target_pairs={{0,1},{1,0},{2,3},{3,2},{4,5},{5,4},{6,7},{7,6},{8,9},{9,8},{10,11... | collective-permute-start | bytes 1572872 | tf_op jit(solution)/shard_map/ppermute | solution.py:38
  97.4 22.3 %collective-permute-start.31 = (bf16[2,512,256]{2,1,0:T(8,128)(2,1)S(1)}, bf16[2,512,256]{2,1,0:T(8,128)(2,1)S(1)}, u32[]{:S(2)}, u32[]{:S(2)}) collective-permute-start(bf16[2,512,256]{2,1,0:T(8,128)(2,1)S(1)} %collective-permute-done.30.rest_6_), channel_id=1, source_target_pairs={{0,1},{1,0},{2,3},{3,2},{4,5},{5,4},{6,7},{7,6},{8,9},{9,8},{10,11... | collective-permute-start | bytes 1572872 | tf_op jit(solution)/shard_map/ppermute | solution.py:38
  100.3 11.1 %collective-permute-start.19 = (bf16[1072,128]{1,0:T(8,128)(2,1)S(1)}, bf16[1072,128]{1,0:T(8,128)(2,1)S(1)}, u32[]{:S(2)}, u32[]{:S(2)}) collective-permute-start(bf16[1072,128]{1,0:T(8,128)(2,1)S(1)} %shard_map.145), channel_id=1, source_target_pairs={{0,16},{8,24},{16,0},{24,8},{32,48},{40,56},{48,32},{56,40},{64,80... | collective-permute-start | bytes 823304 | tf_op jit(solution)/shard_map/ppermute | solution.py:29
  101.8 15.0 %collective-permute-start.21 = (bf16[1072,128]{1,0:T(8,128)(2,1)S(1)}, bf16[1072,128]{1,0:T(8,128)(2,1)S(1)}, u32[]{:S(2)}, u32[]{:S(2)}) collective-permute-start(bf16[1072,128]{1,0:T(8,128)(2,1)S(1)} %shard_map.146), channel_id=1, source_target_pairs={{0,8},{8,16},{16,24},{24,0},{32,40},{40,48},{48,56},{56,32},{64,72... | collective-permute-start | bytes 823304 | tf_op jit(solution)/shard_map/ppermute | solution.py:29
  111.4 24.1 %collective-permute-start.36 = (bf16[256,512]{1,0:T(8,128)(2,1)S(1)}, bf16[256,512]{1,0:T(8,128)(2,1)S(1)}, u32[]{:S(2)}, u32[]{:S(2)}) collective-permute-start(bf16[256,512]{1,0:T(8,128)(2,1)S(1)} %collective-permute-done.35.rest_0_), channel_id=1, source_target_pairs={{0,1},{1,0},{2,3},{3,2},{4,5},{5,4},{6,7},{7,6},{8,9},{9,8},{10,11... | collective-permute-start | bytes 786440 | tf_op jit(solution)/shard_map/ppermute | solution.py:38
  116.8 20.5 %collective-permute-start.38 = (bf16[256,512]{1,0:T(8,128)(2,1)S(1)}, bf16[256,512]{1,0:T(8,128)(2,1)S(1)}, u32[]{:S(2)}, u32[]{:S(2)}) collective-permute-start(bf16[256,512]{1,0:T(8,128)(2,1)S(1)} %collective-permute-done.37.rest_2_), channel_id=1, source_target_pairs={{0,1},{1,0},{2,3},{3,2},{4,5},{5,4},{6,7},{7,6},{8,9},{9,8},{10,11... | collective-permute-start | bytes 786440 | tf_op jit(solution)/shard_map/ppermute | solution.py:38
  119.1 4.6 %collective-permute-start.22 = (bf16[272,128]{1,0:T(8,128)(2,1)S(1)}, bf16[272,128]{1,0:T(8,128)(2,1)S(1)}, u32[]{:S(2)}, u32[]{:S(2)}) collective-permute-start(bf16[272,128]{1,0:T(8,128)(2,1)S(1)} %get-tuple-element.28), channel_id=1, source_target_pairs={{0,96},{8,104},{16,112},{24,120},{32,0},{40,8},{48,16},{56,24},{64... | collective-permute-start | bytes 208904 | tf_op jit(solution)/shard_map/ppermute | solution.py:22
  119.1 19.7 %collective-permute-start.40 = (bf16[256,512]{1,0:T(8,128)(2,1)S(1)}, bf16[256,512]{1,0:T(8,128)(2,1)S(1)}, u32[]{:S(2)}, u32[]{:S(2)}) collective-permute-start(bf16[256,512]{1,0:T(8,128)(2,1)S(1)} %collective-permute-done.39.rest_4_), channel_id=1, source_target_pairs={{0,1},{1,0},{2,3},{3,2},{4,5},{5,4},{6,7},{7,6},{8,9},{9,8},{10,11... | collective-permute-start | bytes 786440 | tf_op jit(solution)/shard_map/ppermute | solution.py:38
  119.7 19.1 %collective-permute-start.42 = (bf16[256,512]{1,0:T(8,128)(2,1)S(1)}, bf16[256,512]{1,0:T(8,128)(2,1)S(1)}, u32[]{:S(2)}, u32[]{:S(2)}) collective-permute-start(bf16[256,512]{1,0:T(8,128)(2,1)S(1)} %collective-permute-done.41.rest_6_), channel_id=1, source_target_pairs={{0,1},{1,0},{2,3},{3,2},{4,5},{5,4},{6,7},{7,6},{8,9},{9,8},{10,11... | collective-permute-start | bytes 786440 | tf_op jit(solution)/shard_map/ppermute | solution.py:38
  123.7 5.8 %collective-permute-start.23 = (bf16[272,128]{1,0:T(8,128)(2,1)S(1)}, bf16[272,128]{1,0:T(8,128)(2,1)S(1)}, u32[]{:S(2)}, u32[]{:S(2)}) collective-permute-start(bf16[272,128]{1,0:T(8,128)(2,1)S(1)} %get-tuple-element.29), channel_id=1, source_target_pairs={{0,64},{8,72},{16,80},{24,88},{32,96},{40,104},{48,112},{56,120},{... | collective-permute-start | bytes 208904 | tf_op jit(solution)/shard_map/ppermute | solution.py:22
  129.5 5.5 %collective-permute-start.24 = (bf16[272,128]{1,0:T(8,128)(2,1)S(1)}, bf16[272,128]{1,0:T(8,128)(2,1)S(1)}, u32[]{:S(2)}, u32[]{:S(2)}) collective-permute-start(bf16[272,128]{1,0:T(8,128)(2,1)S(1)} %get-tuple-element.30), channel_id=1, source_target_pairs={{0,32},{8,40},{16,48},{24,56},{32,64},{40,72},{48,80},{56,88},{64,... | collective-permute-start | bytes 208904 | tf_op jit(solution)/shard_map/ppermute | solution.py:22
  135.4 6.2 %collective-permute-start.32 = (bf16[128,256]{1,0:T(8,128)(2,1)S(1)}, bf16[128,256]{1,0:T(8,128)(2,1)S(1)}, u32[]{:S(2)}, u32[]{:S(2)}) collective-permute-start(bf16[128,256]{1,0:T(8,128)(2,1)S(1)} %shard_map.150.a0), channel_id=1, source_target_pairs={{0,32},{8,40},{16,48},{24,56},{32,64},{40,72},{48,80},{56,88},{64,... | collective-permute-start | bytes 196616 | tf_op jit(solution)/shard_map/ppermute | solution.py:22
  135.5 6.2 %collective-permute-start.33 = (bf16[128,256]{1,0:T(8,128)(2,1)S(1)}, bf16[128,256]{1,0:T(8,128)(2,1)S(1)}, u32[]{:S(2)}, u32[]{:S(2)}) collective-permute-start(bf16[128,256]{1,0:T(8,128)(2,1)S(1)} %shard_map.150.a0), channel_id=1, source_target_pairs={{0,64},{8,72},{16,80},{24,88},{32,96},{40,104},{48,112},{56,120},{... | collective-permute-start | bytes 196616 | tf_op jit(solution)/shard_map/ppermute | solution.py:22
  137.3 5.3 %collective-permute-start.34 = (bf16[128,256]{1,0:T(8,128)(2,1)S(1)}, bf16[128,256]{1,0:T(8,128)(2,1)S(1)}, u32[]{:S(2)}, u32[]{:S(2)}) collective-permute-start(bf16[128,256]{1,0:T(8,128)(2,1)S(1)} %shard_map.150.a0), channel_id=1, source_target_pairs={{0,96},{8,104},{16,112},{24,120},{32,0},{40,8},{48,16},{56,24},{64... | collective-permute-start | bytes 196616 | tf_op jit(solution)/shard_map/ppermute | solution.py:22
  143.0 5.5 %collective-permute-start.43 = (bf16[128,256]{1,0:T(8,128)(2,1)S(1)}, bf16[128,256]{1,0:T(8,128)(2,1)S(1)}, u32[]{:S(2)}, u32[]{:S(2)}) collective-permute-start(bf16[128,256]{1,0:T(8,128)(2,1)S(1)} %get-tuple-element.38), channel_id=1, source_target_pairs={{0,8},{8,16},{16,24},{24,0},{32,40},{40,48},{48,56},{56,32},{64,72... | collective-permute-start | bytes 196616 | tf_op jit(solution)/shard_map/ppermute | solution.py:29
  143.1 5.7 %collective-permute-start.44 = (bf16[128,256]{1,0:T(8,128)(2,1)S(1)}, bf16[128,256]{1,0:T(8,128)(2,1)S(1)}, u32[]{:S(2)}, u32[]{:S(2)}) collective-permute-start(bf16[128,256]{1,0:T(8,128)(2,1)S(1)} %get-tuple-element.39), channel_id=1, source_target_pairs={{0,24},{8,0},{16,8},{24,16},{32,56},{40,32},{48,40},{56,48},{64,88... | collective-permute-start | bytes 196616 | tf_op jit(solution)/shard_map/ppermute | solution.py:29
  146.3 5.8 %collective-permute-start.45 = (bf16[128,256]{1,0:T(8,128)(2,1)S(1)}, bf16[128,256]{1,0:T(8,128)(2,1)S(1)}, u32[]{:S(2)}, u32[]{:S(2)}) collective-permute-start(bf16[128,256]{1,0:T(8,128)(2,1)S(1)} %get-tuple-element.40), channel_id=1, source_target_pairs={{0,16},{8,24},{16,0},{24,8},{32,48},{40,56},{48,32},{56,40},{64,80... | collective-permute-start | bytes 196616 | tf_op jit(solution)/shard_map/ppermute | solution.py:29

commit v3 on v2

--- a/solution.py
+++ b/solution.py
@@ -486,7 +486,10 @@
         )
 
     own = history(0)
-    back = {j: z_shift(history(j), -j) for j in ORDER}
+    back = {}
+    for j in ORDER:
+        part = history(j)
+        back[j] = z_shift(part, -j)
     block = near((2 * rows + 16, HEAD), bf16)
     mixed = kernel_call(
         row_mix_body,

time: 153 us -> 153 us (level)
  no operation moved by 1% of the time
where the time goes in v3:
time: 153 us
  starting transfers between devices  83 us (54%)
  waiting for transfers between devices  54.2 us (35%)
  Pallas kernels  13.5 us (9%)
    ppermute x9, starting transfers between devices, x_shift(): return lax.ppermute(x, 'wt', pairs)  42.5 us
    ppermute x12, waiting for transfers between devices, z_shift(): return lax.ppermute(x, 'ctx', pairs)  29 us
    ppermute x12, waiting for transfers between devices, y_shift(): return lax.ppermute(x, 'ctx', pairs)  21.6 us
    ppermute x12, starting transfers between devices, z_shift(): return lax.ppermute(x, 'ctx', pairs)  20 us
    ppermute x12, starting transfers between devices, y_shift(): return lax.ppermute(x, 'ctx', pairs)  18.1 us
    pallas_call x14, Pallas kernels, kernel_call(): pl.pallas_call(body, in_specs=[s for s, _ in ins], out_specs=VMEM if sing...  13.5 us
    ppermute x9, waiting for transfers between devices, x_shift(): return lax.ppermute(x, 'wt', pairs)  3.62 us
  transfers between devices with their start and end apart: 46, of which 17 were waited for; matrix products, arithmetic and copies ran while one was open for 1% of the time, Pallas kernels for 6%

profile of v3, /device:TPU:0, one launch (start us, length us, event | category | flops | bytes accessed | tf_op | source)
XLA Modules:
  0.0 152.8 jit_solution(4165068726469625689)
XLA Ops:
  0.7 2.5 %shard_map.139 = (bf16[128,256]{1,0:T(8,128)(2,1)S(1)}, bf16[512,256]{1,0:T(8,128)(2,1)S(1)}, bf16[2,512,256]{2,1,0:T(8,128)(2,1)S(1)}, f32[128,128]{1,0:T(8,128)S(1)}, f32[128,128]{1,0:T(8,128)S(1)}) custom-call(s32[8]{0:T(128)} %source.1, s32[2]{0:T(128)} %refs_0_.7, bf16[128,1280]{1,0:T(8,128)(2,1)} %frames.1, bf16[1280,256]{1,0:T(8,128)(2,1)} %weight.1, ...), custom_call_target="tpu_custom_call" | custom-call | tf_op jit(solution)/shard_map/pallas_call | solution.py:93
  3.2 1.8 %collective-permute-start = (bf16[128,256]{1,0:T(8,128)(2,1)S(1)}, bf16[128,256]{1,0:T(8,128)(2,1)S(1)}, u32[]{:S(2)}, u32[]{:S(2)}) collective-permute-start(bf16[128,256]{1,0:T(8,128)(2,1)S(1)} %get-tuple-element.22.a0), channel_id=1, source_target_pairs={{0,32},{8,40},{16,48},{24,56},{32,64},{40,72},{48,80},{56,88},{64,... | collective-permute-start | bytes 196616 | tf_op jit(solution)/shard_map/ppermute | solution.py:22
  4.9 2.9 %collective-permute-start.1 = (bf16[128,256]{1,0:T(8,128)(2,1)S(1)}, bf16[128,256]{1,0:T(8,128)(2,1)S(1)}, u32[]{:S(2)}, u32[]{:S(2)}) collective-permute-start(bf16[128,256]{1,0:T(8,128)(2,1)S(1)} %get-tuple-element.22.a0), channel_id=1, source_target_pairs={{0,64},{8,72},{16,80},{24,88},{32,96},{40,104},{48,112},{56,120},{... | collective-permute-start | bytes 196616 | tf_op jit(solution)/shard_map/ppermute | solution.py:22
  7.8 1.3 collective-permute-start.2
  9.2 3.0 %collective-permute-start.9 = (bf16[512,256]{1,0:T(8,128)(2,1)S(1)}, bf16[512,256]{1,0:T(8,128)(2,1)S(1)}, u32[]{:S(2)}, u32[]{:S(2)}) collective-permute-start(bf16[512,256]{1,0:T(8,128)(2,1)S(1)} %get-tuple-element.25.rest_0_), channel_id=1, source_target_pairs={{0,4},{1,5},{2,6},{3,7},{4,0},{5,1},{6,2},{7,3},{8,12},{9,13},{10,... | collective-permute-start | bytes 786440 | tf_op jit(solution)/shard_map/ppermute | solution.py:34
  12.2 1.1 collective-permute-start.11
  13.3 0.9 collective-permute-start.7
  14.3 2.0 %collective-permute-start.3 = (bf16[4,128,256]{2,1,0:T(8,128)(2,1)S(1)}, bf16[4,128,256]{2,1,0:T(8,128)(2,1)S(1)}, u32[]{:S(2)}, u32[]{:S(2)}) collective-permute-start(bf16[4,128,256]{2,1,0:T(8,128)(2,1)S(1)} %shard_map.140.s0), channel_id=1, source_target_pairs={{0,8},{8,16},{16,24},{24,0},{32,40},{40,48},{48,56},{56,32},{64,72... | collective-permute-start | bytes 786440 | tf_op jit(solution)/shard_map/ppermute | solution.py:29
  16.2 3.6 %collective-permute-done.9.rest_4_ = bf16[512,256]{1,0:T(8,128)(2,1)S(1)} collective-permute-done((bf16[512,256]{1,0:T(8,128)(2,1)S(1)}, bf16[512,256]{1,0:T(8,128)(2,1)S(1)}, u32[]{:S(2)}, u32[]{:S(2)}) %collective-permute-start.9) | collective-permute-done | bytes 262176 | tf_op jit(solution)/shard_map/ppermute | solution.py:34
  19.8 3.9 %collective-permute-start.4 = (bf16[4,128,256]{2,1,0:T(8,128)(2,1)S(1)}, bf16[4,128,256]{2,1,0:T(8,128)(2,1)S(1)}, u32[]{:S(2)}, u32[]{:S(2)}) collective-permute-start(bf16[4,128,256]{2,1,0:T(8,128)(2,1)S(1)} %shard_map.140.s0), channel_id=1, source_target_pairs={{0,16},{8,24},{16,0},{24,8},{32,48},{40,56},{48,32},{56,40},{64,80... | collective-permute-start | bytes 786440 | tf_op jit(solution)/shard_map/ppermute | solution.py:29
  23.7 3.9 %collective-permute-start.5 = (bf16[4,128,256]{2,1,0:T(8,128)(2,1)S(1)}, bf16[4,128,256]{2,1,0:T(8,128)(2,1)S(1)}, u32[]{:S(2)}, u32[]{:S(2)}) collective-permute-start(bf16[4,128,256]{2,1,0:T(8,128)(2,1)S(1)} %shard_map.140.s0), channel_id=1, source_target_pairs={{0,24},{8,0},{16,8},{24,16},{32,56},{40,32},{48,40},{56,48},{64,88... | collective-permute-start | bytes 786440 | tf_op jit(solution)/shard_map/ppermute | solution.py:29
  27.7 0.5 collective-permute-start.12
  28.2 0.1 collective-permute-start.8
  28.3 3.9 %collective-permute-done.4.s2 = bf16[4,128,256]{2,1,0:T(8,128)(2,1)S(1)} collective-permute-done((bf16[4,128,256]{2,1,0:T(8,128)(2,1)S(1)}, bf16[4,128,256]{2,1,0:T(8,128)(2,1)S(1)}, u32[]{:S(2)}, u32[]{:S(2)}) %collective-permute-start.4) | collective-permute-done | bytes 262176 | tf_op jit(solution)/shard_map/ppermute | solution.py:29
  32.1 0.6 collective-permute-start.26
  32.7 1.7 %collective-permute-done.5.s3 = bf16[4,128,256]{2,1,0:T(8,128)(2,1)S(1)} collective-permute-done((bf16[4,128,256]{2,1,0:T(8,128)(2,1)S(1)}, bf16[4,128,256]{2,1,0:T(8,128)(2,1)S(1)}, u32[]{:S(2)}, u32[]{:S(2)}) %collective-permute-start.5) | collective-permute-done | bytes 262176 | tf_op jit(solution)/shard_map/ppermute | solution.py:29
  34.4 1.0 shard_map.141
  35.4 0.7 collective-permute-start.13
  36.2 2.5 %collective-permute-start.28 = (bf16[2,512,256]{2,1,0:T(8,128)(2,1)S(1)}, bf16[2,512,256]{2,1,0:T(8,128)(2,1)S(1)}, u32[]{:S(2)}, u32[]{:S(2)}) collective-permute-start(bf16[2,512,256]{2,1,0:T(8,128)(2,1)S(1)} %get-tuple-element.32.rest_0_), channel_id=1, source_target_pairs={{0,4},{1,5},{2,6},{3,7},{4,0},{5,1},{6,2},{7,3},{8,12},{9,13},{10,... | collective-permute-start | bytes 1572872 | tf_op jit(solution)/shard_map/ppermute | solution.py:34
  38.7 2.1 %collective-permute-start.30 = (bf16[2,512,256]{2,1,0:T(8,128)(2,1)S(1)}, bf16[2,512,256]{2,1,0:T(8,128)(2,1)S(1)}, u32[]{:S(2)}, u32[]{:S(2)}) collective-permute-start(bf16[2,512,256]{2,1,0:T(8,128)(2,1)S(1)} %get-tuple-element.32.rest_0_), channel_id=1, source_target_pairs={{0,6},{1,7},{2,0},{3,1},{4,2},{5,3},{6,4},{7,5},{8,14},{9,15},{10,... | collective-permute-start | bytes 1572872 | tf_op jit(solution)/shard_map/ppermute | solution.py:34
  40.8 0.7 collective-permute-start.35
  41.5 5.8 %collective-permute-start.14 = (bf16[128,256]{1,0:T(8,128)(2,1)S(1)}, bf16[128,256]{1,0:T(8,128)(2,1)S(1)}, u32[]{:S(2)}, u32[]{:S(2)}) collective-permute-start(bf16[128,256]{1,0:T(8,128)(2,1)S(1)} %get-tuple-element.26.a0.query), channel_id=1, source_target_pairs={{0,64},{8,72},{16,80},{24,88},{32,96},{40,104},{48,112},{56,120},{... | collective-permute-start | bytes 196616 | tf_op jit(solution)/shard_map/ppermute | solution.py:22
  47.3 2.2 %collective-permute-done.14.a2 = bf16[128,256]{1,0:T(8,128)(2,1)S(1)} collective-permute-done((bf16[128,256]{1,0:T(8,128)(2,1)S(1)}, bf16[128,256]{1,0:T(8,128)(2,1)S(1)}, u32[]{:S(2)}, u32[]{:S(2)}) %collective-permute-start.14) | collective-permute-done | bytes 65568 | tf_op jit(solution)/shard_map/ppermute | solution.py:22
  49.6 2.1 %collective-permute-start.15 = (bf16[128,256]{1,0:T(8,128)(2,1)S(1)}, bf16[128,256]{1,0:T(8,128)(2,1)S(1)}, u32[]{:S(2)}, u32[]{:S(2)}) collective-permute-start(bf16[128,256]{1,0:T(8,128)(2,1)S(1)} %get-tuple-element.26.a0.query), channel_id=1, source_target_pairs={{0,96},{8,104},{16,112},{24,120},{32,0},{40,8},{48,16},{56,24},{64... | collective-permute-start | bytes 196616 | tf_op jit(solution)/shard_map/ppermute | solution.py:22
  51.6 2.2 %collective-permute-done.15.a3 = bf16[128,256]{1,0:T(8,128)(2,1)S(1)} collective-permute-done((bf16[128,256]{1,0:T(8,128)(2,1)S(1)}, bf16[128,256]{1,0:T(8,128)(2,1)S(1)}, u32[]{:S(2)}, u32[]{:S(2)}) %collective-permute-start.15) | collective-permute-done | bytes 65568 | tf_op jit(solution)/shard_map/ppermute | solution.py:22
  53.9 0.5 collective-permute-start.16
  54.3 15.1 %collective-permute-start.37 = (bf16[256,512]{1,0:T(8,128)(2,1)S(1)}, bf16[256,512]{1,0:T(8,128)(2,1)S(1)}, u32[]{:S(2)}, u32[]{:S(2)}) collective-permute-start(bf16[256,512]{1,0:T(8,128)(2,1)S(1)} %collective-permute-done.35.rest_0_), channel_id=1, source_target_pairs={{0,2},{1,3},{2,4},{3,5},{4,6},{5,7},{6,0},{7,1},{8,10},{9,11},{10,... | collective-permute-start | bytes 786440 | tf_op jit(solution)/shard_map/ppermute | solution.py:34
  69.5 11.4 %collective-permute-start.39 = (bf16[256,512]{1,0:T(8,128)(2,1)S(1)}, bf16[256,512]{1,0:T(8,128)(2,1)S(1)}, u32[]{:S(2)}, u32[]{:S(2)}) collective-permute-start(bf16[256,512]{1,0:T(8,128)(2,1)S(1)} %collective-permute-done.35.rest_0_), channel_id=1, source_target_pairs={{0,4},{1,5},{2,6},{3,7},{4,0},{5,1},{6,2},{7,3},{8,12},{9,13},{10,... | collective-permute-start | bytes 786440 | tf_op jit(solution)/shard_map/ppermute | solution.py:34
  80.8 4.4 %collective-permute-start.18 = (bf16[4,128,256]{2,1,0:T(8,128)(2,1)S(1)}, bf16[4,128,256]{2,1,0:T(8,128)(2,1)S(1)}, u32[]{:S(2)}, u32[]{:S(2)}) collective-permute-start(bf16[4,128,256]{2,1,0:T(8,128)(2,1)S(1)} %shard_map.142.refs_1_), channel_id=1, source_target_pairs={{0,16},{8,24},{16,0},{24,8},{32,48},{40,56},{48,32},{56,40},{64,80... | collective-permute-start | bytes 786440 | tf_op jit(solution)/shard_map/ppermute | solution.py:29
  85.2 1.5 shard_map.144
  86.7 0.7 collective-permute-start.17
  87.4 5.7 %collective-permute-start.41 = (bf16[256,512]{1,0:T(8,128)(2,1)S(1)}, bf16[256,512]{1,0:T(8,128)(2,1)S(1)}, u32[]{:S(2)}, u32[]{:S(2)}) collective-permute-start(bf16[256,512]{1,0:T(8,128)(2,1)S(1)} %collective-permute-done.35.rest_0_), channel_id=1, source_target_pairs={{0,6},{1,7},{2,0},{3,1},{4,2},{5,3},{6,4},{7,5},{8,14},{9,15},{10,... | collective-permute-start | bytes 786440 | tf_op jit(solution)/shard_map/ppermute | solution.py:34
  93.1 0.5 collective-permute-start.29
  93.6 3.8 %collective-permute-done.20.refs_1_ = bf16[4,128,256]{2,1,0:T(8,128)(2,1)S(1)} collective-permute-done((bf16[4,128,256]{2,1,0:T(8,128)(2,1)S(1)}, bf16[4,128,256]{2,1,0:T(8,128)(2,1)S(1)}, u32[]{:S(2)}, u32[]{:S(2)}) %collective-permute-start.20) | collective-permute-done | bytes 262176 | tf_op jit(solution)/shard_map/ppermute | solution.py:29
  97.4 1.5 shard_map.145
  98.9 1.5 shard_map.146
  100.3 0.7 collective-permute-start.19
  101.0 0.8 collective-permute-done.17.p1
  101.8 0.7 collective-permute-start.21
  102.5 8.9 %collective-permute-done.19.p2 = bf16[1072,128]{1,0:T(8,128)(2,1)S(1)} collective-permute-done((bf16[1072,128]{1,0:T(8,128)(2,1)S(1)}, bf16[1072,128]{1,0:T(8,128)(2,1)S(1)}, u32[]{:S(2)}, u32[]{:S(2)}) %collective-permute-start.19) | collective-permute-done | bytes 274464 | tf_op jit(solution)/shard_map/ppermute | solution.py:29
  111.4 5.4 %collective-permute-done.21.p3 = bf16[1072,128]{1,0:T(8,128)(2,1)S(1)} collective-permute-done((bf16[1072,128]{1,0:T(8,128)(2,1)S(1)}, bf16[1072,128]{1,0:T(8,128)(2,1)S(1)}, u32[]{:S(2)}, u32[]{:S(2)}) %collective-permute-start.21) | collective-permute-done | bytes 274464 | tf_op jit(solution)/shard_map/ppermute | solution.py:29
  116.8 1.4 shard_map.143.p0
  118.2 0.8 shard_map.147
  119.1 0.6 collective-permute-start.40
  119.7 0.1 collective-permute-start.42
  119.8 3.9 %collective-permute-done.22.p1 = bf16[272,128]{1,0:T(8,128)(2,1)S(1)} collective-permute-done((bf16[272,128]{1,0:T(8,128)(2,1)S(1)}, bf16[272,128]{1,0:T(8,128)(2,1)S(1)}, u32[]{:S(2)}, u32[]{:S(2)}) %collective-permute-start.22) | collective-permute-done | bytes 69664 | tf_op jit(solution)/shard_map/ppermute | solution.py:22
  123.7 5.8 %collective-permute-done.23.p2 = bf16[272,128]{1,0:T(8,128)(2,1)S(1)} collective-permute-done((bf16[272,128]{1,0:T(8,128)(2,1)S(1)}, bf16[272,128]{1,0:T(8,128)(2,1)S(1)}, u32[]{:S(2)}, u32[]{:S(2)}) %collective-permute-start.23) | collective-permute-done | bytes 69664 | tf_op jit(solution)/shard_map/ppermute | solution.py:22
  129.5 0.8 shard_map.148
  130.3 1.0 shard_map.149
  131.3 3.7 %collective-permute-done.24.p3 = bf16[272,128]{1,0:T(8,128)(2,1)S(1)} collective-permute-done((bf16[272,128]{1,0:T(8,128)(2,1)S(1)}, bf16[272,128]{1,0:T(8,128)(2,1)S(1)}, u32[]{:S(2)}, u32[]{:S(2)}) %collective-permute-start.24) | collective-permute-done | bytes 69664 | tf_op jit(solution)/shard_map/ppermute | solution.py:22
  135.0 0.4 shard_map.150.a0
  135.5 1.7 %collective-permute-start.33 = (bf16[128,256]{1,0:T(8,128)(2,1)S(1)}, bf16[128,256]{1,0:T(8,128)(2,1)S(1)}, u32[]{:S(2)}, u32[]{:S(2)}) collective-permute-start(bf16[128,256]{1,0:T(8,128)(2,1)S(1)} %shard_map.150.a0), channel_id=1, source_target_pairs={{0,64},{8,72},{16,80},{24,88},{32,96},{40,104},{48,112},{56,120},{... | collective-permute-start | bytes 196616 | tf_op jit(solution)/shard_map/ppermute | solution.py:22
  137.3 1.6 %collective-permute-start.34 = (bf16[128,256]{1,0:T(8,128)(2,1)S(1)}, bf16[128,256]{1,0:T(8,128)(2,1)S(1)}, u32[]{:S(2)}, u32[]{:S(2)}) collective-permute-start(bf16[128,256]{1,0:T(8,128)(2,1)S(1)} %shard_map.150.a0), channel_id=1, source_target_pairs={{0,96},{8,104},{16,112},{24,120},{32,0},{40,8},{48,16},{56,24},{64... | collective-permute-start | bytes 196616 | tf_op jit(solution)/shard_map/ppermute | solution.py:22
  138.8 2.9 %collective-permute-done.32.a1 = bf16[128,256]{1,0:T(8,128)(2,1)S(1)} collective-permute-done((bf16[128,256]{1,0:T(8,128)(2,1)S(1)}, bf16[128,256]{1,0:T(8,128)(2,1)S(1)}, u32[]{:S(2)}, u32[]{:S(2)}) %collective-permute-start.32) | collective-permute-done | bytes 65568 | tf_op jit(solution)/shard_map/ppermute | solution.py:22
  141.7 0.9 collective-permute-done.34.a3
  142.6 0.5 shard_map.151
  143.0 0.1 collective-permute-start.43
  143.1 3.2 %collective-permute-start.44 = (bf16[128,256]{1,0:T(8,128)(2,1)S(1)}, bf16[128,256]{1,0:T(8,128)(2,1)S(1)}, u32[]{:S(2)}, u32[]{:S(2)}) collective-permute-start(bf16[128,256]{1,0:T(8,128)(2,1)S(1)} %get-tuple-element.39), channel_id=1, source_target_pairs={{0,24},{8,0},{16,8},{24,16},{32,56},{40,32},{48,40},{56,48},{64,88... | collective-permute-start | bytes 196616 | tf_op jit(solution)/shard_map/ppermute | solution.py:29
  146.3 0.6 copy.15
  147.0 0.6 copy.16
  147.6 1.0 collective-permute-done.43.g1
  148.6 0.3 collective-permute-done.44.g2
  148.9 3.3 %collective-permute-done.45.g3 = bf16[128,256]{1,0:T(8,128)(2,1)S(1)} collective-permute-done((bf16[128,256]{1,0:T(8,128)(2,1)S(1)}, bf16[128,256]{1,0:T(8,128)(2,1)S(1)}, u32[]{:S(2)}, u32[]{:S(2)}) %collective-permute-start.45) | collective-permute-done | bytes 65568 | tf_op jit(solution)/shard_map/ppermute | solution.py:29
  152.1 0.7 shard_map.152
  (52 shorter events, 0.3 us)
Async XLA Ops:
  0.6 33.8 %copy-start.2 = (f32[4096]{0:T(1024)S(1)}, f32[4096]{0:T(1024)}, u32[]{:S(2)}) copy-start(f32[4096]{0:T(1024)} %param.16) | copy-start | bytes 49156
  0.6 40.2 %copy-start.3 = (bf16[256,512]{1,0:T(8,128)(2,1)S(1)}, bf16[256,512]{1,0:T(8,128)(2,1)}, u32[]{:S(2)}) copy-start(bf16[256,512]{1,0:T(8,128)(2,1)} %param.18) | copy-start | bytes 786436
  3.2 10.2 %collective-permute-start = (bf16[128,256]{1,0:T(8,128)(2,1)S(1)}, bf16[128,256]{1,0:T(8,128)(2,1)S(1)}, u32[]{:S(2)}, u32[]{:S(2)}) collective-permute-start(bf16[128,256]{1,0:T(8,128)(2,1)S(1)} %get-tuple-element.22.a0), channel_id=1, source_target_pairs={{0,32},{8,40},{16,48},{24,56},{32,64},{40,72},{48,80},{56,88},{64,... | collective-permute-start | bytes 196616 | tf_op jit(solution)/shard_map/ppermute | solution.py:22
  4.9 9.3 %collective-permute-start.1 = (bf16[128,256]{1,0:T(8,128)(2,1)S(1)}, bf16[128,256]{1,0:T(8,128)(2,1)S(1)}, u32[]{:S(2)}, u32[]{:S(2)}) collective-permute-start(bf16[128,256]{1,0:T(8,128)(2,1)S(1)} %get-tuple-element.22.a0), channel_id=1, source_target_pairs={{0,64},{8,72},{16,80},{24,88},{32,96},{40,104},{48,112},{56,120},{... | collective-permute-start | bytes 196616 | tf_op jit(solution)/shard_map/ppermute | solution.py:22
  7.8 6.4 %collective-permute-start.2 = (bf16[128,256]{1,0:T(8,128)(2,1)S(1)}, bf16[128,256]{1,0:T(8,128)(2,1)S(1)}, u32[]{:S(2)}, u32[]{:S(2)}) collective-permute-start(bf16[128,256]{1,0:T(8,128)(2,1)S(1)} %get-tuple-element.22.a0), channel_id=1, source_target_pairs={{0,96},{8,104},{16,112},{24,120},{32,0},{40,8},{48,16},{56,24},{64... | collective-permute-start | bytes 196616 | tf_op jit(solution)/shard_map/ppermute | solution.py:22
  9.2 76.1 %copy-start = (bf16[2,128,4096]{2,1,0:T(8,128)(2,1)S(1)}, bf16[2,128,4096]{2,1,0:T(8,128)(2,1)}, u32[]{:S(2)}) copy-start(bf16[2,128,4096]{2,1,0:T(8,128)(2,1)} %refs_2_.7) | copy-start | bytes 6291460
  9.2 76.1 %copy-start.1 = (bf16[2,128,4096]{2,1,0:T(8,128)(2,1)S(1)}, bf16[2,128,4096]{2,1,0:T(8,128)(2,1)}, u32[]{:S(2)}) copy-start(bf16[2,128,4096]{2,1,0:T(8,128)(2,1)} %refs_3_.7) | copy-start | bytes 6291460
  9.2 10.7 %collective-permute-start.9 = (bf16[512,256]{1,0:T(8,128)(2,1)S(1)}, bf16[512,256]{1,0:T(8,128)(2,1)S(1)}, u32[]{:S(2)}, u32[]{:S(2)}) collective-permute-start(bf16[512,256]{1,0:T(8,128)(2,1)S(1)} %get-tuple-element.25.rest_0_), channel_id=1, source_target_pairs={{0,4},{1,5},{2,6},{3,7},{4,0},{5,1},{6,2},{7,3},{8,12},{9,13},{10,... | collective-permute-start | bytes 786440 | tf_op jit(solution)/shard_map/ppermute | solution.py:34
  12.2 11.5 %collective-permute-start.11 = (bf16[512,256]{1,0:T(8,128)(2,1)S(1)}, bf16[512,256]{1,0:T(8,128)(2,1)S(1)}, u32[]{:S(2)}, u32[]{:S(2)}) collective-permute-start(bf16[512,256]{1,0:T(8,128)(2,1)S(1)} %get-tuple-element.25.rest_0_), channel_id=1, source_target_pairs={{0,6},{1,7},{2,0},{3,1},{4,2},{5,3},{6,4},{7,5},{8,14},{9,15},{10,... | collective-permute-start | bytes 786440 | tf_op jit(solution)/shard_map/ppermute | solution.py:34
  13.3 14.3 %collective-permute-start.7 = (bf16[512,256]{1,0:T(8,128)(2,1)S(1)}, bf16[512,256]{1,0:T(8,128)(2,1)S(1)}, u32[]{:S(2)}, u32[]{:S(2)}) collective-permute-start(bf16[512,256]{1,0:T(8,128)(2,1)S(1)} %get-tuple-element.25.rest_0_), channel_id=1, source_target_pairs={{0,2},{1,3},{2,4},{3,5},{4,6},{5,7},{6,0},{7,1},{8,10},{9,11},{10,... | collective-permute-start | bytes 786440 | tf_op jit(solution)/shard_map/ppermute | solution.py:34
  14.2 13.4 %collective-permute-start.6 = (bf16[512,256]{1,0:T(8,128)(2,1)S(1)}, bf16[512,256]{1,0:T(8,128)(2,1)S(1)}, u32[]{:S(2)}, u32[]{:S(2)}) collective-permute-start(bf16[512,256]{1,0:T(8,128)(2,1)S(1)} %get-tuple-element.25.rest_0_), channel_id=1, source_target_pairs={{0,1},{1,0},{2,3},{3,2},{4,5},{5,4},{6,7},{7,6},{8,9},{9,8},{10,11... | collective-permute-start | bytes 786440 | tf_op jit(solution)/shard_map/ppermute | solution.py:38
  14.3 13.9 %collective-permute-start.3 = (bf16[4,128,256]{2,1,0:T(8,128)(2,1)S(1)}, bf16[4,128,256]{2,1,0:T(8,128)(2,1)S(1)}, u32[]{:S(2)}, u32[]{:S(2)}) collective-permute-start(bf16[4,128,256]{2,1,0:T(8,128)(2,1)S(1)} %shard_map.140.s0), channel_id=1, source_target_pairs={{0,8},{8,16},{16,24},{24,0},{32,40},{40,48},{48,56},{56,32},{64,72... | collective-permute-start | bytes 786440 | tf_op jit(solution)/shard_map/ppermute | solution.py:29
  19.8 12.3 %collective-permute-start.4 = (bf16[4,128,256]{2,1,0:T(8,128)(2,1)S(1)}, bf16[4,128,256]{2,1,0:T(8,128)(2,1)S(1)}, u32[]{:S(2)}, u32[]{:S(2)}) collective-permute-start(bf16[4,128,256]{2,1,0:T(8,128)(2,1)S(1)} %shard_map.140.s0), channel_id=1, source_target_pairs={{0,16},{8,24},{16,0},{24,8},{32,48},{40,56},{48,32},{56,40},{64,80... | collective-permute-start | bytes 786440 | tf_op jit(solution)/shard_map/ppermute | solution.py:29
  23.7 10.7 %collective-permute-start.5 = (bf16[4,128,256]{2,1,0:T(8,128)(2,1)S(1)}, bf16[4,128,256]{2,1,0:T(8,128)(2,1)S(1)}, u32[]{:S(2)}, u32[]{:S(2)}) collective-permute-start(bf16[4,128,256]{2,1,0:T(8,128)(2,1)S(1)} %shard_map.140.s0), channel_id=1, source_target_pairs={{0,24},{8,0},{16,8},{24,16},{32,56},{40,32},{48,40},{56,48},{64,88... | collective-permute-start | bytes 786440 | tf_op jit(solution)/shard_map/ppermute | solution.py:29
  27.7 6.8 %collective-permute-start.10 = (bf16[512,256]{1,0:T(8,128)(2,1)S(1)}, bf16[512,256]{1,0:T(8,128)(2,1)S(1)}, u32[]{:S(2)}, u32[]{:S(2)}) collective-permute-start(bf16[512,256]{1,0:T(8,128)(2,1)S(1)} %collective-permute-done.9.rest_4_), channel_id=1, source_target_pairs={{0,1},{1,0},{2,3},{3,2},{4,5},{5,4},{6,7},{7,6},{8,9},{9,8},{10,11... | collective-permute-start | bytes 786440 | tf_op jit(solution)/shard_map/ppermute | solution.py:38
  27.7 6.8 %collective-permute-start.12 = (bf16[512,256]{1,0:T(8,128)(2,1)S(1)}, bf16[512,256]{1,0:T(8,128)(2,1)S(1)}, u32[]{:S(2)}, u32[]{:S(2)}) collective-permute-start(bf16[512,256]{1,0:T(8,128)(2,1)S(1)} %collective-permute-done.11.rest_6_), channel_id=1, source_target_pairs={{0,1},{1,0},{2,3},{3,2},{4,5},{5,4},{6,7},{7,6},{8,9},{9,8},{10,11... | collective-permute-start | bytes 786440 | tf_op jit(solution)/shard_map/ppermute | solution.py:38
  28.2 6.2 %collective-permute-start.8 = (bf16[512,256]{1,0:T(8,128)(2,1)S(1)}, bf16[512,256]{1,0:T(8,128)(2,1)S(1)}, u32[]{:S(2)}, u32[]{:S(2)}) collective-permute-start(bf16[512,256]{1,0:T(8,128)(2,1)S(1)} %collective-permute-done.7.rest_2_), channel_id=1, source_target_pairs={{0,1},{1,0},{2,3},{3,2},{4,5},{5,4},{6,7},{7,6},{8,9},{9,8},{10,11... | collective-permute-start | bytes 786440 | tf_op jit(solution)/shard_map/ppermute | solution.py:38
  32.1 22.2 %collective-permute-start.26 = (bf16[2,512,256]{2,1,0:T(8,128)(2,1)S(1)}, bf16[2,512,256]{2,1,0:T(8,128)(2,1)S(1)}, u32[]{:S(2)}, u32[]{:S(2)}) collective-permute-start(bf16[2,512,256]{2,1,0:T(8,128)(2,1)S(1)} %get-tuple-element.32.rest_0_), channel_id=1, source_target_pairs={{0,2},{1,3},{2,4},{3,5},{4,6},{5,7},{6,0},{7,1},{8,10},{9,11},{10,... | collective-permute-start | bytes 1572872 | tf_op jit(solution)/shard_map/ppermute | solution.py:34
  35.4 6.1 %collective-permute-start.13 = (bf16[128,256]{1,0:T(8,128)(2,1)S(1)}, bf16[128,256]{1,0:T(8,128)(2,1)S(1)}, u32[]{:S(2)}, u32[]{:S(2)}) collective-permute-start(bf16[128,256]{1,0:T(8,128)(2,1)S(1)} %get-tuple-element.26.a0.query), channel_id=1, source_target_pairs={{0,32},{8,40},{16,48},{24,56},{32,64},{40,72},{48,80},{56,88},{64,... | collective-permute-start | bytes 196616 | tf_op jit(solution)/shard_map/ppermute | solution.py:22
  36.2 33.3 %collective-permute-start.28 = (bf16[2,512,256]{2,1,0:T(8,128)(2,1)S(1)}, bf16[2,512,256]{2,1,0:T(8,128)(2,1)S(1)}, u32[]{:S(2)}, u32[]{:S(2)}) collective-permute-start(bf16[2,512,256]{2,1,0:T(8,128)(2,1)S(1)} %get-tuple-element.32.rest_0_), channel_id=1, source_target_pairs={{0,4},{1,5},{2,6},{3,7},{4,0},{5,1},{6,2},{7,3},{8,12},{9,13},{10,... | collective-permute-start | bytes 1572872 | tf_op jit(solution)/shard_map/ppermute | solution.py:34
  38.7 42.1 %collective-permute-start.30 = (bf16[2,512,256]{2,1,0:T(8,128)(2,1)S(1)}, bf16[2,512,256]{2,1,0:T(8,128)(2,1)S(1)}, u32[]{:S(2)}, u32[]{:S(2)}) collective-permute-start(bf16[2,512,256]{2,1,0:T(8,128)(2,1)S(1)} %get-tuple-element.32.rest_0_), channel_id=1, source_target_pairs={{0,6},{1,7},{2,0},{3,1},{4,2},{5,3},{6,4},{7,5},{8,14},{9,15},{10,... | collective-permute-start | bytes 1572872 | tf_op jit(solution)/shard_map/ppermute | solution.py:34
  40.8 13.0 %collective-permute-start.35 = (bf16[256,512]{1,0:T(8,128)(2,1)S(1)}, bf16[256,512]{1,0:T(8,128)(2,1)S(1)}, u32[]{:S(2)}, u32[]{:S(2)}) collective-permute-start(bf16[256,512]{1,0:T(8,128)(2,1)S(1)} %copy-done.3), channel_id=1, source_target_pairs={{0,0},{1,1},{8,8},{9,9},{16,16},{17,17},{24,24},{25,25},{32,2},{33... | collective-permute-start | bytes 786440 | tf_op jit(solution)/shard_map/ppermute | solution.py:52
  41.5 8.1 %collective-permute-start.14 = (bf16[128,256]{1,0:T(8,128)(2,1)S(1)}, bf16[128,256]{1,0:T(8,128)(2,1)S(1)}, u32[]{:S(2)}, u32[]{:S(2)}) collective-permute-start(bf16[128,256]{1,0:T(8,128)(2,1)S(1)} %get-tuple-element.26.a0.query), channel_id=1, source_target_pairs={{0,64},{8,72},{16,80},{24,88},{32,96},{40,104},{48,112},{56,120},{... | collective-permute-start | bytes 196616 | tf_op jit(solution)/shard_map/ppermute | solution.py:22
  49.6 4.3 %collective-permute-start.15 = (bf16[128,256]{1,0:T(8,128)(2,1)S(1)}, bf16[128,256]{1,0:T(8,128)(2,1)S(1)}, u32[]{:S(2)}, u32[]{:S(2)}) collective-permute-start(bf16[128,256]{1,0:T(8,128)(2,1)S(1)} %get-tuple-element.26.a0.query), channel_id=1, source_target_pairs={{0,96},{8,104},{16,112},{24,120},{32,0},{40,8},{48,16},{56,24},{64... | collective-permute-start | bytes 196616 | tf_op jit(solution)/shard_map/ppermute | solution.py:22
  53.8 32.9 %collective-permute-start.25 = (bf16[2,512,256]{2,1,0:T(8,128)(2,1)S(1)}, bf16[2,512,256]{2,1,0:T(8,128)(2,1)S(1)}, u32[]{:S(2)}, u32[]{:S(2)}) collective-permute-start(bf16[2,512,256]{2,1,0:T(8,128)(2,1)S(1)} %get-tuple-element.32.rest_0_), channel_id=1, source_target_pairs={{0,1},{1,0},{2,3},{3,2},{4,5},{5,4},{6,7},{7,6},{8,9},{9,8},{10,11... | collective-permute-start | bytes 1572872 | tf_op jit(solution)/shard_map/ppermute | solution.py:38
  53.9 31.4 %collective-permute-start.16 = (bf16[4,128,256]{2,1,0:T(8,128)(2,1)S(1)}, bf16[4,128,256]{2,1,0:T(8,128)(2,1)S(1)}, u32[]{:S(2)}, u32[]{:S(2)}) collective-permute-start(bf16[4,128,256]{2,1,0:T(8,128)(2,1)S(1)} %shard_map.142.refs_1_), channel_id=1, source_target_pairs={{0,8},{8,16},{16,24},{24,0},{32,40},{40,48},{48,56},{56,32},{64,72... | collective-permute-start | bytes 786440 | tf_op jit(solution)/shard_map/ppermute | solution.py:29
  54.3 33.1 %collective-permute-start.37 = (bf16[256,512]{1,0:T(8,128)(2,1)S(1)}, bf16[256,512]{1,0:T(8,128)(2,1)S(1)}, u32[]{:S(2)}, u32[]{:S(2)}) collective-permute-start(bf16[256,512]{1,0:T(8,128)(2,1)S(1)} %collective-permute-done.35.rest_0_), channel_id=1, source_target_pairs={{0,2},{1,3},{2,4},{3,5},{4,6},{5,7},{6,0},{7,1},{8,10},{9,11},{10,... | collective-permute-start | bytes 786440 | tf_op jit(solution)/shard_map/ppermute | solution.py:34
  69.5 23.6 %collective-permute-start.39 = (bf16[256,512]{1,0:T(8,128)(2,1)S(1)}, bf16[256,512]{1,0:T(8,128)(2,1)S(1)}, u32[]{:S(2)}, u32[]{:S(2)}) collective-permute-start(bf16[256,512]{1,0:T(8,128)(2,1)S(1)} %collective-permute-done.35.rest_0_), channel_id=1, source_target_pairs={{0,4},{1,5},{2,6},{3,7},{4,0},{5,1},{6,2},{7,3},{8,12},{9,13},{10,... | collective-permute-start | bytes 786440 | tf_op jit(solution)/shard_map/ppermute | solution.py:34
  80.8 12.2 %collective-permute-start.18 = (bf16[4,128,256]{2,1,0:T(8,128)(2,1)S(1)}, bf16[4,128,256]{2,1,0:T(8,128)(2,1)S(1)}, u32[]{:S(2)}, u32[]{:S(2)}) collective-permute-start(bf16[4,128,256]{2,1,0:T(8,128)(2,1)S(1)} %shard_map.142.refs_1_), channel_id=1, source_target_pairs={{0,16},{8,24},{16,0},{24,8},{32,48},{40,56},{48,32},{56,40},{64,80... | collective-permute-start | bytes 786440 | tf_op jit(solution)/shard_map/ppermute | solution.py:29
  85.2 12.2 %collective-permute-start.20 = (bf16[4,128,256]{2,1,0:T(8,128)(2,1)S(1)}, bf16[4,128,256]{2,1,0:T(8,128)(2,1)S(1)}, u32[]{:S(2)}, u32[]{:S(2)}) collective-permute-start(bf16[4,128,256]{2,1,0:T(8,128)(2,1)S(1)} %shard_map.142.refs_1_), channel_id=1, source_target_pairs={{0,24},{8,0},{16,8},{24,16},{32,56},{40,32},{48,40},{56,48},{64,88... | collective-permute-start | bytes 786440 | tf_op jit(solution)/shard_map/ppermute | solution.py:29
  86.7 15.1 %collective-permute-start.17 = (bf16[1072,128]{1,0:T(8,128)(2,1)S(1)}, bf16[1072,128]{1,0:T(8,128)(2,1)S(1)}, u32[]{:S(2)}, u32[]{:S(2)}) collective-permute-start(bf16[1072,128]{1,0:T(8,128)(2,1)S(1)} %shard_map.144), channel_id=1, source_target_pairs={{0,24},{8,0},{16,8},{24,16},{32,56},{40,32},{48,40},{56,48},{64,88... | collective-permute-start | bytes 823304 | tf_op jit(solution)/shard_map/ppermute | solution.py:29
  87.4 13.0 %collective-permute-start.41 = (bf16[256,512]{1,0:T(8,128)(2,1)S(1)}, bf16[256,512]{1,0:T(8,128)(2,1)S(1)}, u32[]{:S(2)}, u32[]{:S(2)}) collective-permute-start(bf16[256,512]{1,0:T(8,128)(2,1)S(1)} %collective-permute-done.35.rest_0_), channel_id=1, source_target_pairs={{0,6},{1,7},{2,0},{3,1},{4,2},{5,3},{6,4},{7,5},{8,14},{9,15},{10,... | collective-permute-start | bytes 786440 | tf_op jit(solution)/shard_map/ppermute | solution.py:34
  93.1 26.0 %collective-permute-start.27 = (bf16[2,512,256]{2,1,0:T(8,128)(2,1)S(1)}, bf16[2,512,256]{2,1,0:T(8,128)(2,1)S(1)}, u32[]{:S(2)}, u32[]{:S(2)}) collective-permute-start(bf16[2,512,256]{2,1,0:T(8,128)(2,1)S(1)} %collective-permute-done.26.rest_2_), channel_id=1, source_target_pairs={{0,1},{1,0},{2,3},{3,2},{4,5},{5,4},{6,7},{7,6},{8,9},{9,8},{10,11... | collective-permute-start | bytes 1572872 | tf_op jit(solution)/shard_map/ppermute | solution.py:38
  93.1 26.1 %collective-permute-start.29 = (bf16[2,512,256]{2,1,0:T(8,128)(2,1)S(1)}, bf16[2,512,256]{2,1,0:T(8,128)(2,1)S(1)}, u32[]{:S(2)}, u32[]{:S(2)}) collective-permute-start(bf16[2,512,256]{2,1,0:T(8,128)(2,1)S(1)} %collective-permute-done.28.rest_4_), channel_id=1, source_target_pairs={{0,1},{1,0},{2,3},{3,2},{4,5},{5,4},{6,7},{7,6},{8,9},{9,8},{10,11... | collective-permute-start | bytes 1572872 | tf_op jit(solution)/shard_map/ppermute | solution.py:38
  97.4 22.3 %collective-permute-start.31 = (bf16[2,512,256]{2,1,0:T(8,128)(2,1)S(1)}, bf16[2,512,256]{2,1,0:T(8,128)(2,1)S(1)}, u32[]{:S(2)}, u32[]{:S(2)}) collective-permute-start(bf16[2,512,256]{2,1,0:T(8,128)(2,1)S(1)} %collective-permute-done.30.rest_6_), channel_id=1, source_target_pairs={{0,1},{1,0},{2,3},{3,2},{4,5},{5,4},{6,7},{7,6},{8,9},{9,8},{10,11... | collective-permute-start | bytes 1572872 | tf_op jit(solution)/shard_map/ppermute | solution.py:38
  100.3 11.1 %collective-permute-start.19 = (bf16[1072,128]{1,0:T(8,128)(2,1)S(1)}, bf16[1072,128]{1,0:T(8,128)(2,1)S(1)}, u32[]{:S(2)}, u32[]{:S(2)}) collective-permute-start(bf16[1072,128]{1,0:T(8,128)(2,1)S(1)} %shard_map.145), channel_id=1, source_target_pairs={{0,16},{8,24},{16,0},{24,8},{32,48},{40,56},{48,32},{56,40},{64,80... | collective-permute-start | bytes 823304 | tf_op jit(solution)/shard_map/ppermute | solution.py:29
  101.8 15.0 %collective-permute-start.21 = (bf16[1072,128]{1,0:T(8,128)(2,1)S(1)}, bf16[1072,128]{1,0:T(8,128)(2,1)S(1)}, u32[]{:S(2)}, u32[]{:S(2)}) collective-permute-start(bf16[1072,128]{1,0:T(8,128)(2,1)S(1)} %shard_map.146), channel_id=1, source_target_pairs={{0,8},{8,16},{16,24},{24,0},{32,40},{40,48},{48,56},{56,32},{64,72... | collective-permute-start | bytes 823304 | tf_op jit(solution)/shard_map/ppermute | solution.py:29
  111.4 24.1 %collective-permute-start.36 = (bf16[256,512]{1,0:T(8,128)(2,1)S(1)}, bf16[256,512]{1,0:T(8,128)(2,1)S(1)}, u32[]{:S(2)}, u32[]{:S(2)}) collective-permute-start(bf16[256,512]{1,0:T(8,128)(2,1)S(1)} %collective-permute-done.35.rest_0_), channel_id=1, source_target_pairs={{0,1},{1,0},{2,3},{3,2},{4,5},{5,4},{6,7},{7,6},{8,9},{9,8},{10,11... | collective-permute-start | bytes 786440 | tf_op jit(solution)/shard_map/ppermute | solution.py:38
  116.8 20.5 %collective-permute-start.38 = (bf16[256,512]{1,0:T(8,128)(2,1)S(1)}, bf16[256,512]{1,0:T(8,128)(2,1)S(1)}, u32[]{:S(2)}, u32[]{:S(2)}) collective-permute-start(bf16[256,512]{1,0:T(8,128)(2,1)S(1)} %collective-permute-done.37.rest_2_), channel_id=1, source_target_pairs={{0,1},{1,0},{2,3},{3,2},{4,5},{5,4},{6,7},{7,6},{8,9},{9,8},{10,11... | collective-permute-start | bytes 786440 | tf_op jit(solution)/shard_map/ppermute | solution.py:38
  119.1 4.6 %collective-permute-start.22 = (bf16[272,128]{1,0:T(8,128)(2,1)S(1)}, bf16[272,128]{1,0:T(8,128)(2,1)S(1)}, u32[]{:S(2)}, u32[]{:S(2)}) collective-permute-start(bf16[272,128]{1,0:T(8,128)(2,1)S(1)} %get-tuple-element.28), channel_id=1, source_target_pairs={{0,96},{8,104},{16,112},{24,120},{32,0},{40,8},{48,16},{56,24},{64... | collective-permute-start | bytes 208904 | tf_op jit(solution)/shard_map/ppermute | solution.py:22
  119.1 19.7 %collective-permute-start.40 = (bf16[256,512]{1,0:T(8,128)(2,1)S(1)}, bf16[256,512]{1,0:T(8,128)(2,1)S(1)}, u32[]{:S(2)}, u32[]{:S(2)}) collective-permute-start(bf16[256,512]{1,0:T(8,128)(2,1)S(1)} %collective-permute-done.39.rest_4_), channel_id=1, source_target_pairs={{0,1},{1,0},{2,3},{3,2},{4,5},{5,4},{6,7},{7,6},{8,9},{9,8},{10,11... | collective-permute-start | bytes 786440 | tf_op jit(solution)/shard_map/ppermute | solution.py:38
  119.7 19.1 %collective-permute-start.42 = (bf16[256,512]{1,0:T(8,128)(2,1)S(1)}, bf16[256,512]{1,0:T(8,128)(2,1)S(1)}, u32[]{:S(2)}, u32[]{:S(2)}) collective-permute-start(bf16[256,512]{1,0:T(8,128)(2,1)S(1)} %collective-permute-done.41.rest_6_), channel_id=1, source_target_pairs={{0,1},{1,0},{2,3},{3,2},{4,5},{5,4},{6,7},{7,6},{8,9},{9,8},{10,11... | collective-permute-start | bytes 786440 | tf_op jit(solution)/shard_map/ppermute | solution.py:38
  123.7 5.8 %collective-permute-start.23 = (bf16[272,128]{1,0:T(8,128)(2,1)S(1)}, bf16[272,128]{1,0:T(8,128)(2,1)S(1)}, u32[]{:S(2)}, u32[]{:S(2)}) collective-permute-start(bf16[272,128]{1,0:T(8,128)(2,1)S(1)} %get-tuple-element.29), channel_id=1, source_target_pairs={{0,64},{8,72},{16,80},{24,88},{32,96},{40,104},{48,112},{56,120},{... | collective-permute-start | bytes 208904 | tf_op jit(solution)/shard_map/ppermute | solution.py:22
  129.5 5.5 %collective-permute-start.24 = (bf16[272,128]{1,0:T(8,128)(2,1)S(1)}, bf16[272,128]{1,0:T(8,128)(2,1)S(1)}, u32[]{:S(2)}, u32[]{:S(2)}) collective-permute-start(bf16[272,128]{1,0:T(8,128)(2,1)S(1)} %get-tuple-element.30), channel_id=1, source_target_pairs={{0,32},{8,40},{16,48},{24,56},{32,64},{40,72},{48,80},{56,88},{64,... | collective-permute-start | bytes 208904 | tf_op jit(solution)/shard_map/ppermute | solution.py:22
  135.4 6.2 %collective-permute-start.32 = (bf16[128,256]{1,0:T(8,128)(2,1)S(1)}, bf16[128,256]{1,0:T(8,128)(2,1)S(1)}, u32[]{:S(2)}, u32[]{:S(2)}) collective-permute-start(bf16[128,256]{1,0:T(8,128)(2,1)S(1)} %shard_map.150.a0), channel_id=1, source_target_pairs={{0,32},{8,40},{16,48},{24,56},{32,64},{40,72},{48,80},{56,88},{64,... | collective-permute-start | bytes 196616 | tf_op jit(solution)/shard_map/ppermute | solution.py:22
  135.5 6.2 %collective-permute-start.33 = (bf16[128,256]{1,0:T(8,128)(2,1)S(1)}, bf16[128,256]{1,0:T(8,128)(2,1)S(1)}, u32[]{:S(2)}, u32[]{:S(2)}) collective-permute-start(bf16[128,256]{1,0:T(8,128)(2,1)S(1)} %shard_map.150.a0), channel_id=1, source_target_pairs={{0,64},{8,72},{16,80},{24,88},{32,96},{40,104},{48,112},{56,120},{... | collective-permute-start | bytes 196616 | tf_op jit(solution)/shard_map/ppermute | solution.py:22
  137.3 5.3 %collective-permute-start.34 = (bf16[128,256]{1,0:T(8,128)(2,1)S(1)}, bf16[128,256]{1,0:T(8,128)(2,1)S(1)}, u32[]{:S(2)}, u32[]{:S(2)}) collective-permute-start(bf16[128,256]{1,0:T(8,128)(2,1)S(1)} %shard_map.150.a0), channel_id=1, source_target_pairs={{0,96},{8,104},{16,112},{24,120},{32,0},{40,8},{48,16},{56,24},{64... | collective-permute-start | bytes 196616 | tf_op jit(solution)/shard_map/ppermute | solution.py:22
  143.0 5.5 %collective-permute-start.43 = (bf16[128,256]{1,0:T(8,128)(2,1)S(1)}, bf16[128,256]{1,0:T(8,128)(2,1)S(1)}, u32[]{:S(2)}, u32[]{:S(2)}) collective-permute-start(bf16[128,256]{1,0:T(8,128)(2,1)S(1)} %get-tuple-element.38), channel_id=1, source_target_pairs={{0,8},{8,16},{16,24},{24,0},{32,40},{40,48},{48,56},{56,32},{64,72... | collective-permute-start | bytes 196616 | tf_op jit(solution)/shard_map/ppermute | solution.py:29
  143.1 5.7 %collective-permute-start.44 = (bf16[128,256]{1,0:T(8,128)(2,1)S(1)}, bf16[128,256]{1,0:T(8,128)(2,1)S(1)}, u32[]{:S(2)}, u32[]{:S(2)}) collective-permute-start(bf16[128,256]{1,0:T(8,128)(2,1)S(1)} %get-tuple-element.39), channel_id=1, source_target_pairs={{0,24},{8,0},{16,8},{24,16},{32,56},{40,32},{48,40},{56,48},{64,88... | collective-permute-start | bytes 196616 | tf_op jit(solution)/shard_map/ppermute | solution.py:29
  146.3 5.8 %collective-permute-start.45 = (bf16[128,256]{1,0:T(8,128)(2,1)S(1)}, bf16[128,256]{1,0:T(8,128)(2,1)S(1)}, u32[]{:S(2)}, u32[]{:S(2)}) collective-permute-start(bf16[128,256]{1,0:T(8,128)(2,1)S(1)} %get-tuple-element.40), channel_id=1, source_target_pairs={{0,16},{8,24},{16,0},{24,8},{32,48},{40,56},{48,32},{56,40},{64,80... | collective-permute-start | bytes 196616 | tf_op jit(solution)/shard_map/ppermute | solution.py:29

commit v4 on v3

--- a/solution.py
+++ b/solution.py
@@ -43,7 +43,7 @@
         return (y * SIDE + z) * 2 * SIDE + 2 * i + c
 
     pairs = [
-        (place(i, y, z, c), place(y, i, z, c))
+        (place(i, y, z, c), place((i + y) % SIDE, i, z, c))
         for i in range(SIDE)
         for y in range(SIDE)
         for z in range(SIDE)
@@ -201,7 +201,7 @@
 
 
 def query_body(s0, s1, s2, s3, gain, cosine, sine, *rest):
-    weights, (query, normed) = rest[:8], rest[8:]
+    weights, (query, turned, normed) = rest[:8], rest[8:]
     place = position()
     stacks = (s0, s1, s2, s3)
     rows = s0.shape[1]
@@ -220,7 +220,9 @@
     projected = pieces_product(place, normed, weights, lambda w: w[...])
     for h in range(projected.shape[1] // HEAD):
         cut = slice(h * HEAD, (h + 1) * HEAD)
-        query[:, cut] = spin(projected[:, cut], cosine[...], sine[...]).astype(bf16)
+        head = spin(projected[:, cut], cosine[...], sine[...])
+        query[:, cut] = head.astype(bf16)
+        turned[cut, :] = jnp.transpose(head).astype(bf16)
 
 
 def key_value_body(normed, cosine, sine, *rest):
@@ -249,7 +251,7 @@
 def history_body(step, lengths, stack, k_cache, v_cache, out, scores, weights):
     meetings, span = k_cache.shape[0], k_cache.shape[1]
     place = position()
-    rows = stack.shape[1]
+    rows = stack.shape[2]
     new = rows // meetings
     heads = 2 * SIDE
     starts = []
@@ -257,23 +259,22 @@
         block = SIDE * ((place[2] + SIDE - k) % SIDE) + (place[3] + SIDE - step) % SIDE
         for h in range(2):
             starts.append(pl.multiple_of(block * 256 + h * HEAD, HEAD))
+    early = lax.broadcasted_iota(jnp.int32, (span, rows), 1) < new
+    first = (place[2] * SIDE + place[3]) * span
+    spot = first + lax.broadcasted_iota(jnp.int32, (span, rows), 0)
+    live = spot < jnp.where(early, lengths[0], lengths[1])
     for i, start in enumerate(starts):
-        cut = slice(i % 2 * HEAD, (i % 2 + 1) * HEAD)
-        for m in range(meetings):
-            here = slice(m * new, (m + 1) * new)
-            scores[i, here, :] = matmul_t(
-                stack[i // 2, here, cut], k_cache[m, :, pl.ds(start, HEAD)]
-            )
-    first = (place[2] * SIDE + place[3]) * span
-    spot = first + lax.broadcasted_iota(jnp.int32, (rows, span), 1)
-    upper = lax.broadcasted_iota(jnp.int32, (rows, span), 0) < new
-    live = spot < jnp.where(upper, lengths[0], lengths[1])
-    lane = lax.broadcasted_iota(jnp.int32, (rows, HEAD), 1)
-    stats = jnp.zeros((rows, HEAD), f32)
+        query = stack[i // 2, i % 2 * HEAD : (i % 2 + 1) * HEAD, :]
+        both = [matmul(k_cache[m, :, pl.ds(start, HEAD)], query) for m in range(meetings)]
+        scores[i] = jnp.where(early, both[0], both[1])
+    tops, totals = [], []
     for i in range(heads):
-        weight, most, total = soft_weights(scores[i] * HEAD**-0.5, live)
-        weights[i] = weight.astype(bf16)
-        stats = jnp.where(lane == i, most, jnp.where(lane == heads + i, total, stats))
+        score = jnp.where(live, scores[i] * HEAD**-0.5, FLOOR)
+        most = jnp.max(score, axis=0, keepdims=True)
+        weight = jnp.exp(score - jnp.where(most > 0.5 * FLOOR, most, 0.0))
+        tops.append(most)
+        totals.append(jnp.sum(weight, axis=0, keepdims=True))
+        weights[i] = jnp.transpose(weight.astype(bf16))
     for i, start in enumerate(starts):
         for m in range(meetings):
             here = slice(m * new, (m + 1) * new)
@@ -281,9 +282,9 @@
             out[at : at + new, :] = matmul(
                 weights[i, here, :], v_cache[m, :, pl.ds(start, HEAD)]
             ).astype(bf16)
-    turned = jnp.transpose(stats)[: 2 * heads]
+    stats = jnp.concatenate(tops + totals, axis=0)
     base = heads * rows
-    for n, piece in enumerate(split_in_three(turned)):
+    for n, piece in enumerate(split_in_three(stats)):
         out[base + 16 * n : base + 16 * n + 16, :] = piece.astype(bf16)
 
 
@@ -381,7 +382,7 @@
     for c in range(2):
         total = None
         for j in range(SIDE):
-            part = matmul(across[(place[0] + SIDE - j) % SIDE], weights[2 * j + c][...])
+            part = matmul(across[(place[0] + 2 * SIDE - place[2] - j) % SIDE], weights[2 * j + c][...])
             total = part if total is None else total + part
         first = 2 * ((place[1] + c) % 2)
         sums[first] = total[:, :256]
@@ -449,17 +450,18 @@
     out_weights = over_x(swapped)
 
     gain = norm_gain.reshape(SIDE * SIDE, 1, cols)
-    query, normed = kernel_call(
+    query, query_turned, normed = kernel_call(
         query_body,
         [(VMEM, s) for s in stacks]
         + [(VMEM, gain), (VMEM, cosine), (VMEM, sine)]
         + [(VMEM, w) for w in query_weights],
         (
             near((rows, cols), bf16),
+            near((cols, rows), bf16),
             near((SIDE * SIDE, rows, cols), bf16),
         ),
     )
-    query_column = stacked(from_ring(query, y_shift))
+    query_column = stacked(from_ring(query_turned, y_shift))
     query_stacks = from_ring(query_column, z_shift)
 
     keys, values = kernel_call(

time: 153 us -> 147 us (0.961)
  starting transfers between devices: 83 us -> 77.2 us
    ppermute x9, starting transfers between devices: 42.5 us -> 36.9 us  [x_shift(): return lax.ppermute(x, 'wt', pairs)]
where the time goes in v4:
time: 147 us
  starting transfers between devices  77.2 us (53%)
  waiting for transfers between devices  54.5 us (37%)
  Pallas kernels  12.8 us (9%)
    ppermute x9, starting transfers between devices, x_shift(): return lax.ppermute(x, 'wt', pairs)  36.9 us
    ppermute x12, waiting for transfers between devices, z_shift(): return lax.ppermute(x, 'ctx', pairs)  29.5 us
    ppermute x12, waiting for transfers between devices, y_shift(): return lax.ppermute(x, 'ctx', pairs)  21.4 us
    ppermute x12, starting transfers between devices, z_shift(): return lax.ppermute(x, 'ctx', pairs)  19.6 us
    ppermute x12, starting transfers between devices, y_shift(): return lax.ppermute(x, 'ctx', pairs)  18.2 us
    pallas_call x14, Pallas kernels, kernel_call(): pl.pallas_call(body, in_specs=[s for s, _ in ins], out_specs=VMEM if sing...  12.8 us
    ppermute x9, waiting for transfers between devices, x_shift(): return lax.ppermute(x, 'wt', pairs)  3.62 us
  transfers between devices with their start and end apart: 46, of which 17 were waited for; matrix products, arithmetic and copies ran while one was open for 1% of the time, Pallas kernels for 6%

profile of v4, /device:TPU:0, one launch (start us, length us, event | category | flops | bytes accessed | tf_op | source)
XLA Modules:
  0.0 146.7 jit_solution(2808786567618934622)
XLA Ops:
  0.7 2.5 %shard_map.139 = (bf16[128,256]{1,0:T(8,128)(2,1)S(1)}, bf16[512,256]{1,0:T(8,128)(2,1)S(1)}, bf16[2,512,256]{2,1,0:T(8,128)(2,1)S(1)}, f32[128,128]{1,0:T(8,128)S(1)}, f32[128,128]{1,0:T(8,128)S(1)}) custom-call(s32[8]{0:T(128)} %source.1, s32[2]{0:T(128)} %refs_0_.7, bf16[128,1280]{1,0:T(8,128)(2,1)} %frames.1, bf16[1280,256]{1,0:T(8,128)(2,1)} %weight.1, ...), custom_call_target="tpu_custom_call" | custom-call | tf_op jit(solution)/shard_map/pallas_call | solution.py:93
  3.2 1.8 %collective-permute-start = (bf16[128,256]{1,0:T(8,128)(2,1)S(1)}, bf16[128,256]{1,0:T(8,128)(2,1)S(1)}, u32[]{:S(2)}, u32[]{:S(2)}) collective-permute-start(bf16[128,256]{1,0:T(8,128)(2,1)S(1)} %get-tuple-element.23.a0), channel_id=1, source_target_pairs={{0,32},{8,40},{16,48},{24,56},{32,64},{40,72},{48,80},{56,88},{64,... | collective-permute-start | bytes 196616 | tf_op jit(solution)/shard_map/ppermute | solution.py:22
  4.9 2.9 %collective-permute-start.1 = (bf16[128,256]{1,0:T(8,128)(2,1)S(1)}, bf16[128,256]{1,0:T(8,128)(2,1)S(1)}, u32[]{:S(2)}, u32[]{:S(2)}) collective-permute-start(bf16[128,256]{1,0:T(8,128)(2,1)S(1)} %get-tuple-element.23.a0), channel_id=1, source_target_pairs={{0,64},{8,72},{16,80},{24,88},{32,96},{40,104},{48,112},{56,120},{... | collective-permute-start | bytes 196616 | tf_op jit(solution)/shard_map/ppermute | solution.py:22
  7.8 1.3 collective-permute-start.2
  9.2 3.0 %collective-permute-start.9 = (bf16[512,256]{1,0:T(8,128)(2,1)S(1)}, bf16[512,256]{1,0:T(8,128)(2,1)S(1)}, u32[]{:S(2)}, u32[]{:S(2)}) collective-permute-start(bf16[512,256]{1,0:T(8,128)(2,1)S(1)} %get-tuple-element.26.rest_0_), channel_id=1, source_target_pairs={{0,4},{1,5},{2,6},{3,7},{4,0},{5,1},{6,2},{7,3},{8,12},{9,13},{10,... | collective-permute-start | bytes 786440 | tf_op jit(solution)/shard_map/ppermute | solution.py:34
  12.2 1.1 collective-permute-start.11
  13.3 0.9 collective-permute-start.7
  14.3 2.0 %collective-permute-start.3 = (bf16[4,128,256]{2,1,0:T(8,128)(2,1)S(1)}, bf16[4,128,256]{2,1,0:T(8,128)(2,1)S(1)}, u32[]{:S(2)}, u32[]{:S(2)}) collective-permute-start(bf16[4,128,256]{2,1,0:T(8,128)(2,1)S(1)} %shard_map.140.s0), channel_id=1, source_target_pairs={{0,8},{8,16},{16,24},{24,0},{32,40},{40,48},{48,56},{56,32},{64,72... | collective-permute-start | bytes 786440 | tf_op jit(solution)/shard_map/ppermute | solution.py:29
  16.2 3.6 %collective-permute-done.9.rest_4_ = bf16[512,256]{1,0:T(8,128)(2,1)S(1)} collective-permute-done((bf16[512,256]{1,0:T(8,128)(2,1)S(1)}, bf16[512,256]{1,0:T(8,128)(2,1)S(1)}, u32[]{:S(2)}, u32[]{:S(2)}) %collective-permute-start.9) | collective-permute-done | bytes 262176 | tf_op jit(solution)/shard_map/ppermute | solution.py:34
  19.8 3.9 %collective-permute-start.4 = (bf16[4,128,256]{2,1,0:T(8,128)(2,1)S(1)}, bf16[4,128,256]{2,1,0:T(8,128)(2,1)S(1)}, u32[]{:S(2)}, u32[]{:S(2)}) collective-permute-start(bf16[4,128,256]{2,1,0:T(8,128)(2,1)S(1)} %shard_map.140.s0), channel_id=1, source_target_pairs={{0,16},{8,24},{16,0},{24,8},{32,48},{40,56},{48,32},{56,40},{64,80... | collective-permute-start | bytes 786440 | tf_op jit(solution)/shard_map/ppermute | solution.py:29
  23.7 3.9 %collective-permute-start.5 = (bf16[4,128,256]{2,1,0:T(8,128)(2,1)S(1)}, bf16[4,128,256]{2,1,0:T(8,128)(2,1)S(1)}, u32[]{:S(2)}, u32[]{:S(2)}) collective-permute-start(bf16[4,128,256]{2,1,0:T(8,128)(2,1)S(1)} %shard_map.140.s0), channel_id=1, source_target_pairs={{0,24},{8,0},{16,8},{24,16},{32,56},{40,32},{48,40},{56,48},{64,88... | collective-permute-start | bytes 786440 | tf_op jit(solution)/shard_map/ppermute | solution.py:29
  27.7 0.5 collective-permute-start.12
  28.2 0.1 collective-permute-start.8
  28.3 3.9 %collective-permute-done.4.s2 = bf16[4,128,256]{2,1,0:T(8,128)(2,1)S(1)} collective-permute-done((bf16[4,128,256]{2,1,0:T(8,128)(2,1)S(1)}, bf16[4,128,256]{2,1,0:T(8,128)(2,1)S(1)}, u32[]{:S(2)}, u32[]{:S(2)}) %collective-permute-start.4) | collective-permute-done | bytes 262176 | tf_op jit(solution)/shard_map/ppermute | solution.py:29
  32.1 0.6 collective-permute-start.26
  32.7 1.7 %collective-permute-done.5.s3 = bf16[4,128,256]{2,1,0:T(8,128)(2,1)S(1)} collective-permute-done((bf16[4,128,256]{2,1,0:T(8,128)(2,1)S(1)}, bf16[4,128,256]{2,1,0:T(8,128)(2,1)S(1)}, u32[]{:S(2)}, u32[]{:S(2)}) %collective-permute-start.5) | collective-permute-done | bytes 262176 | tf_op jit(solution)/shard_map/ppermute | solution.py:29
  34.4 1.1 shard_map.141
  35.5 0.7 collective-permute-start.13
  36.2 2.5 %collective-permute-start.28 = (bf16[2,512,256]{2,1,0:T(8,128)(2,1)S(1)}, bf16[2,512,256]{2,1,0:T(8,128)(2,1)S(1)}, u32[]{:S(2)}, u32[]{:S(2)}) collective-permute-start(bf16[2,512,256]{2,1,0:T(8,128)(2,1)S(1)} %get-tuple-element.34.rest_0_), channel_id=1, source_target_pairs={{0,4},{1,5},{2,6},{3,7},{4,0},{5,1},{6,2},{7,3},{8,12},{9,13},{10,... | collective-permute-start | bytes 1572872 | tf_op jit(solution)/shard_map/ppermute | solution.py:34
  38.8 2.1 %collective-permute-start.30 = (bf16[2,512,256]{2,1,0:T(8,128)(2,1)S(1)}, bf16[2,512,256]{2,1,0:T(8,128)(2,1)S(1)}, u32[]{:S(2)}, u32[]{:S(2)}) collective-permute-start(bf16[2,512,256]{2,1,0:T(8,128)(2,1)S(1)} %get-tuple-element.34.rest_0_), channel_id=1, source_target_pairs={{0,6},{1,7},{2,0},{3,1},{4,2},{5,3},{6,4},{7,5},{8,14},{9,15},{10,... | collective-permute-start | bytes 1572872 | tf_op jit(solution)/shard_map/ppermute | solution.py:34
  40.9 0.7 collective-permute-start.35
  41.6 5.8 %collective-permute-start.14 = (bf16[256,128]{1,0:T(8,128)(2,1)S(1)}, bf16[256,128]{1,0:T(8,128)(2,1)S(1)}, u32[]{:S(2)}, u32[]{:S(2)}) collective-permute-start(bf16[256,128]{1,0:T(8,128)(2,1)S(1)} %get-tuple-element.27.a0), channel_id=1, source_target_pairs={{0,64},{8,72},{16,80},{24,88},{32,96},{40,104},{48,112},{56,120},{... | collective-permute-start | bytes 196616 | tf_op jit(solution)/shard_map/ppermute | solution.py:22
  47.4 2.2 %collective-permute-done.14.a2 = bf16[256,128]{1,0:T(8,128)(2,1)S(1)} collective-permute-done((bf16[256,128]{1,0:T(8,128)(2,1)S(1)}, bf16[256,128]{1,0:T(8,128)(2,1)S(1)}, u32[]{:S(2)}, u32[]{:S(2)}) %collective-permute-start.14) | collective-permute-done | bytes 65568 | tf_op jit(solution)/shard_map/ppermute | solution.py:22
  49.6 2.2 %collective-permute-start.15 = (bf16[256,128]{1,0:T(8,128)(2,1)S(1)}, bf16[256,128]{1,0:T(8,128)(2,1)S(1)}, u32[]{:S(2)}, u32[]{:S(2)}) collective-permute-start(bf16[256,128]{1,0:T(8,128)(2,1)S(1)} %get-tuple-element.27.a0), channel_id=1, source_target_pairs={{0,96},{8,104},{16,112},{24,120},{32,0},{40,8},{48,16},{56,24},{64... | collective-permute-start | bytes 196616 | tf_op jit(solution)/shard_map/ppermute | solution.py:22
  51.9 2.0 %collective-permute-done.15.a3 = bf16[256,128]{1,0:T(8,128)(2,1)S(1)} collective-permute-done((bf16[256,128]{1,0:T(8,128)(2,1)S(1)}, bf16[256,128]{1,0:T(8,128)(2,1)S(1)}, u32[]{:S(2)}, u32[]{:S(2)}) %collective-permute-start.15) | collective-permute-done | bytes 65568 | tf_op jit(solution)/shard_map/ppermute | solution.py:22
  53.9 0.5 collective-permute-start.16
  54.4 8.8 %collective-permute-start.37 = (bf16[256,512]{1,0:T(8,128)(2,1)S(1)}, bf16[256,512]{1,0:T(8,128)(2,1)S(1)}, u32[]{:S(2)}, u32[]{:S(2)}) collective-permute-start(bf16[256,512]{1,0:T(8,128)(2,1)S(1)} %collective-permute-done.35.rest_0_), channel_id=1, source_target_pairs={{0,2},{1,3},{2,4},{3,5},{4,6},{5,7},{6,0},{7,1},{8,10},{9,11},{10,... | collective-permute-start | bytes 786440 | tf_op jit(solution)/shard_map/ppermute | solution.py:34
  63.2 12.1 %collective-permute-start.39 = (bf16[256,512]{1,0:T(8,128)(2,1)S(1)}, bf16[256,512]{1,0:T(8,128)(2,1)S(1)}, u32[]{:S(2)}, u32[]{:S(2)}) collective-permute-start(bf16[256,512]{1,0:T(8,128)(2,1)S(1)} %collective-permute-done.35.rest_0_), channel_id=1, source_target_pairs={{0,4},{1,5},{2,6},{3,7},{4,0},{5,1},{6,2},{7,3},{8,12},{9,13},{10,... | collective-permute-start | bytes 786440 | tf_op jit(solution)/shard_map/ppermute | solution.py:34
  75.3 4.4 %collective-permute-start.18 = (bf16[4,256,128]{2,1,0:T(8,128)(2,1)S(1)}, bf16[4,256,128]{2,1,0:T(8,128)(2,1)S(1)}, u32[]{:S(2)}, u32[]{:S(2)}) collective-permute-start(bf16[4,256,128]{2,1,0:T(8,128)(2,1)S(1)} %shard_map.142.refs_1_), channel_id=1, source_target_pairs={{0,16},{8,24},{16,0},{24,8},{32,48},{40,56},{48,32},{56,40},{64,80... | collective-permute-start | bytes 786440 | tf_op jit(solution)/shard_map/ppermute | solution.py:29
  79.7 1.3 shard_map.144
  81.0 0.7 collective-permute-start.17
  81.7 5.7 %collective-permute-start.41 = (bf16[256,512]{1,0:T(8,128)(2,1)S(1)}, bf16[256,512]{1,0:T(8,128)(2,1)S(1)}, u32[]{:S(2)}, u32[]{:S(2)}) collective-permute-start(bf16[256,512]{1,0:T(8,128)(2,1)S(1)} %collective-permute-done.35.rest_0_), channel_id=1, source_target_pairs={{0,6},{1,7},{2,0},{3,1},{4,2},{5,3},{6,4},{7,5},{8,14},{9,15},{10,... | collective-permute-start | bytes 786440 | tf_op jit(solution)/shard_map/ppermute | solution.py:34
  87.4 0.5 collective-permute-start.29
  87.9 4.0 %collective-permute-done.20.refs_1_ = bf16[4,256,128]{2,1,0:T(8,128)(2,1)S(1)} collective-permute-done((bf16[4,256,128]{2,1,0:T(8,128)(2,1)S(1)}, bf16[4,256,128]{2,1,0:T(8,128)(2,1)S(1)}, u32[]{:S(2)}, u32[]{:S(2)}) %collective-permute-start.20) | collective-permute-done | bytes 262176 | tf_op jit(solution)/shard_map/ppermute | solution.py:29
  91.9 1.3 shard_map.145
  93.2 1.3 shard_map.146
  94.4 0.7 collective-permute-start.19
  95.1 1.1 collective-permute-done.17.p1
  96.2 0.3 collective-permute-start.21
  96.6 8.9 %collective-permute-done.19.p2 = bf16[1072,128]{1,0:T(8,128)(2,1)S(1)} collective-permute-done((bf16[1072,128]{1,0:T(8,128)(2,1)S(1)}, bf16[1072,128]{1,0:T(8,128)(2,1)S(1)}, u32[]{:S(2)}, u32[]{:S(2)}) %collective-permute-start.19) | collective-permute-done | bytes 274464 | tf_op jit(solution)/shard_map/ppermute | solution.py:29
  105.5 5.4 %collective-permute-done.21.p3 = bf16[1072,128]{1,0:T(8,128)(2,1)S(1)} collective-permute-done((bf16[1072,128]{1,0:T(8,128)(2,1)S(1)}, bf16[1072,128]{1,0:T(8,128)(2,1)S(1)}, u32[]{:S(2)}, u32[]{:S(2)}) %collective-permute-start.21) | collective-permute-done | bytes 274464 | tf_op jit(solution)/shard_map/ppermute | solution.py:29
  110.9 1.3 shard_map.143.p0
  112.2 0.8 shard_map.147
  113.1 0.6 collective-permute-start.40
  113.6 0.1 collective-permute-start.42
  113.7 3.9 %collective-permute-done.22.p1 = bf16[272,128]{1,0:T(8,128)(2,1)S(1)} collective-permute-done((bf16[272,128]{1,0:T(8,128)(2,1)S(1)}, bf16[272,128]{1,0:T(8,128)(2,1)S(1)}, u32[]{:S(2)}, u32[]{:S(2)}) %collective-permute-start.22) | collective-permute-done | bytes 69664 | tf_op jit(solution)/shard_map/ppermute | solution.py:22
  117.6 5.8 %collective-permute-done.23.p2 = bf16[272,128]{1,0:T(8,128)(2,1)S(1)} collective-permute-done((bf16[272,128]{1,0:T(8,128)(2,1)S(1)}, bf16[272,128]{1,0:T(8,128)(2,1)S(1)}, u32[]{:S(2)}, u32[]{:S(2)}) %collective-permute-start.23) | collective-permute-done | bytes 69664 | tf_op jit(solution)/shard_map/ppermute | solution.py:22
  123.4 0.8 shard_map.148
  124.2 1.0 shard_map.149
  125.2 3.7 %collective-permute-done.24.p3 = bf16[272,128]{1,0:T(8,128)(2,1)S(1)} collective-permute-done((bf16[272,128]{1,0:T(8,128)(2,1)S(1)}, bf16[272,128]{1,0:T(8,128)(2,1)S(1)}, u32[]{:S(2)}, u32[]{:S(2)}) %collective-permute-start.24) | collective-permute-done | bytes 69664 | tf_op jit(solution)/shard_map/ppermute | solution.py:22
  129.0 0.4 shard_map.150.a0
  129.5 1.7 %collective-permute-start.33 = (bf16[128,256]{1,0:T(8,128)(2,1)S(1)}, bf16[128,256]{1,0:T(8,128)(2,1)S(1)}, u32[]{:S(2)}, u32[]{:S(2)}) collective-permute-start(bf16[128,256]{1,0:T(8,128)(2,1)S(1)} %shard_map.150.a0), channel_id=1, source_target_pairs={{0,64},{8,72},{16,80},{24,88},{32,96},{40,104},{48,112},{56,120},{... | collective-permute-start | bytes 196616 | tf_op jit(solution)/shard_map/ppermute | solution.py:22
  131.2 1.6 %collective-permute-start.34 = (bf16[128,256]{1,0:T(8,128)(2,1)S(1)}, bf16[128,256]{1,0:T(8,128)(2,1)S(1)}, u32[]{:S(2)}, u32[]{:S(2)}) collective-permute-start(bf16[128,256]{1,0:T(8,128)(2,1)S(1)} %shard_map.150.a0), channel_id=1, source_target_pairs={{0,96},{8,104},{16,112},{24,120},{32,0},{40,8},{48,16},{56,24},{64... | collective-permute-start | bytes 196616 | tf_op jit(solution)/shard_map/ppermute | solution.py:22
  132.8 2.9 %collective-permute-done.32.a1 = bf16[128,256]{1,0:T(8,128)(2,1)S(1)} collective-permute-done((bf16[128,256]{1,0:T(8,128)(2,1)S(1)}, bf16[128,256]{1,0:T(8,128)(2,1)S(1)}, u32[]{:S(2)}, u32[]{:S(2)}) %collective-permute-start.32) | collective-permute-done | bytes 65568 | tf_op jit(solution)/shard_map/ppermute | solution.py:22
  135.6 0.9 collective-permute-done.34.a3
  136.5 0.5 shard_map.151
  137.0 0.1 collective-permute-start.43
  137.0 3.2 %collective-permute-start.44 = (bf16[128,256]{1,0:T(8,128)(2,1)S(1)}, bf16[128,256]{1,0:T(8,128)(2,1)S(1)}, u32[]{:S(2)}, u32[]{:S(2)}) collective-permute-start(bf16[128,256]{1,0:T(8,128)(2,1)S(1)} %get-tuple-element.41), channel_id=1, source_target_pairs={{0,24},{8,0},{16,8},{24,16},{32,56},{40,32},{48,40},{56,48},{64,88... | collective-permute-start | bytes 196616 | tf_op jit(solution)/shard_map/ppermute | solution.py:29
  140.3 0.6 copy.15
  140.9 0.6 copy.16
  141.5 1.0 collective-permute-done.43.g1
  142.5 0.3 collective-permute-done.44.g2
  142.8 3.3 %collective-permute-done.45.g3 = bf16[128,256]{1,0:T(8,128)(2,1)S(1)} collective-permute-done((bf16[128,256]{1,0:T(8,128)(2,1)S(1)}, bf16[128,256]{1,0:T(8,128)(2,1)S(1)}, u32[]{:S(2)}, u32[]{:S(2)}) %collective-permute-start.45) | collective-permute-done | bytes 65568 | tf_op jit(solution)/shard_map/ppermute | solution.py:29
  146.0 0.7 shard_map.152
  (52 shorter events, 0.3 us)
Async XLA Ops:
  0.6 33.8 %copy-start.2 = (f32[4096]{0:T(1024)S(1)}, f32[4096]{0:T(1024)}, u32[]{:S(2)}) copy-start(f32[4096]{0:T(1024)} %param.16) | copy-start | bytes 49156
  0.6 40.2 %copy-start.3 = (bf16[256,512]{1,0:T(8,128)(2,1)S(1)}, bf16[256,512]{1,0:T(8,128)(2,1)}, u32[]{:S(2)}) copy-start(bf16[256,512]{1,0:T(8,128)(2,1)} %param.18) | copy-start | bytes 786436
  3.2 10.2 %collective-permute-start = (bf16[128,256]{1,0:T(8,128)(2,1)S(1)}, bf16[128,256]{1,0:T(8,128)(2,1)S(1)}, u32[]{:S(2)}, u32[]{:S(2)}) collective-permute-start(bf16[128,256]{1,0:T(8,128)(2,1)S(1)} %get-tuple-element.23.a0), channel_id=1, source_target_pairs={{0,32},{8,40},{16,48},{24,56},{32,64},{40,72},{48,80},{56,88},{64,... | collective-permute-start | bytes 196616 | tf_op jit(solution)/shard_map/ppermute | solution.py:22
  4.9 9.3 %collective-permute-start.1 = (bf16[128,256]{1,0:T(8,128)(2,1)S(1)}, bf16[128,256]{1,0:T(8,128)(2,1)S(1)}, u32[]{:S(2)}, u32[]{:S(2)}) collective-permute-start(bf16[128,256]{1,0:T(8,128)(2,1)S(1)} %get-tuple-element.23.a0), channel_id=1, source_target_pairs={{0,64},{8,72},{16,80},{24,88},{32,96},{40,104},{48,112},{56,120},{... | collective-permute-start | bytes 196616 | tf_op jit(solution)/shard_map/ppermute | solution.py:22
  7.8 6.4 %collective-permute-start.2 = (bf16[128,256]{1,0:T(8,128)(2,1)S(1)}, bf16[128,256]{1,0:T(8,128)(2,1)S(1)}, u32[]{:S(2)}, u32[]{:S(2)}) collective-permute-start(bf16[128,256]{1,0:T(8,128)(2,1)S(1)} %get-tuple-element.23.a0), channel_id=1, source_target_pairs={{0,96},{8,104},{16,112},{24,120},{32,0},{40,8},{48,16},{56,24},{64... | collective-permute-start | bytes 196616 | tf_op jit(solution)/shard_map/ppermute | solution.py:22
  9.2 70.5 %copy-start = (bf16[2,128,4096]{2,1,0:T(8,128)(2,1)S(1)}, bf16[2,128,4096]{2,1,0:T(8,128)(2,1)}, u32[]{:S(2)}) copy-start(bf16[2,128,4096]{2,1,0:T(8,128)(2,1)} %refs_2_.7) | copy-start | bytes 6291460
  9.2 70.5 %copy-start.1 = (bf16[2,128,4096]{2,1,0:T(8,128)(2,1)S(1)}, bf16[2,128,4096]{2,1,0:T(8,128)(2,1)}, u32[]{:S(2)}) copy-start(bf16[2,128,4096]{2,1,0:T(8,128)(2,1)} %refs_3_.7) | copy-start | bytes 6291460
  9.2 10.7 %collective-permute-start.9 = (bf16[512,256]{1,0:T(8,128)(2,1)S(1)}, bf16[512,256]{1,0:T(8,128)(2,1)S(1)}, u32[]{:S(2)}, u32[]{:S(2)}) collective-permute-start(bf16[512,256]{1,0:T(8,128)(2,1)S(1)} %get-tuple-element.26.rest_0_), channel_id=1, source_target_pairs={{0,4},{1,5},{2,6},{3,7},{4,0},{5,1},{6,2},{7,3},{8,12},{9,13},{10,... | collective-permute-start | bytes 786440 | tf_op jit(solution)/shard_map/ppermute | solution.py:34
  12.2 11.5 %collective-permute-start.11 = (bf16[512,256]{1,0:T(8,128)(2,1)S(1)}, bf16[512,256]{1,0:T(8,128)(2,1)S(1)}, u32[]{:S(2)}, u32[]{:S(2)}) collective-permute-start(bf16[512,256]{1,0:T(8,128)(2,1)S(1)} %get-tuple-element.26.rest_0_), channel_id=1, source_target_pairs={{0,6},{1,7},{2,0},{3,1},{4,2},{5,3},{6,4},{7,5},{8,14},{9,15},{10,... | collective-permute-start | bytes 786440 | tf_op jit(solution)/shard_map/ppermute | solution.py:34
  13.3 14.3 %collective-permute-start.7 = (bf16[512,256]{1,0:T(8,128)(2,1)S(1)}, bf16[512,256]{1,0:T(8,128)(2,1)S(1)}, u32[]{:S(2)}, u32[]{:S(2)}) collective-permute-start(bf16[512,256]{1,0:T(8,128)(2,1)S(1)} %get-tuple-element.26.rest_0_), channel_id=1, source_target_pairs={{0,2},{1,3},{2,4},{3,5},{4,6},{5,7},{6,0},{7,1},{8,10},{9,11},{10,... | collective-permute-start | bytes 786440 | tf_op jit(solution)/shard_map/ppermute | solution.py:34
  14.2 13.4 %collective-permute-start.6 = (bf16[512,256]{1,0:T(8,128)(2,1)S(1)}, bf16[512,256]{1,0:T(8,128)(2,1)S(1)}, u32[]{:S(2)}, u32[]{:S(2)}) collective-permute-start(bf16[512,256]{1,0:T(8,128)(2,1)S(1)} %get-tuple-element.26.rest_0_), channel_id=1, source_target_pairs={{0,1},{1,0},{2,3},{3,2},{4,5},{5,4},{6,7},{7,6},{8,9},{9,8},{10,11... | collective-permute-start | bytes 786440 | tf_op jit(solution)/shard_map/ppermute | solution.py:38
  14.3 13.9 %collective-permute-start.3 = (bf16[4,128,256]{2,1,0:T(8,128)(2,1)S(1)}, bf16[4,128,256]{2,1,0:T(8,128)(2,1)S(1)}, u32[]{:S(2)}, u32[]{:S(2)}) collective-permute-start(bf16[4,128,256]{2,1,0:T(8,128)(2,1)S(1)} %shard_map.140.s0), channel_id=1, source_target_pairs={{0,8},{8,16},{16,24},{24,0},{32,40},{40,48},{48,56},{56,32},{64,72... | collective-permute-start | bytes 786440 | tf_op jit(solution)/shard_map/ppermute | solution.py:29
  19.8 12.3 %collective-permute-start.4 = (bf16[4,128,256]{2,1,0:T(8,128)(2,1)S(1)}, bf16[4,128,256]{2,1,0:T(8,128)(2,1)S(1)}, u32[]{:S(2)}, u32[]{:S(2)}) collective-permute-start(bf16[4,128,256]{2,1,0:T(8,128)(2,1)S(1)} %shard_map.140.s0), channel_id=1, source_target_pairs={{0,16},{8,24},{16,0},{24,8},{32,48},{40,56},{48,32},{56,40},{64,80... | collective-permute-start | bytes 786440 | tf_op jit(solution)/shard_map/ppermute | solution.py:29
  23.7 10.7 %collective-permute-start.5 = (bf16[4,128,256]{2,1,0:T(8,128)(2,1)S(1)}, bf16[4,128,256]{2,1,0:T(8,128)(2,1)S(1)}, u32[]{:S(2)}, u32[]{:S(2)}) collective-permute-start(bf16[4,128,256]{2,1,0:T(8,128)(2,1)S(1)} %shard_map.140.s0), channel_id=1, source_target_pairs={{0,24},{8,0},{16,8},{24,16},{32,56},{40,32},{48,40},{56,48},{64,88... | collective-permute-start | bytes 786440 | tf_op jit(solution)/shard_map/ppermute | solution.py:29
  27.7 6.8 %collective-permute-start.10 = (bf16[512,256]{1,0:T(8,128)(2,1)S(1)}, bf16[512,256]{1,0:T(8,128)(2,1)S(1)}, u32[]{:S(2)}, u32[]{:S(2)}) collective-permute-start(bf16[512,256]{1,0:T(8,128)(2,1)S(1)} %collective-permute-done.9.rest_4_), channel_id=1, source_target_pairs={{0,1},{1,0},{2,3},{3,2},{4,5},{5,4},{6,7},{7,6},{8,9},{9,8},{10,11... | collective-permute-start | bytes 786440 | tf_op jit(solution)/shard_map/ppermute | solution.py:38
  27.7 6.8 %collective-permute-start.12 = (bf16[512,256]{1,0:T(8,128)(2,1)S(1)}, bf16[512,256]{1,0:T(8,128)(2,1)S(1)}, u32[]{:S(2)}, u32[]{:S(2)}) collective-permute-start(bf16[512,256]{1,0:T(8,128)(2,1)S(1)} %collective-permute-done.11.rest_6_), channel_id=1, source_target_pairs={{0,1},{1,0},{2,3},{3,2},{4,5},{5,4},{6,7},{7,6},{8,9},{9,8},{10,11... | collective-permute-start | bytes 786440 | tf_op jit(solution)/shard_map/ppermute | solution.py:38
  28.2 6.2 %collective-permute-start.8 = (bf16[512,256]{1,0:T(8,128)(2,1)S(1)}, bf16[512,256]{1,0:T(8,128)(2,1)S(1)}, u32[]{:S(2)}, u32[]{:S(2)}) collective-permute-start(bf16[512,256]{1,0:T(8,128)(2,1)S(1)} %collective-permute-done.7.rest_2_), channel_id=1, source_target_pairs={{0,1},{1,0},{2,3},{3,2},{4,5},{5,4},{6,7},{7,6},{8,9},{9,8},{10,11... | collective-permute-start | bytes 786440 | tf_op jit(solution)/shard_map/ppermute | solution.py:38
  32.1 22.3 %collective-permute-start.26 = (bf16[2,512,256]{2,1,0:T(8,128)(2,1)S(1)}, bf16[2,512,256]{2,1,0:T(8,128)(2,1)S(1)}, u32[]{:S(2)}, u32[]{:S(2)}) collective-permute-start(bf16[2,512,256]{2,1,0:T(8,128)(2,1)S(1)} %get-tuple-element.34.rest_0_), channel_id=1, source_target_pairs={{0,2},{1,3},{2,4},{3,5},{4,6},{5,7},{6,0},{7,1},{8,10},{9,11},{10,... | collective-permute-start | bytes 1572872 | tf_op jit(solution)/shard_map/ppermute | solution.py:34
  35.5 6.1 %collective-permute-start.13 = (bf16[256,128]{1,0:T(8,128)(2,1)S(1)}, bf16[256,128]{1,0:T(8,128)(2,1)S(1)}, u32[]{:S(2)}, u32[]{:S(2)}) collective-permute-start(bf16[256,128]{1,0:T(8,128)(2,1)S(1)} %get-tuple-element.27.a0), channel_id=1, source_target_pairs={{0,32},{8,40},{16,48},{24,56},{32,64},{40,72},{48,80},{56,88},{64,... | collective-permute-start | bytes 196616 | tf_op jit(solution)/shard_map/ppermute | solution.py:22
  36.2 27.0 %collective-permute-start.28 = (bf16[2,512,256]{2,1,0:T(8,128)(2,1)S(1)}, bf16[2,512,256]{2,1,0:T(8,128)(2,1)S(1)}, u32[]{:S(2)}, u32[]{:S(2)}) collective-permute-start(bf16[2,512,256]{2,1,0:T(8,128)(2,1)S(1)} %get-tuple-element.34.rest_0_), channel_id=1, source_target_pairs={{0,4},{1,5},{2,6},{3,7},{4,0},{5,1},{6,2},{7,3},{8,12},{9,13},{10,... | collective-permute-start | bytes 1572872 | tf_op jit(solution)/shard_map/ppermute | solution.py:34
  38.8 36.5 %collective-permute-start.30 = (bf16[2,512,256]{2,1,0:T(8,128)(2,1)S(1)}, bf16[2,512,256]{2,1,0:T(8,128)(2,1)S(1)}, u32[]{:S(2)}, u32[]{:S(2)}) collective-permute-start(bf16[2,512,256]{2,1,0:T(8,128)(2,1)S(1)} %get-tuple-element.34.rest_0_), channel_id=1, source_target_pairs={{0,6},{1,7},{2,0},{3,1},{4,2},{5,3},{6,4},{7,5},{8,14},{9,15},{10,... | collective-permute-start | bytes 1572872 | tf_op jit(solution)/shard_map/ppermute | solution.py:34
  40.9 13.0 %collective-permute-start.35 = (bf16[256,512]{1,0:T(8,128)(2,1)S(1)}, bf16[256,512]{1,0:T(8,128)(2,1)S(1)}, u32[]{:S(2)}, u32[]{:S(2)}) collective-permute-start(bf16[256,512]{1,0:T(8,128)(2,1)S(1)} %copy-done.3), channel_id=1, source_target_pairs={{0,0},{1,1},{8,8},{9,9},{16,16},{17,17},{24,24},{25,25},{32,2},{33... | collective-permute-start | bytes 786440 | tf_op jit(solution)/shard_map/ppermute | solution.py:52
  41.6 8.1 %collective-permute-start.14 = (bf16[256,128]{1,0:T(8,128)(2,1)S(1)}, bf16[256,128]{1,0:T(8,128)(2,1)S(1)}, u32[]{:S(2)}, u32[]{:S(2)}) collective-permute-start(bf16[256,128]{1,0:T(8,128)(2,1)S(1)} %get-tuple-element.27.a0), channel_id=1, source_target_pairs={{0,64},{8,72},{16,80},{24,88},{32,96},{40,104},{48,112},{56,120},{... | collective-permute-start | bytes 196616 | tf_op jit(solution)/shard_map/ppermute | solution.py:22
  49.6 4.3 %collective-permute-start.15 = (bf16[256,128]{1,0:T(8,128)(2,1)S(1)}, bf16[256,128]{1,0:T(8,128)(2,1)S(1)}, u32[]{:S(2)}, u32[]{:S(2)}) collective-permute-start(bf16[256,128]{1,0:T(8,128)(2,1)S(1)} %get-tuple-element.27.a0), channel_id=1, source_target_pairs={{0,96},{8,104},{16,112},{24,120},{32,0},{40,8},{48,16},{56,24},{64... | collective-permute-start | bytes 196616 | tf_op jit(solution)/shard_map/ppermute | solution.py:22
  53.9 27.1 %collective-permute-start.25 = (bf16[2,512,256]{2,1,0:T(8,128)(2,1)S(1)}, bf16[2,512,256]{2,1,0:T(8,128)(2,1)S(1)}, u32[]{:S(2)}, u32[]{:S(2)}) collective-permute-start(bf16[2,512,256]{2,1,0:T(8,128)(2,1)S(1)} %get-tuple-element.34.rest_0_), channel_id=1, source_target_pairs={{0,1},{1,0},{2,3},{3,2},{4,5},{5,4},{6,7},{7,6},{8,9},{9,8},{10,11... | collective-permute-start | bytes 1572872 | tf_op jit(solution)/shard_map/ppermute | solution.py:38
  53.9 25.7 %collective-permute-start.16 = (bf16[4,256,128]{2,1,0:T(8,128)(2,1)S(1)}, bf16[4,256,128]{2,1,0:T(8,128)(2,1)S(1)}, u32[]{:S(2)}, u32[]{:S(2)}) collective-permute-start(bf16[4,256,128]{2,1,0:T(8,128)(2,1)S(1)} %shard_map.142.refs_1_), channel_id=1, source_target_pairs={{0,8},{8,16},{16,24},{24,0},{32,40},{40,48},{48,56},{56,32},{64,72... | collective-permute-start | bytes 786440 | tf_op jit(solution)/shard_map/ppermute | solution.py:29
  54.4 27.3 %collective-permute-start.37 = (bf16[256,512]{1,0:T(8,128)(2,1)S(1)}, bf16[256,512]{1,0:T(8,128)(2,1)S(1)}, u32[]{:S(2)}, u32[]{:S(2)}) collective-permute-start(bf16[256,512]{1,0:T(8,128)(2,1)S(1)} %collective-permute-done.35.rest_0_), channel_id=1, source_target_pairs={{0,2},{1,3},{2,4},{3,5},{4,6},{5,7},{6,0},{7,1},{8,10},{9,11},{10,... | collective-permute-start | bytes 786440 | tf_op jit(solution)/shard_map/ppermute | solution.py:34
  63.2 24.1 %collective-permute-start.39 = (bf16[256,512]{1,0:T(8,128)(2,1)S(1)}, bf16[256,512]{1,0:T(8,128)(2,1)S(1)}, u32[]{:S(2)}, u32[]{:S(2)}) collective-permute-start(bf16[256,512]{1,0:T(8,128)(2,1)S(1)} %collective-permute-done.35.rest_0_), channel_id=1, source_target_pairs={{0,4},{1,5},{2,6},{3,7},{4,0},{5,1},{6,2},{7,3},{8,12},{9,13},{10,... | collective-permute-start | bytes 786440 | tf_op jit(solution)/shard_map/ppermute | solution.py:34
  75.3 12.1 %collective-permute-start.18 = (bf16[4,256,128]{2,1,0:T(8,128)(2,1)S(1)}, bf16[4,256,128]{2,1,0:T(8,128)(2,1)S(1)}, u32[]{:S(2)}, u32[]{:S(2)}) collective-permute-start(bf16[4,256,128]{2,1,0:T(8,128)(2,1)S(1)} %shard_map.142.refs_1_), channel_id=1, source_target_pairs={{0,16},{8,24},{16,0},{24,8},{32,48},{40,56},{48,32},{56,40},{64,80... | collective-permute-start | bytes 786440 | tf_op jit(solution)/shard_map/ppermute | solution.py:29
  79.7 12.2 %collective-permute-start.20 = (bf16[4,256,128]{2,1,0:T(8,128)(2,1)S(1)}, bf16[4,256,128]{2,1,0:T(8,128)(2,1)S(1)}, u32[]{:S(2)}, u32[]{:S(2)}) collective-permute-start(bf16[4,256,128]{2,1,0:T(8,128)(2,1)S(1)} %shard_map.142.refs_1_), channel_id=1, source_target_pairs={{0,24},{8,0},{16,8},{24,16},{32,56},{40,32},{48,40},{56,48},{64,88... | collective-permute-start | bytes 786440 | tf_op jit(solution)/shard_map/ppermute | solution.py:29
  81.0 15.3 %collective-permute-start.17 = (bf16[1072,128]{1,0:T(8,128)(2,1)S(1)}, bf16[1072,128]{1,0:T(8,128)(2,1)S(1)}, u32[]{:S(2)}, u32[]{:S(2)}) collective-permute-start(bf16[1072,128]{1,0:T(8,128)(2,1)S(1)} %shard_map.144), channel_id=1, source_target_pairs={{0,24},{8,0},{16,8},{24,16},{32,56},{40,32},{48,40},{56,48},{64,88... | collective-permute-start | bytes 823304 | tf_op jit(solution)/shard_map/ppermute | solution.py:29
  81.7 12.8 %collective-permute-start.41 = (bf16[256,512]{1,0:T(8,128)(2,1)S(1)}, bf16[256,512]{1,0:T(8,128)(2,1)S(1)}, u32[]{:S(2)}, u32[]{:S(2)}) collective-permute-start(bf16[256,512]{1,0:T(8,128)(2,1)S(1)} %collective-permute-done.35.rest_0_), channel_id=1, source_target_pairs={{0,6},{1,7},{2,0},{3,1},{4,2},{5,3},{6,4},{7,5},{8,14},{9,15},{10,... | collective-permute-start | bytes 786440 | tf_op jit(solution)/shard_map/ppermute | solution.py:34
  87.4 25.6 %collective-permute-start.27 = (bf16[2,512,256]{2,1,0:T(8,128)(2,1)S(1)}, bf16[2,512,256]{2,1,0:T(8,128)(2,1)S(1)}, u32[]{:S(2)}, u32[]{:S(2)}) collective-permute-start(bf16[2,512,256]{2,1,0:T(8,128)(2,1)S(1)} %collective-permute-done.26.rest_2_), channel_id=1, source_target_pairs={{0,1},{1,0},{2,3},{3,2},{4,5},{5,4},{6,7},{7,6},{8,9},{9,8},{10,11... | collective-permute-start | bytes 1572872 | tf_op jit(solution)/shard_map/ppermute | solution.py:38
  87.4 25.7 %collective-permute-start.29 = (bf16[2,512,256]{2,1,0:T(8,128)(2,1)S(1)}, bf16[2,512,256]{2,1,0:T(8,128)(2,1)S(1)}, u32[]{:S(2)}, u32[]{:S(2)}) collective-permute-start(bf16[2,512,256]{2,1,0:T(8,128)(2,1)S(1)} %collective-permute-done.28.rest_4_), channel_id=1, source_target_pairs={{0,1},{1,0},{2,3},{3,2},{4,5},{5,4},{6,7},{7,6},{8,9},{9,8},{10,11... | collective-permute-start | bytes 1572872 | tf_op jit(solution)/shard_map/ppermute | solution.py:38
  91.9 21.8 %collective-permute-start.31 = (bf16[2,512,256]{2,1,0:T(8,128)(2,1)S(1)}, bf16[2,512,256]{2,1,0:T(8,128)(2,1)S(1)}, u32[]{:S(2)}, u32[]{:S(2)}) collective-permute-start(bf16[2,512,256]{2,1,0:T(8,128)(2,1)S(1)} %collective-permute-done.30.rest_6_), channel_id=1, source_target_pairs={{0,1},{1,0},{2,3},{3,2},{4,5},{5,4},{6,7},{7,6},{8,9},{9,8},{10,11... | collective-permute-start | bytes 1572872 | tf_op jit(solution)/shard_map/ppermute | solution.py:38
  94.4 11.1 %collective-permute-start.19 = (bf16[1072,128]{1,0:T(8,128)(2,1)S(1)}, bf16[1072,128]{1,0:T(8,128)(2,1)S(1)}, u32[]{:S(2)}, u32[]{:S(2)}) collective-permute-start(bf16[1072,128]{1,0:T(8,128)(2,1)S(1)} %shard_map.145), channel_id=1, source_target_pairs={{0,16},{8,24},{16,0},{24,8},{32,48},{40,56},{48,32},{56,40},{64,80... | collective-permute-start | bytes 823304 | tf_op jit(solution)/shard_map/ppermute | solution.py:29
  96.2 14.6 %collective-permute-start.21 = (bf16[1072,128]{1,0:T(8,128)(2,1)S(1)}, bf16[1072,128]{1,0:T(8,128)(2,1)S(1)}, u32[]{:S(2)}, u32[]{:S(2)}) collective-permute-start(bf16[1072,128]{1,0:T(8,128)(2,1)S(1)} %shard_map.146), channel_id=1, source_target_pairs={{0,8},{8,16},{16,24},{24,0},{32,40},{40,48},{48,56},{56,32},{64,72... | collective-permute-start | bytes 823304 | tf_op jit(solution)/shard_map/ppermute | solution.py:29
  105.5 23.9 %collective-permute-start.36 = (bf16[256,512]{1,0:T(8,128)(2,1)S(1)}, bf16[256,512]{1,0:T(8,128)(2,1)S(1)}, u32[]{:S(2)}, u32[]{:S(2)}) collective-permute-start(bf16[256,512]{1,0:T(8,128)(2,1)S(1)} %collective-permute-done.35.rest_0_), channel_id=1, source_target_pairs={{0,1},{1,0},{2,3},{3,2},{4,5},{5,4},{6,7},{7,6},{8,9},{9,8},{10,11... | collective-permute-start | bytes 786440 | tf_op jit(solution)/shard_map/ppermute | solution.py:38
  110.9 20.3 %collective-permute-start.38 = (bf16[256,512]{1,0:T(8,128)(2,1)S(1)}, bf16[256,512]{1,0:T(8,128)(2,1)S(1)}, u32[]{:S(2)}, u32[]{:S(2)}) collective-permute-start(bf16[256,512]{1,0:T(8,128)(2,1)S(1)} %collective-permute-done.37.rest_2_), channel_id=1, source_target_pairs={{0,1},{1,0},{2,3},{3,2},{4,5},{5,4},{6,7},{7,6},{8,9},{9,8},{10,11... | collective-permute-start | bytes 786440 | tf_op jit(solution)/shard_map/ppermute | solution.py:38
  113.0 4.6 %collective-permute-start.22 = (bf16[272,128]{1,0:T(8,128)(2,1)S(1)}, bf16[272,128]{1,0:T(8,128)(2,1)S(1)}, u32[]{:S(2)}, u32[]{:S(2)}) collective-permute-start(bf16[272,128]{1,0:T(8,128)(2,1)S(1)} %get-tuple-element.29), channel_id=1, source_target_pairs={{0,96},{8,104},{16,112},{24,120},{32,0},{40,8},{48,16},{56,24},{64... | collective-permute-start | bytes 208904 | tf_op jit(solution)/shard_map/ppermute | solution.py:22
  113.1 19.7 %collective-permute-start.40 = (bf16[256,512]{1,0:T(8,128)(2,1)S(1)}, bf16[256,512]{1,0:T(8,128)(2,1)S(1)}, u32[]{:S(2)}, u32[]{:S(2)}) collective-permute-start(bf16[256,512]{1,0:T(8,128)(2,1)S(1)} %collective-permute-done.39.rest_4_), channel_id=1, source_target_pairs={{0,1},{1,0},{2,3},{3,2},{4,5},{5,4},{6,7},{7,6},{8,9},{9,8},{10,11... | collective-permute-start | bytes 786440 | tf_op jit(solution)/shard_map/ppermute | solution.py:38
  113.6 19.1 %collective-permute-start.42 = (bf16[256,512]{1,0:T(8,128)(2,1)S(1)}, bf16[256,512]{1,0:T(8,128)(2,1)S(1)}, u32[]{:S(2)}, u32[]{:S(2)}) collective-permute-start(bf16[256,512]{1,0:T(8,128)(2,1)S(1)} %collective-permute-done.41.rest_6_), channel_id=1, source_target_pairs={{0,1},{1,0},{2,3},{3,2},{4,5},{5,4},{6,7},{7,6},{8,9},{9,8},{10,11... | collective-permute-start | bytes 786440 | tf_op jit(solution)/shard_map/ppermute | solution.py:38
  117.6 5.8 %collective-permute-start.23 = (bf16[272,128]{1,0:T(8,128)(2,1)S(1)}, bf16[272,128]{1,0:T(8,128)(2,1)S(1)}, u32[]{:S(2)}, u32[]{:S(2)}) collective-permute-start(bf16[272,128]{1,0:T(8,128)(2,1)S(1)} %get-tuple-element.30), channel_id=1, source_target_pairs={{0,64},{8,72},{16,80},{24,88},{32,96},{40,104},{48,112},{56,120},{... | collective-permute-start | bytes 208904 | tf_op jit(solution)/shard_map/ppermute | solution.py:22
  123.4 5.5 %collective-permute-start.24 = (bf16[272,128]{1,0:T(8,128)(2,1)S(1)}, bf16[272,128]{1,0:T(8,128)(2,1)S(1)}, u32[]{:S(2)}, u32[]{:S(2)}) collective-permute-start(bf16[272,128]{1,0:T(8,128)(2,1)S(1)} %get-tuple-element.31), channel_id=1, source_target_pairs={{0,32},{8,40},{16,48},{24,56},{32,64},{40,72},{48,80},{56,88},{64,... | collective-permute-start | bytes 208904 | tf_op jit(solution)/shard_map/ppermute | solution.py:22
  129.4 6.2 %collective-permute-start.32 = (bf16[128,256]{1,0:T(8,128)(2,1)S(1)}, bf16[128,256]{1,0:T(8,128)(2,1)S(1)}, u32[]{:S(2)}, u32[]{:S(2)}) collective-permute-start(bf16[128,256]{1,0:T(8,128)(2,1)S(1)} %shard_map.150.a0), channel_id=1, source_target_pairs={{0,32},{8,40},{16,48},{24,56},{32,64},{40,72},{48,80},{56,88},{64,... | collective-permute-start | bytes 196616 | tf_op jit(solution)/shard_map/ppermute | solution.py:22
  129.5 6.2 %collective-permute-start.33 = (bf16[128,256]{1,0:T(8,128)(2,1)S(1)}, bf16[128,256]{1,0:T(8,128)(2,1)S(1)}, u32[]{:S(2)}, u32[]{:S(2)}) collective-permute-start(bf16[128,256]{1,0:T(8,128)(2,1)S(1)} %shard_map.150.a0), channel_id=1, source_target_pairs={{0,64},{8,72},{16,80},{24,88},{32,96},{40,104},{48,112},{56,120},{... | collective-permute-start | bytes 196616 | tf_op jit(solution)/shard_map/ppermute | solution.py:22
  131.2 5.3 %collective-permute-start.34 = (bf16[128,256]{1,0:T(8,128)(2,1)S(1)}, bf16[128,256]{1,0:T(8,128)(2,1)S(1)}, u32[]{:S(2)}, u32[]{:S(2)}) collective-permute-start(bf16[128,256]{1,0:T(8,128)(2,1)S(1)} %shard_map.150.a0), channel_id=1, source_target_pairs={{0,96},{8,104},{16,112},{24,120},{32,0},{40,8},{48,16},{56,24},{64... | collective-permute-start | bytes 196616 | tf_op jit(solution)/shard_map/ppermute | solution.py:22
  137.0 5.5 %collective-permute-start.43 = (bf16[128,256]{1,0:T(8,128)(2,1)S(1)}, bf16[128,256]{1,0:T(8,128)(2,1)S(1)}, u32[]{:S(2)}, u32[]{:S(2)}) collective-permute-start(bf16[128,256]{1,0:T(8,128)(2,1)S(1)} %get-tuple-element.40), channel_id=1, source_target_pairs={{0,8},{8,16},{16,24},{24,0},{32,40},{40,48},{48,56},{56,32},{64,72... | collective-permute-start | bytes 196616 | tf_op jit(solution)/shard_map/ppermute | solution.py:29
  137.0 5.7 %collective-permute-start.44 = (bf16[128,256]{1,0:T(8,128)(2,1)S(1)}, bf16[128,256]{1,0:T(8,128)(2,1)S(1)}, u32[]{:S(2)}, u32[]{:S(2)}) collective-permute-start(bf16[128,256]{1,0:T(8,128)(2,1)S(1)} %get-tuple-element.41), channel_id=1, source_target_pairs={{0,24},{8,0},{16,8},{24,16},{32,56},{40,32},{48,40},{56,48},{64,88... | collective-permute-start | bytes 196616 | tf_op jit(solution)/shard_map/ppermute | solution.py:29
  140.3 5.8 %collective-permute-start.45 = (bf16[128,256]{1,0:T(8,128)(2,1)S(1)}, bf16[128,256]{1,0:T(8,128)(2,1)S(1)}, u32[]{:S(2)}, u32[]{:S(2)}) collective-permute-start(bf16[128,256]{1,0:T(8,128)(2,1)S(1)} %get-tuple-element.42), channel_id=1, source_target_pairs={{0,16},{8,24},{16,0},{24,8},{32,48},{40,56},{48,32},{56,40},{64,80... | collective-permute-start | bytes 196616 | tf_op jit(solution)/shard_map/ppermute | solution.py:29
